TPU v7x, 32 devices: a whole 2x2x4 slice. The times are simulated.
32 devices in a mesh: blk: 32 (over z, y, x, core).
Axes of the slice: x: 2, y: 2, z: 4, core: 2. Of those that a mesh axis runs over, the one named last changes fastest.
Arguments:
- frames: float32 [128, 128, 1280], P('blk'), may hold values from -6 to 6
- widths: float32 [128], replicated, may hold values from 2 to 12
- kernel: float32 [3, 3], replicated, may hold values from -3 to 3
Outputs:
- filtered: float32 [128, 128, 1280], P(None, 'blk')
All inputs are finite; a program needn't handle non-finite values.
Results may differ from a plain program's by a relative error of at most 0.00007.
Values sent between devices are 32-bit elements; how exact they have to be, the bound alone decides.
No kernel may reach another device: no remote copies, remote signals or barrier semaphores. Data moves between devices by JAX's collectives and lax.ppermute only.
A program may use at most 64 MiB of HBM per device.

v0:
```python
import jax
import jax.numpy as jnp
from jax import lax
from jax.sharding import PartitionSpec as P

BAND = 24


def temporal_matrix(widths, length):
    steps = jnp.arange(length, dtype=jnp.int32)
    offset = (steps[:, None] - steps[None, :]).astype(jnp.float32)
    inside = jnp.abs(offset) <= BAND
    spread = widths[:, None]
    weights = jnp.where(inside, jnp.exp(-offset * offset / (2.0 * spread * spread)), 0.0)
    return weights / jnp.sum(weights, axis=1, keepdims=True)


def stencil(padded, kernel):
    rows_out = padded.shape[1] - 2
    columns = padded.shape[2]
    widened = jnp.pad(padded, ((0, 0), (0, 0), (1, 1)))
    summed = jnp.zeros((padded.shape[0], rows_out, columns), jnp.float32)
    for row_off in range(3):
        for col_off in range(3):
            summed = (
                summed
                + kernel[row_off, col_off]
                * widened[:, row_off : row_off + rows_out, col_off : col_off + columns]
            )
    return summed


def local(frames, widths, kernel):
    weights = temporal_matrix(widths, widths.shape[0])
    local_filtered = stencil(jnp.pad(frames, ((0, 0), (1, 1), (0, 0))), kernel)
    return jnp.einsum(
        "ts,srw->trw",
        weights,
        lax.all_to_all(local_filtered, "blk", split_axis=1, concat_axis=0, tiled=True),
        precision=lax.Precision.HIGHEST,
    )


def solution(mesh):
    return jax.shard_map(
        local,
        mesh=mesh,
        in_specs=(P("blk", None, None), P(), P()),
        out_specs=P(None, "blk", None),
        check_vma=False,
    )
```

profile of v0, /device:TPU:0, one launch (start us, length us, event | category | flops | bytes accessed | tf_op | source)
XLA Modules:
  0.0 102.4 jit_solution(13410759657057529813)
XLA Ops:
  0.0 1.7 %fusion.13 = (f32[1,1]{1,0:T(1,128)}, f32[1,1]{1,0:T(1,128)}, f32[1,1]{1,0:T(1,128)}, f32[1,1]{1,0:T(1,128)}, f32[1,1]{1,0:T(1,128)}, /*index=5*/f32[1,1]{1,0:T(...) fusion(f32[3,3]{1,0:T(4,128)} %param.5), kind=kLoop, calls=%fused_computation.18 | loop fusion | bytes 72 | tf_op jit(solution)/shard_map/slice | solution.py:27
  1.7 3.4 %copy.6 = f32[4,128,1280]{2,0,1:T(4,128)S(1)} copy(f32[4,128,1280]{2,1,0:T(8,128)} %param.3) | data formatting | bytes 5242880 | tf_op args[0]
  5.1 0.0 copy-start
  5.1 0.5 pad.8
  5.6 1.3 %copy-done = f32[4,128,1280]{2,1,0:T(8,128)S(1)} copy-done((f32[4,128,1280]{2,1,0:T(8,128)S(1)}, f32[4,128,1280]{2,1,0:T(8,128)}, u32[]{:S(2)}) %copy-start) | copy-done | bytes 2621464
  6.9 17.9 %multiply_add_fusion = f32[4,128,1280]{2,0,1:T(4,128)} fusion(f32[4,130,1280]{2,0,1:T(4,128)S(1)} %pad.8, f32[]{:T(128)} %bitcast.9, f32[]{:T(128)} %bitcast.8, f32[]{:T(128)} %bitcast.7, f32[]{:T(128)} %bitcast.6, f32[]{:T(128)} %bitcast.5, f32[]{:T(128)} %bitcast.4, f32[]{:T(128)} %bitcast.3, f32[]{:T(128)} %bitcast.2, f32[]{:T(128)} %bitcast.1, ...), kind=kLoop, calls=%fused_computation.1 | loop fusion | flops 11141120 | bytes 13148196 | tf_op jit(solution)/shard_map/add | solution.py:26
  24.8 0.0 copy-start.1
  24.8 7.3 %all-to-all-start = ((f32[4,128,1280]{2,0,1:T(4,128)}), f32[4,128,1280]{2,0,1:T(4,128)S(1)}, u32[]{:S(2)}, u32[]{:S(2)}) async-start(f32[4,128,1280]{2,0,1:T(4,128)} %multiply_add_fusion), calls=%async_computation | async-start | bytes 5242880 | tf_op jit(solution)/shard_map/all_to_all | solution.py:39
  32.1 0.0 copy-done.1
  32.2 0.2 fusion.10
  32.3 59.9 %all-to-all-done = f32[4,128,1280]{2,0,1:T(4,128)S(1)} async-done(((f32[4,128,1280]{2,0,1:T(4,128)}), f32[4,128,1280]{2,0,1:T(4,128)S(1)}, u32[]{:S(2)}, u32[]{:S(2)}) %all-to-all-start) | async-done | bytes 2621472 | tf_op jit(solution)/shard_map/all_to_all | solution.py:39
  92.2 1.7 %copy.12 = f32[4,32,4,1280]{3,0,1,2:T(4,128)} copy(f32[4,32,4,1280]{3,0,2,1:T(4,128)S(1)} %bitcast.19) | data formatting | bytes 5242880 | tf_op jit(solution)/shard_map/all_to_all | solution.py:39
  93.9 2.8 %all_to_all.16 = f32[128,4,1280]{2,0,1:T(8,128)S(1)} reshape(f32[32,4,4,1280]{3,1,0,2:T(4,128)} %bitcast.20) | data formatting | bytes 5242880 | tf_op jit(solution)/shard_map/all_to_all | solution.py:39
  96.7 2.5 %fusion.5 = f32[128,4,1280]{2,0,1:T(8,128)S(1)} fusion(f32[128,4,1280]{2,0,1:T(8,128)S(1)} %all_to_all.16, f32[128]{0:T(128)S(1)} %fusion.10, f32[128]{0:T(128)S(1)} %multiply_multiply_fusion), kind=kOutput, calls=%fused_computation.9 | convolution fusion | flops 1006780416 | bytes 5243904 | tf_op jit(solution)/shard_map/ts,srw->trw/dot_general | solution.py:36
  99.2 3.2 %copy.9 = f32[128,4,1280]{2,1,0:T(4,128)} copy(f32[128,4,1280]{2,0,1:T(8,128)S(1)} %fusion.5) | data formatting | bytes 5242880 | tf_op jit(solution)/shard_map/ts,srw->trw/dot_general | solution.py:36
  (1 shorter events, 0.0 us)
Async XLA Ops:
  5.1 1.7 %copy-start = (f32[4,128,1280]{2,1,0:T(8,128)S(1)}, f32[4,128,1280]{2,1,0:T(8,128)}, u32[]{:S(2)}) copy-start(f32[4,128,1280]{2,1,0:T(8,128)} %param.3) | copy-start | bytes 7864324
  24.8 7.3 %copy-start.1 = (f32[128]{0:T(128)S(1)}, f32[128]{0:T(128)}, u32[]{:S(2)}) copy-start(f32[128]{0:T(128)} %param.4) | copy-start | bytes 1540
  24.8 67.4 %all-to-all-start = ((f32[4,128,1280]{2,0,1:T(4,128)}), f32[4,128,1280]{2,0,1:T(4,128)S(1)}, u32[]{:S(2)}, u32[]{:S(2)}) async-start(f32[4,128,1280]{2,0,1:T(4,128)} %multiply_add_fusion), calls=%async_computation | async-start | bytes 5242880 | tf_op jit(solution)/shard_map/all_to_all | solution.py:39
where the time goes:
time: 103 us; the launch traced here: 102 us
  waiting for transfers between devices  59.9 us (58%)
  other arithmetic  18.1 us (18%)
  local copies, waits for them, and re-layouts  14.5 us (14%)
  starting transfers between devices  7.33 us (7%)
  matrix products  2.49 us (2%)
    all_to_all x1, waiting for transfers between devices, local(): lax.all_to_all(local_filtered, 'blk', split_axis=1, concat_axis=0, tiled=...  59.9 us
    add x1, other arithmetic, stencil(): summed + kernel[row_off, col_off] * widened[:, row_off:row_off + rows_out...  17.9 us
    all_to_all x1, starting transfers between devices, local(): lax.all_to_all(local_filtered, 'blk', split_axis=1, concat_axis=0, tiled=...  7.33 us
    unnamed x5, local copies, waits for them, and re-layouts  4.7 us
    all_to_all x2, local copies, waits for them, and re-layouts, local(): lax.all_to_all(local_filtered, 'blk', split_axis=1, concat_axis=0, tiled=...  4.49 us
    dot_general x1, local copies, waits for them, and re-layouts, local(): jnp.einsum('ts,srw->trw', weights, lax.all_to_all(local_filtered, 'blk',...  3.18 us
    dot_general x1, matrix products, local(): jnp.einsum('ts,srw->trw', weights, lax.all_to_all(local_filtered, 'blk',...  2.49 us
  transfers between devices with their start and end apart: 1, of which 1 were waited for; matrix products, arithmetic and copies ran while one was open for 0% of the time, Pallas kernels for 0%

commit v1 on v0

v1 whole, which is shorter than its diff:
```python
import functools

import jax
import jax.numpy as jnp
from jax import lax
from jax.experimental import pallas as pl
from jax.experimental.pallas import tpu as pltpu
from jax.sharding import PartitionSpec as P


BAND = 24
SUBLANES = 8
KERNEL_BYTES = 20 << 20
VMEM = pltpu.VMEM
SMEM = pltpu.SMEM


def message_order(devices):
    half = devices // 2
    across = [half ^ low for low in range(half)]
    within = list(range(1, half))
    order = across[:2]
    for pair in zip(within, across[2:]):
        order.extend(pair)
    return order + within[half - 2 :]


def filter_tile(me, tap, above, here, below, tile, tiles, rows):
    row = lax.broadcasted_iota(jnp.int32, here.shape, 0)
    column = lax.broadcasted_iota(jnp.int32, here.shape, 1)
    columns = here.shape[1]
    above = jnp.where(tile > 0, above, 0.0)
    below = jnp.where(tile < tiles - 1, below, 0.0)
    over = pltpu.roll(jnp.where(row == SUBLANES - 1, above, here), 1, 0)
    under = pltpu.roll(jnp.where(row == 0, below, here), SUBLANES - 1, 0)
    left, center, right = (
        tap[0][b] * over + tap[1][b] * here + tap[2][b] * under for b in range(3)
    )
    left = jnp.where(column == 0, 0.0, pltpu.roll(left, 1, 1))
    right = jnp.where(column == columns - 1, 0.0, pltpu.roll(right, columns - 1, 1))
    value = left + center + right
    step = rows
    while step < SUBLANES:
        swapped = jnp.where(
            (row & step) == 0,
            pltpu.roll(value, SUBLANES - step, 0),
            pltpu.roll(value, step, 0),
        )
        value = jnp.where((me * rows) & step == 0, value, swapped)
        step *= 2
    return value


def tile_rows(tile, tiles):
    spots = (jnp.maximum(tile - 1, 0), tile, jnp.minimum(tile + 1, tiles - 1))
    return [pl.ds(pl.multiple_of(spot * SUBLANES, SUBLANES), SUBLANES) for spot in spots]


def stencil_kernel(me_ref, kernel_ref, frames_ref, *refs, groups, rows, direct):
    count, height, _ = frames_ref.shape
    strips = SUBLANES // rows
    tiles = height // SUBLANES
    out_refs = refs[: len(groups) * strips]
    me = me_ref[0]
    tap = [[kernel_ref[a, b] for b in range(3)] for a in range(3)]
    if direct:
        near_ref, semaphores = refs[len(out_refs) :]
        copies = []
        for place, group in enumerate(groups):
            spans = tile_rows((me // strips) ^ group, tiles)
            for part, span in enumerate(spans):
                copies.append(
                    pltpu.make_async_copy(
                        frames_ref.at[:, span, :],
                        near_ref.at[place, part],
                        semaphores.at[place, part],
                    )
                )
        for copy in copies:
            copy.start()
        for copy in copies:
            copy.wait()
    for place, group in enumerate(groups):
        tile = (me // strips) ^ group
        spans = tile_rows(tile, tiles)
        for frame in range(count):
            if direct:
                parts = [near_ref[place, part, frame] for part in range(3)]
            else:
                parts = [frames_ref[frame, span, :] for span in spans]
            value = filter_tile(me, tap, *parts, tile, tiles, rows)
            for strip in range(strips):
                out_refs[place * strips + strip][frame * rows : (frame + 1) * rows, :] = value[
                    strip * rows : (strip + 1) * rows, :
                ]


def stencil(me, kernel, frames, groups, rows, direct):
    count, _, columns = frames.shape
    strips = SUBLANES // rows
    outs = len(groups) * strips
    size = count * rows * columns
    scratch = [
        VMEM((len(groups), 3, count, SUBLANES, columns), jnp.float32),
        pltpu.SemaphoreType.DMA((len(groups), 3)),
    ]
    return pl.pallas_call(
        functools.partial(stencil_kernel, groups=groups, rows=rows, direct=direct),
        in_specs=[
            pl.BlockSpec(memory_space=SMEM),
            pl.BlockSpec(memory_space=SMEM),
            pl.BlockSpec(memory_space=pl.ANY if direct else VMEM),
        ],
        out_specs=[pl.BlockSpec(memory_space=VMEM)] * outs,
        out_shape=[jax.ShapeDtypeStruct((count * rows, columns), jnp.float32)] * outs,
        scratch_shapes=scratch if direct else [],
        cost_estimate=pl.CostEstimate(
            flops=18 * size * outs, bytes_accessed=8 * size * outs, transcendentals=0
        ),
        compiler_params=pltpu.CompilerParams(vmem_limit_bytes=KERNEL_BYTES),
        name="stencil",
    )(me, kernel, frames)


def weights_kernel(me_ref, widths_ref, partner_ref, high_ref, low_ref, *, count, rows):
    length = widths_ref.shape[1]
    size = length * rows
    square = (length, length)
    time = lax.broadcasted_iota(jnp.int32, square, 0)
    frame = lax.rem(lax.broadcasted_iota(jnp.int32, square, 1), count)
    source = count * (me_ref[0] ^ partner_ref[...]) + frame
    spread = jnp.broadcast_to(widths_ref[...], square).T
    offset = (time - source).astype(jnp.float32)
    values = jnp.where(
        jnp.abs(offset) <= BAND, jnp.exp(-offset * offset / (2.0 * spread * spread)), 0.0
    )
    matrix = values / jnp.sum(values, axis=1, keepdims=True)
    high = matrix.astype(jnp.bfloat16)
    low = (matrix - high.astype(jnp.float32)).astype(jnp.bfloat16)

    def iota(shape, axis):
        return lax.broadcasted_iota(jnp.int32, shape, axis)

    tall, wide, full = (size, length), (length, size), (size, size)
    down = (iota(tall, 0) // rows == iota(tall, 1)).astype(jnp.bfloat16)
    along = (iota(wide, 0) == iota(wide, 1) // rows).astype(jnp.bfloat16)
    same = lax.rem(iota(full, 0), rows) == lax.rem(iota(full, 1), rows)
    dot = functools.partial(jnp.dot, preferred_element_type=jnp.float32)
    for piece, out_ref in ((high, high_ref), (low, low_ref)):
        wider = dot(down, dot(piece, along).astype(jnp.bfloat16))
        out_ref[...] = jnp.where(same, wider, 0.0).astype(jnp.bfloat16)


def spread_weights(me, widths, partners, count, rows):
    size = widths.shape[0] * rows
    columns = [partner for partner in partners for _ in range(count)]
    return pl.pallas_call(
        functools.partial(weights_kernel, count=count, rows=rows),
        in_specs=[
            pl.BlockSpec(memory_space=SMEM),
            pl.BlockSpec(memory_space=VMEM),
            pl.BlockSpec(memory_space=VMEM),
        ],
        out_specs=[pl.BlockSpec(memory_space=VMEM)] * 2,
        out_shape=[jax.ShapeDtypeStruct((size, size), jnp.bfloat16)] * 2,
        cost_estimate=pl.CostEstimate(
            flops=2 * size**3, bytes_accessed=4 * size**2, transcendentals=size
        ),
        compiler_params=pltpu.CompilerParams(vmem_limit_bytes=KERNEL_BYTES),
        name="weights",
    )(me, widths[None, :], jnp.array([columns], jnp.int32))


def product(high, low, part):
    part_high = part.astype(jnp.bfloat16)
    part_low = (part - part_high.astype(jnp.float32)).astype(jnp.bfloat16)
    dot = functools.partial(jnp.dot, preferred_element_type=jnp.float32)
    return dot(high, part_high) + dot(high, part_low) + dot(low, part_high)


def gather_kernel(high_ref, low_ref, *refs, begin, end, first, width):
    parts, out_ref = refs[:-1], refs[-1]
    if not first:
        so_far, parts = parts[0], parts[1:]
    high, low = high_ref[:, begin:end], low_ref[:, begin:end]
    for start in range(0, out_ref.shape[1], width):
        span = slice(start, start + width)
        part = jnp.concatenate([ref[:, span] for ref in parts], axis=0)
        value = product(high, low, part)
        out_ref[:, span] = value if first else so_far[:, span] + value


def last_kernel(high_ref, low_ref, *refs, begin, end, width):
    so_far, parts, out_ref = refs[0], refs[1:-1], refs[-1]
    times, rows, columns = out_ref.shape
    size = times * rows
    block = pl.ds(pl.multiple_of(pl.program_id(0) * size, size), size)
    high, low = high_ref[block, begin:end], low_ref[block, begin:end]
    for start in range(0, columns, width):
        span = slice(start, start + width)
        part = jnp.concatenate([ref[:, span] for ref in parts], axis=0)
        value = so_far[block, span] + product(high, low, part)
        out_ref[:, :, span] = value.reshape(times, rows, width)


def temporal(high, low, so_far, parts, begin, end, rows, last):
    size, columns = high.shape[0], parts[0].shape[1]
    ins = ([] if so_far is None else [so_far]) + list(parts)
    spans = dict(begin=begin, end=end, width=256)
    if last:
        shape, steps = (size // rows, rows, columns), 4
        block = (size // rows // steps, rows, columns)
        out = dict(grid=(steps,), out_specs=pl.BlockSpec(block, lambda i: (i, 0, 0)))
        body = functools.partial(last_kernel, **spans)
    else:
        shape, out = (size, columns), dict(out_specs=pl.BlockSpec(memory_space=VMEM))
        body = functools.partial(gather_kernel, first=so_far is None, **spans)
    return pl.pallas_call(
        body,
        in_specs=[pl.BlockSpec(memory_space=VMEM)] * (2 + len(ins)),
        out_shape=jax.ShapeDtypeStruct(shape, jnp.float32),
        cost_estimate=pl.CostEstimate(
            flops=6 * size * (end - begin) * columns,
            bytes_accessed=4 * size * columns * 2,
            transcendentals=0,
        ),
        compiler_params=pltpu.CompilerParams(vmem_limit_bytes=KERNEL_BYTES),
        name="temporal",
        **out,
    )(high, low, *ins)


def local(frames, widths, kernel, *, devices):
    count, height, _ = frames.shape
    rows = height // devices
    strips = SUBLANES // rows
    own = lax.axis_index("blk").astype(jnp.int32)[None]
    order = message_order(devices)
    partners = [0] + order
    every = list(dict.fromkeys(k // strips for k in order))
    messages = {}
    for stage, groups in enumerate((tuple(every[:1]), tuple(every[1:]))):
        outs = stencil(own, kernel, frames, groups, rows, stage == 0)
        for place, group in enumerate(groups):
            for strip in range(strips):
                messages[group * strips + strip] = outs[place * strips + strip]
    arrived = [messages[0]]
    for k in order:
        pairs = [(i, i ^ k) for i in range(devices)]
        arrived.append(lax.ppermute(messages[k], "blk", pairs))
    high, low = spread_weights(own, widths, partners, count, rows)
    total = None
    each = count * rows
    cuts = stage_cuts(devices)
    for begin, end in zip(cuts[:-1], cuts[1:]):
        total = temporal(
            high,
            low,
            total,
            arrived[begin:end],
            begin * each,
            end * each,
            rows,
            end == devices,
        )
    return total


def stage_cuts(devices):
    return [0, devices // 2, devices - devices // 4, devices]


def solution(mesh):
    devices = mesh.shape["blk"]
    return jax.shard_map(
        functools.partial(local, devices=devices),
        mesh=mesh,
        in_specs=(P("blk", None, None), P(), P()),
        out_specs=P(None, "blk", None),
        check_vma=False,
    )
```

time: 103 us -> 73.4 us (0.71)
  waiting for transfers between devices: 59.9 us -> 5.79 us
  starting transfers between devices: 7.33 us -> 55 us
  other arithmetic: 18.1 us -> 0 us
  local copies, waits for them, and re-layouts: 14.5 us -> 2.43 us
  Pallas kernels: 0 us -> 9.91 us
  matrix products: 2.49 us -> 0 us
    all_to_all x1 -> x0, waiting for transfers between devices: 59.9 us -> none  [local(): lax.all_to_all(local_filtered, 'blk', split_axis=1, concat_axis=0, tiled=...]
    ppermute x0 -> x31, starting transfers between devices: none -> 55 us  [local(): arrived.append(lax.ppermute(messages[k], 'blk', pairs))]
    add x1 -> x0, other arithmetic: 17.9 us -> none  [stencil(): summed + kernel[row_off, col_off] * widened[:, row_off:row_off + rows_out...]
    pallas_call x0 -> x6, Pallas kernels: none -> 9.91 us  [the longest x3 5.3 us: temporal(): pl.pallas_call(body, in_specs=[pl.BlockSpec(memory_space=VMEM)] * (2 + le...]
    all_to_all x1 -> x0, starting transfers between devices: 7.33 us -> none  [local(): lax.all_to_all(local_filtered, 'blk', split_axis=1, concat_axis=0, tiled=...]
    ppermute x0 -> x31, waiting for transfers between devices: none -> 5.79 us  [local(): arrived.append(lax.ppermute(messages[k], 'blk', pairs))]
    all_to_all x2 -> x0, local copies, waits for them, and re-layouts: 4.49 us -> none  [local(): lax.all_to_all(local_filtered, 'blk', split_axis=1, concat_axis=0, tiled=...]
    dot_general x1 -> x0, local copies, waits for them, and re-layouts: 3.18 us -> none  [local(): jnp.einsum('ts,srw->trw', weights, lax.all_to_all(local_filtered, 'blk',...]
  transfers between devices with their start and end apart: 1 -> 31, of which waited for: 1 -> 5; matrix products, arithmetic and copies ran while one was open for 0% -> 0% of each run, Pallas kernels for 0% -> 8%
where the time goes in v1:
time: 73.4 us; the launch traced here: 73.2 us
  starting transfers between devices  55 us (75%)
  Pallas kernels  9.91 us (14%)
  waiting for transfers between devices  5.79 us (8%)
  local copies, waits for them, and re-layouts  2.43 us (3%)
    ppermute x31, starting transfers between devices, local(): arrived.append(lax.ppermute(messages[k], 'blk', pairs))  55 us
    ppermute x31, waiting for transfers between devices, local(): arrived.append(lax.ppermute(messages[k], 'blk', pairs))  5.79 us
    pallas_call x3, Pallas kernels, temporal(): pl.pallas_call(body, in_specs=[pl.BlockSpec(memory_space=VMEM)] * (2 + le...  5.3 us
    pallas_call x2, Pallas kernels, stencil(): pl.pallas_call(functools.partial(stencil_kernel, groups=groups, rows=rows...  3.73 us
    unnamed x8, local copies, waits for them, and re-layouts  2.43 us
  transfers between devices with their start and end apart: 31, of which 5 were waited for; matrix products, arithmetic and copies ran while one was open for 0% of the time, Pallas kernels for 8%

profile of v1, /device:TPU:0, one launch (start us, length us, event | category | flops | bytes accessed | tf_op | source)
XLA Modules:
  0.0 73.2 jit_solution(12979588922539791450)
XLA Ops:
  0.0 1.7 %copy-done = f32[4,128,1280]{2,1,0:T(8,128)S(1)} copy-done((f32[4,128,1280]{2,1,0:T(8,128)S(1)}, f32[4,128,1280]{2,1,0:T(8,128)}, u32[]{:S(2)}) %copy-start) | copy-done | bytes 2621464
  1.7 0.7 copy-done.1
  2.4 0.9 %stencil.3 = (f32[16,1280]{1,0:T(8,128)S(1)}, f32[16,1280]{1,0:T(8,128)S(1)}) custom-call(s32[1]{0:T(128)} %bitcast.me_ref, f32[3,3]{1,0:T(4,128)S(1)} %copy-done.1, f32[4,128,1280]{2,1,0:T(8,128)S(1)} %copy-done), custom_call_target="tpu_custom_call" | custom-call | flops 737280 | bytes 327680 | tf_op jit(solution)/shard_map/stencil/pallas_call | solution.py:107
  3.4 4.1 %collective-permute-start = (f32[16,1280]{1,0:T(8,128)S(1)}, f32[16,1280]{1,0:T(8,128)S(1)}, u32[]{:S(2)}, u32[]{:S(2)}) collective-permute-start(f32[16,1280]{1,0:T(8,128)S(1)} %get-tuple-element.42), channel_id=1, source_target_pairs={{0,16},{1,17},{2,18},{3,19},{4,20},{5,21},{6,22},{7,23},{8,24},{9,... | collective-permute-start | bytes 245768 | tf_op jit(solution)/shard_map/ppermute | solution.py:250
  7.5 0.0 collective-permute-start.1
  7.5 2.8 %stencil.2 = (f32[16,1280]{1,0:T(8,128)S(1)}, f32[16,1280]{1,0:T(8,128)S(1)}, f32[16,1280]{1,0:T(8,128)S(1)}, f32[16,1280]{1,0:T(8,128)S(1)}, f32[16,1280]{1,0:T...) custom-call(s32[1]{0:T(128)} %bitcast.me_ref, ...), custom_call_target="tpu_custom_call" | custom-call | flops 11059200 | bytes 4915200 | tf_op jit(solution)/shard_map/stencil/pallas_call | solution.py:107
  10.3 0.3 collective-permute-start.2
  10.6 3.8 %collective-permute-start.3 = (f32[16,1280]{1,0:T(8,128)S(1)}, f32[16,1280]{1,0:T(8,128)S(1)}, u32[]{:S(2)}, u32[]{:S(2)}) collective-permute-start(f32[16,1280]{1,0:T(8,128)S(1)} %get-tuple-element.45), channel_id=1, source_target_pairs={{0,18},{1,19},{2,16},{3,17},{4,22},{5,23},{6,20},{7,21},{8,26},{9,... | collective-permute-start | bytes 245768 | tf_op jit(solution)/shard_map/ppermute | solution.py:250
  14.3 0.5 collective-permute-start.4
  14.9 0.0 collective-permute-done.refs_1_
  14.9 0.4 collective-permute-start.5
  15.3 0.0 collective-permute-done.1.refs_2_
  15.3 3.6 %collective-permute-start.6 = (f32[16,1280]{1,0:T(8,128)S(1)}, f32[16,1280]{1,0:T(8,128)S(1)}, u32[]{:S(2)}, u32[]{:S(2)}) collective-permute-start(f32[16,1280]{1,0:T(8,128)S(1)} %get-tuple-element.48), channel_id=1, source_target_pairs={{0,3},{1,2},{2,1},{3,0},{4,7},{5,6},{6,5},{7,4},{8,11},{9,10},{10,... | collective-permute-start | bytes 245768 | tf_op jit(solution)/shard_map/ppermute | solution.py:250
  18.9 0.0 collective-permute-done.2.refs_3_
  18.9 1.1 %collective-permute-start.7 = (f32[16,1280]{1,0:T(8,128)S(1)}, f32[16,1280]{1,0:T(8,128)S(1)}, u32[]{:S(2)}, u32[]{:S(2)}) collective-permute-start(f32[16,1280]{1,0:T(8,128)S(1)} %get-tuple-element.49), channel_id=1, source_target_pairs={{0,20},{1,21},{2,22},{3,23},{4,16},{5,17},{6,18},{7,19},{8,28},{9,... | collective-permute-start | bytes 245768 | tf_op jit(solution)/shard_map/ppermute | solution.py:250
  19.9 0.2 collective-permute-done.3.refs_4_
  20.1 1.5 %collective-permute-start.8 = (f32[16,1280]{1,0:T(8,128)S(1)}, f32[16,1280]{1,0:T(8,128)S(1)}, u32[]{:S(2)}, u32[]{:S(2)}) collective-permute-start(f32[16,1280]{1,0:T(8,128)S(1)} %get-tuple-element.50), channel_id=1, source_target_pairs={{0,4},{1,5},{2,6},{3,7},{4,0},{5,1},{6,2},{7,3},{8,12},{9,13},{10,... | collective-permute-start | bytes 245768 | tf_op jit(solution)/shard_map/ppermute | solution.py:250
  21.6 0.0 collective-permute-done.4.refs_5_
  21.6 0.0 collective-permute-start.9
  21.6 1.6 %collective-permute-done.5.refs_6_ = f32[16,1280]{1,0:T(8,128)S(1)} collective-permute-done((f32[16,1280]{1,0:T(8,128)S(1)}, f32[16,1280]{1,0:T(8,128)S(1)}, u32[]{:S(2)}, u32[]{:S(2)}) %collective-permute-start.5) | collective-permute-done | bytes 81952 | tf_op jit(solution)/shard_map/ppermute | solution.py:250
  23.3 1.2 %collective-permute-start.10 = (f32[16,1280]{1,0:T(8,128)S(1)}, f32[16,1280]{1,0:T(8,128)S(1)}, u32[]{:S(2)}, u32[]{:S(2)}) collective-permute-start(f32[16,1280]{1,0:T(8,128)S(1)} %get-tuple-element.52), channel_id=1, source_target_pairs={{0,5},{1,4},{2,7},{3,6},{4,1},{5,0},{6,3},{7,2},{8,13},{9,12},{10,... | collective-permute-start | bytes 245768 | tf_op jit(solution)/shard_map/ppermute | solution.py:250
  24.5 0.0 collective-permute-done.6.refs_7_
  24.5 2.0 %collective-permute-start.11 = (f32[16,1280]{1,0:T(8,128)S(1)}, f32[16,1280]{1,0:T(8,128)S(1)}, u32[]{:S(2)}, u32[]{:S(2)}) collective-permute-start(f32[16,1280]{1,0:T(8,128)S(1)} %get-tuple-element.53), channel_id=1, source_target_pairs={{0,22},{1,23},{2,20},{3,21},{4,18},{5,19},{6,16},{7,17},{8,30},{9,... | collective-permute-start | bytes 245768 | tf_op jit(solution)/shard_map/ppermute | solution.py:250
  26.5 0.0 collective-permute-done.7.refs_8_
  26.5 2.0 %collective-permute-start.12 = (f32[16,1280]{1,0:T(8,128)S(1)}, f32[16,1280]{1,0:T(8,128)S(1)}, u32[]{:S(2)}, u32[]{:S(2)}) collective-permute-start(f32[16,1280]{1,0:T(8,128)S(1)} %get-tuple-element.54), channel_id=1, source_target_pairs={{0,6},{1,7},{2,4},{3,5},{4,2},{5,3},{6,0},{7,1},{8,14},{9,15},{10,... | collective-permute-start | bytes 245768 | tf_op jit(solution)/shard_map/ppermute | solution.py:250
  28.5 0.0 collective-permute-done.8.refs_9_
  28.5 1.2 %collective-permute-start.13 = (f32[16,1280]{1,0:T(8,128)S(1)}, f32[16,1280]{1,0:T(8,128)S(1)}, u32[]{:S(2)}, u32[]{:S(2)}) collective-permute-start(f32[16,1280]{1,0:T(8,128)S(1)} %get-tuple-element.55), channel_id=1, source_target_pairs={{0,23},{1,22},{2,21},{3,20},{4,19},{5,18},{6,17},{7,16},{8,31},{9,... | collective-permute-start | bytes 245768 | tf_op jit(solution)/shard_map/ppermute | solution.py:250
  29.7 0.0 collective-permute-done.9.refs_10_
  29.7 2.1 %collective-permute-start.14 = (f32[16,1280]{1,0:T(8,128)S(1)}, f32[16,1280]{1,0:T(8,128)S(1)}, u32[]{:S(2)}, u32[]{:S(2)}) collective-permute-start(f32[16,1280]{1,0:T(8,128)S(1)} %get-tuple-element.56), channel_id=1, source_target_pairs={{0,7},{1,6},{2,5},{3,4},{4,3},{5,2},{6,1},{7,0},{8,15},{9,14},{10,... | collective-permute-start | bytes 245768 | tf_op jit(solution)/shard_map/ppermute | solution.py:250
  31.9 7.1 %collective-permute-start.15 = (f32[16,1280]{1,0:T(8,128)S(1)}, f32[16,1280]{1,0:T(8,128)S(1)}, u32[]{:S(2)}, u32[]{:S(2)}) collective-permute-start(f32[16,1280]{1,0:T(8,128)S(1)} %get-tuple-element.57), channel_id=1, source_target_pairs={{0,24},{1,25},{2,26},{3,27},{4,28},{5,29},{6,30},{7,31},{8,16},{9,... | collective-permute-start | bytes 245768 | tf_op jit(solution)/shard_map/ppermute | solution.py:250
  38.9 0.7 collective-permute-start.17
  39.6 0.0 collective-permute-done.13.refs_14_
  39.6 1.6 %collective-permute-start.18 = (f32[16,1280]{1,0:T(8,128)S(1)}, f32[16,1280]{1,0:T(8,128)S(1)}, u32[]{:S(2)}, u32[]{:S(2)}) collective-permute-start(f32[16,1280]{1,0:T(8,128)S(1)} %get-tuple-element.60), channel_id=1, source_target_pairs={{0,9},{1,8},{2,11},{3,10},{4,13},{5,12},{6,15},{7,14},{8,1},{9,0},... | collective-permute-start | bytes 245768 | tf_op jit(solution)/shard_map/ppermute | solution.py:250
  41.3 0.0 collective-permute-done.14.refs_15_
  41.3 3.4 %collective-permute-start.19 = (f32[16,1280]{1,0:T(8,128)S(1)}, f32[16,1280]{1,0:T(8,128)S(1)}, u32[]{:S(2)}, u32[]{:S(2)}) collective-permute-start(f32[16,1280]{1,0:T(8,128)S(1)} %get-tuple-element.61), channel_id=1, source_target_pairs={{0,26},{1,27},{2,24},{3,25},{4,30},{5,31},{6,28},{7,29},{8,18},{9,... | collective-permute-start | bytes 245768 | tf_op jit(solution)/shard_map/ppermute | solution.py:250
  44.7 0.0 collective-permute-done.15.refs_1_
  44.7 0.8 %collective-permute-start.20 = (f32[16,1280]{1,0:T(8,128)S(1)}, f32[16,1280]{1,0:T(8,128)S(1)}, u32[]{:S(2)}, u32[]{:S(2)}) collective-permute-start(f32[16,1280]{1,0:T(8,128)S(1)} %get-tuple-element.62), channel_id=1, source_target_pairs={{0,10},{1,11},{2,8},{3,9},{4,14},{5,15},{6,12},{7,13},{8,2},{9,3},... | collective-permute-start | bytes 245768 | tf_op jit(solution)/shard_map/ppermute | solution.py:250
  45.6 0.0 collective-permute-done.16.refs_2_
  45.6 2.2 %collective-permute-start.21 = (f32[16,1280]{1,0:T(8,128)S(1)}, f32[16,1280]{1,0:T(8,128)S(1)}, u32[]{:S(2)}, u32[]{:S(2)}) collective-permute-start(f32[16,1280]{1,0:T(8,128)S(1)} %get-tuple-element.63), channel_id=1, source_target_pairs={{0,27},{1,26},{2,25},{3,24},{4,31},{5,30},{6,29},{7,28},{8,19},{9,... | collective-permute-start | bytes 245768 | tf_op jit(solution)/shard_map/ppermute | solution.py:250
  47.7 0.0 collective-permute-done.17.refs_3_
  47.7 0.5 collective-permute-start.22
  48.2 0.0 collective-permute-done.18.refs_4_
  48.2 2.8 %collective-permute-start.23 = (f32[16,1280]{1,0:T(8,128)S(1)}, f32[16,1280]{1,0:T(8,128)S(1)}, u32[]{:S(2)}, u32[]{:S(2)}) collective-permute-start(f32[16,1280]{1,0:T(8,128)S(1)} %get-tuple-element.65), channel_id=1, source_target_pairs={{0,28},{1,29},{2,30},{3,31},{4,24},{5,25},{6,26},{7,27},{8,20},{9,... | collective-permute-start | bytes 245768 | tf_op jit(solution)/shard_map/ppermute | solution.py:250
  51.0 0.0 collective-permute-done.19.refs_5_
  51.0 1.4 %collective-permute-start.24 = (f32[16,1280]{1,0:T(8,128)S(1)}, f32[16,1280]{1,0:T(8,128)S(1)}, u32[]{:S(2)}, u32[]{:S(2)}) collective-permute-start(f32[16,1280]{1,0:T(8,128)S(1)} %get-tuple-element.66), channel_id=1, source_target_pairs={{0,12},{1,13},{2,14},{3,15},{4,8},{5,9},{6,10},{7,11},{8,4},{9,5},... | collective-permute-start | bytes 245768 | tf_op jit(solution)/shard_map/ppermute | solution.py:250
  52.4 0.0 collective-permute-done.20.refs_6_
  52.4 1.2 %collective-permute-start.25 = (f32[16,1280]{1,0:T(8,128)S(1)}, f32[16,1280]{1,0:T(8,128)S(1)}, u32[]{:S(2)}, u32[]{:S(2)}) collective-permute-start(f32[16,1280]{1,0:T(8,128)S(1)} %get-tuple-element.67), channel_id=1, source_target_pairs={{0,29},{1,28},{2,31},{3,30},{4,25},{5,24},{6,27},{7,26},{8,21},{9,... | collective-permute-start | bytes 245768 | tf_op jit(solution)/shard_map/ppermute | solution.py:250
  53.6 0.9 %weights.1 = (bf16[512,512]{1,0:T(8,128)(2,1)S(1)}, bf16[512,512]{1,0:T(8,128)(2,1)S(1)}) custom-call(s32[1]{0:T(128)} %bitcast.me_ref, f32[1,128]{1,0:T(1,128)S(1)} %bitcast.2, s32[1,128]{1,0:T(1,128)S(1)} %copy-done.3), custom_call_target="tpu_custom_call" | custom-call | flops 268435456 | bytes 1048576 | tf_op jit(solution)/shard_map/weights/pallas_call | solution.py:157
  54.5 1.1 %collective-permute-start.26 = (f32[16,1280]{1,0:T(8,128)S(1)}, f32[16,1280]{1,0:T(8,128)S(1)}, u32[]{:S(2)}, u32[]{:S(2)}) collective-permute-start(f32[16,1280]{1,0:T(8,128)S(1)} %get-tuple-element.68), channel_id=1, source_target_pairs={{0,13},{1,12},{2,15},{3,14},{4,9},{5,8},{6,11},{7,10},{8,5},{9,4},... | collective-permute-start | bytes 245768 | tf_op jit(solution)/shard_map/ppermute | solution.py:250
  55.7 0.0 collective-permute-done.22.refs_8_
  55.7 3.5 %collective-permute-start.27 = (f32[16,1280]{1,0:T(8,128)S(1)}, f32[16,1280]{1,0:T(8,128)S(1)}, u32[]{:S(2)}, u32[]{:S(2)}) collective-permute-start(f32[16,1280]{1,0:T(8,128)S(1)} %get-tuple-element.69), channel_id=1, source_target_pairs={{0,30},{1,31},{2,28},{3,29},{4,26},{5,27},{6,24},{7,25},{8,22},{9,... | collective-permute-start | bytes 245768 | tf_op jit(solution)/shard_map/ppermute | solution.py:250
  59.1 0.0 collective-permute-done.23.refs_1_
  59.1 1.6 %collective-permute-start.28 = (f32[16,1280]{1,0:T(8,128)S(1)}, f32[16,1280]{1,0:T(8,128)S(1)}, u32[]{:S(2)}, u32[]{:S(2)}) collective-permute-start(f32[16,1280]{1,0:T(8,128)S(1)} %get-tuple-element.70), channel_id=1, source_target_pairs={{0,14},{1,15},{2,12},{3,13},{4,10},{5,11},{6,8},{7,9},{8,6},{9,7},... | collective-permute-start | bytes 245768 | tf_op jit(solution)/shard_map/ppermute | solution.py:250
  60.8 0.0 collective-permute-done.24.refs_2_
  60.8 1.6 %collective-permute-start.29 = (f32[16,1280]{1,0:T(8,128)S(1)}, f32[16,1280]{1,0:T(8,128)S(1)}, u32[]{:S(2)}, u32[]{:S(2)}) collective-permute-start(f32[16,1280]{1,0:T(8,128)S(1)} %get-tuple-element.71), channel_id=1, source_target_pairs={{0,31},{1,30},{2,29},{3,28},{4,27},{5,26},{6,25},{7,24},{8,23},{9,... | collective-permute-start | bytes 245768 | tf_op jit(solution)/shard_map/ppermute | solution.py:250
  62.4 0.0 collective-permute-done.25.refs_3_
  62.4 1.6 %collective-permute-start.30 = (f32[16,1280]{1,0:T(8,128)S(1)}, f32[16,1280]{1,0:T(8,128)S(1)}, u32[]{:S(2)}, u32[]{:S(2)}) collective-permute-start(f32[16,1280]{1,0:T(8,128)S(1)} %get-tuple-element.72), channel_id=1, source_target_pairs={{0,15},{1,14},{2,13},{3,12},{4,11},{5,10},{6,9},{7,8},{8,7},{9,6},... | collective-permute-start | bytes 245768 | tf_op jit(solution)/shard_map/ppermute | solution.py:250
  64.0 1.2 %temporal.3.refs_0_ = f32[512,1280]{1,0:T(8,128)S(1)} custom-call(bf16[512,512]{1,0:T(8,128)(2,1)S(1)} %get-tuple-element.39.high_ref, bf16[512,512]{1,0:T(8,128)(2,1)S(1)} %get-tuple-element.40.low_ref, f32[16,1280]{1,0:T(8,128)S(1)} %get-tuple-element.41.refs_0_, f32[16,1280]{1,0:T(8,128)S(1)} %collective-permute-done.refs_1_, ...), custom_call_target="tpu_custom_call" | custom-call | flops 1006632960 | bytes 5242880 | tf_op jit(solution)/shard_map/temporal/pallas_call | solution.py:218
  65.2 1.2 %temporal.4.refs_0_ = f32[512,1280]{1,0:T(8,128)S(1)} custom-call(bf16[512,512]{1,0:T(8,128)(2,1)S(1)} %get-tuple-element.39.high_ref, bf16[512,512]{1,0:T(8,128)(2,1)S(1)} %get-tuple-element.40.low_ref, f32[512,1280]{1,0:T(8,128)S(1)} %temporal.3.refs_0_, f32[16,1280]{1,0:T(8,128)S(1)} %collective-permute-done.15.refs_1_, ...), custom_call_target="tpu_custom_call" | custom-call | flops 503316480 | bytes 5242880 | tf_op jit(solution)/shard_map/temporal/pallas_call | solution.py:218
  66.3 0.0 collective-permute-done.27.refs_5_
  66.4 0.3 collective-permute-done.28.refs_6_
  66.6 2.6 %collective-permute-done.29.refs_7_ = f32[16,1280]{1,0:T(8,128)S(1)} collective-permute-done((f32[16,1280]{1,0:T(8,128)S(1)}, f32[16,1280]{1,0:T(8,128)S(1)}, u32[]{:S(2)}, u32[]{:S(2)}) %collective-permute-start.29) | collective-permute-done | bytes 81952 | tf_op jit(solution)/shard_map/ppermute | solution.py:250
  69.2 1.1 %collective-permute-done.30.refs_8_ = f32[16,1280]{1,0:T(8,128)S(1)} collective-permute-done((f32[16,1280]{1,0:T(8,128)S(1)}, f32[16,1280]{1,0:T(8,128)S(1)}, u32[]{:S(2)}, u32[]{:S(2)}) %collective-permute-start.30) | collective-permute-done | bytes 81952 | tf_op jit(solution)/shard_map/ppermute | solution.py:250
  70.3 2.9 %temporal.5 = f32[128,4,1280]{2,1,0:T(4,128)} custom-call(bf16[512,512]{1,0:T(8,128)(2,1)S(1)} %get-tuple-element.39.high_ref, bf16[512,512]{1,0:T(8,128)(2,1)S(1)} %get-tuple-element.40.low_ref, f32[512,1280]{1,0:T(8,128)S(1)} %temporal.4.refs_0_, f32[16,1280]{1,0:T(8,128)S(1)} %collective-permute-done.23.refs_1_, ...), custom_call_target="tpu_custom_call" | custom-call | flops 503316480 | bytes 5242880 | tf_op jit(solution)/shard_map/temporal/pallas_call | solution.py:218
  (12 shorter events, 0.0 us)
Async XLA Ops:
  0.0 1.7 %copy-start = (f32[4,128,1280]{2,1,0:T(8,128)S(1)}, f32[4,128,1280]{2,1,0:T(8,128)}, u32[]{:S(2)}) copy-start(f32[4,128,1280]{2,1,0:T(8,128)} %frames_ref.3) | copy-start | bytes 7864324
  1.7 0.7 copy-start.1
  2.4 51.2 %copy-start.2 = (f32[128]{0:T(128)S(1)}, f32[128]{0:T(128)}, u32[]{:S(2)}) copy-start(f32[128]{0:T(128)} %param.5) | copy-start | bytes 1540
  2.4 51.2 %copy-start.3 = (s32[1,128]{1,0:T(1,128)S(1)}, s32[1,128]{1,0:T(1,128)}, u32[]{:S(2)}) copy-start(s32[1,128]{1,0:T(1,128)} %constant.6.clone.partner_ref) | copy-start | bytes 1540
  3.4 11.5 %collective-permute-start = (f32[16,1280]{1,0:T(8,128)S(1)}, f32[16,1280]{1,0:T(8,128)S(1)}, u32[]{:S(2)}, u32[]{:S(2)}) collective-permute-start(f32[16,1280]{1,0:T(8,128)S(1)} %get-tuple-element.42), channel_id=1, source_target_pairs={{0,16},{1,17},{2,18},{3,19},{4,20},{5,21},{6,22},{7,23},{8,24},{9,... | collective-permute-start | bytes 245768 | tf_op jit(solution)/shard_map/ppermute | solution.py:250
  7.5 7.8 %collective-permute-start.1 = (f32[16,1280]{1,0:T(8,128)S(1)}, f32[16,1280]{1,0:T(8,128)S(1)}, u32[]{:S(2)}, u32[]{:S(2)}) collective-permute-start(f32[16,1280]{1,0:T(8,128)S(1)} %get-tuple-element.43), channel_id=1, source_target_pairs={{0,17},{1,16},{2,19},{3,18},{4,21},{5,20},{6,23},{7,22},{8,25},{9,... | collective-permute-start | bytes 245768 | tf_op jit(solution)/shard_map/ppermute | solution.py:250
  10.3 8.6 %collective-permute-start.2 = (f32[16,1280]{1,0:T(8,128)S(1)}, f32[16,1280]{1,0:T(8,128)S(1)}, u32[]{:S(2)}, u32[]{:S(2)}) collective-permute-start(f32[16,1280]{1,0:T(8,128)S(1)} %get-tuple-element.44), channel_id=1, source_target_pairs={{0,1},{1,0},{2,3},{3,2},{4,5},{5,4},{6,7},{7,6},{8,9},{9,8},{10,11... | collective-permute-start | bytes 245768 | tf_op jit(solution)/shard_map/ppermute | solution.py:250
  10.6 9.5 %collective-permute-start.3 = (f32[16,1280]{1,0:T(8,128)S(1)}, f32[16,1280]{1,0:T(8,128)S(1)}, u32[]{:S(2)}, u32[]{:S(2)}) collective-permute-start(f32[16,1280]{1,0:T(8,128)S(1)} %get-tuple-element.45), channel_id=1, source_target_pairs={{0,18},{1,19},{2,16},{3,17},{4,22},{5,23},{6,20},{7,21},{8,26},{9,... | collective-permute-start | bytes 245768 | tf_op jit(solution)/shard_map/ppermute | solution.py:250
  14.3 7.3 %collective-permute-start.4 = (f32[16,1280]{1,0:T(8,128)S(1)}, f32[16,1280]{1,0:T(8,128)S(1)}, u32[]{:S(2)}, u32[]{:S(2)}) collective-permute-start(f32[16,1280]{1,0:T(8,128)S(1)} %get-tuple-element.46), channel_id=1, source_target_pairs={{0,2},{1,3},{2,0},{3,1},{4,6},{5,7},{6,4},{7,5},{8,10},{9,11},{10,... | collective-permute-start | bytes 245768 | tf_op jit(solution)/shard_map/ppermute | solution.py:250
  14.9 8.4 %collective-permute-start.5 = (f32[16,1280]{1,0:T(8,128)S(1)}, f32[16,1280]{1,0:T(8,128)S(1)}, u32[]{:S(2)}, u32[]{:S(2)}) collective-permute-start(f32[16,1280]{1,0:T(8,128)S(1)} %get-tuple-element.47), channel_id=1, source_target_pairs={{0,19},{1,18},{2,17},{3,16},{4,23},{5,22},{6,21},{7,20},{8,27},{9,... | collective-permute-start | bytes 245768 | tf_op jit(solution)/shard_map/ppermute | solution.py:250
  15.3 9.2 %collective-permute-start.6 = (f32[16,1280]{1,0:T(8,128)S(1)}, f32[16,1280]{1,0:T(8,128)S(1)}, u32[]{:S(2)}, u32[]{:S(2)}) collective-permute-start(f32[16,1280]{1,0:T(8,128)S(1)} %get-tuple-element.48), channel_id=1, source_target_pairs={{0,3},{1,2},{2,1},{3,0},{4,7},{5,6},{6,5},{7,4},{8,11},{9,10},{10,... | collective-permute-start | bytes 245768 | tf_op jit(solution)/shard_map/ppermute | solution.py:250
  18.9 7.6 %collective-permute-start.7 = (f32[16,1280]{1,0:T(8,128)S(1)}, f32[16,1280]{1,0:T(8,128)S(1)}, u32[]{:S(2)}, u32[]{:S(2)}) collective-permute-start(f32[16,1280]{1,0:T(8,128)S(1)} %get-tuple-element.49), channel_id=1, source_target_pairs={{0,20},{1,21},{2,22},{3,23},{4,16},{5,17},{6,18},{7,19},{8,28},{9,... | collective-permute-start | bytes 245768 | tf_op jit(solution)/shard_map/ppermute | solution.py:250
  20.1 8.4 %collective-permute-start.8 = (f32[16,1280]{1,0:T(8,128)S(1)}, f32[16,1280]{1,0:T(8,128)S(1)}, u32[]{:S(2)}, u32[]{:S(2)}) collective-permute-start(f32[16,1280]{1,0:T(8,128)S(1)} %get-tuple-element.50), channel_id=1, source_target_pairs={{0,4},{1,5},{2,6},{3,7},{4,0},{5,1},{6,2},{7,3},{8,12},{9,13},{10,... | collective-permute-start | bytes 245768 | tf_op jit(solution)/shard_map/ppermute | solution.py:250
  21.6 8.1 %collective-permute-start.9 = (f32[16,1280]{1,0:T(8,128)S(1)}, f32[16,1280]{1,0:T(8,128)S(1)}, u32[]{:S(2)}, u32[]{:S(2)}) collective-permute-start(f32[16,1280]{1,0:T(8,128)S(1)} %get-tuple-element.51), channel_id=1, source_target_pairs={{0,21},{1,20},{2,23},{3,22},{4,17},{5,16},{6,19},{7,18},{8,29},{9,... | collective-permute-start | bytes 245768 | tf_op jit(solution)/shard_map/ppermute | solution.py:250
  23.3 8.6 %collective-permute-start.10 = (f32[16,1280]{1,0:T(8,128)S(1)}, f32[16,1280]{1,0:T(8,128)S(1)}, u32[]{:S(2)}, u32[]{:S(2)}) collective-permute-start(f32[16,1280]{1,0:T(8,128)S(1)} %get-tuple-element.52), channel_id=1, source_target_pairs={{0,5},{1,4},{2,7},{3,6},{4,1},{5,0},{6,3},{7,2},{8,13},{9,12},{10,... | collective-permute-start | bytes 245768 | tf_op jit(solution)/shard_map/ppermute | solution.py:250
  24.5 14.5 %collective-permute-start.11 = (f32[16,1280]{1,0:T(8,128)S(1)}, f32[16,1280]{1,0:T(8,128)S(1)}, u32[]{:S(2)}, u32[]{:S(2)}) collective-permute-start(f32[16,1280]{1,0:T(8,128)S(1)} %get-tuple-element.53), channel_id=1, source_target_pairs={{0,22},{1,23},{2,20},{3,21},{4,18},{5,19},{6,16},{7,17},{8,30},{9,... | collective-permute-start | bytes 245768 | tf_op jit(solution)/shard_map/ppermute | solution.py:250
  26.5 12.5 %collective-permute-start.12 = (f32[16,1280]{1,0:T(8,128)S(1)}, f32[16,1280]{1,0:T(8,128)S(1)}, u32[]{:S(2)}, u32[]{:S(2)}) collective-permute-start(f32[16,1280]{1,0:T(8,128)S(1)} %get-tuple-element.54), channel_id=1, source_target_pairs={{0,6},{1,7},{2,4},{3,5},{4,2},{5,3},{6,0},{7,1},{8,14},{9,15},{10,... | collective-permute-start | bytes 245768 | tf_op jit(solution)/shard_map/ppermute | solution.py:250
  28.5 11.1 %collective-permute-start.13 = (f32[16,1280]{1,0:T(8,128)S(1)}, f32[16,1280]{1,0:T(8,128)S(1)}, u32[]{:S(2)}, u32[]{:S(2)}) collective-permute-start(f32[16,1280]{1,0:T(8,128)S(1)} %get-tuple-element.55), channel_id=1, source_target_pairs={{0,23},{1,22},{2,21},{3,20},{4,19},{5,18},{6,17},{7,16},{8,31},{9,... | collective-permute-start | bytes 245768 | tf_op jit(solution)/shard_map/ppermute | solution.py:250
  29.7 11.6 %collective-permute-start.14 = (f32[16,1280]{1,0:T(8,128)S(1)}, f32[16,1280]{1,0:T(8,128)S(1)}, u32[]{:S(2)}, u32[]{:S(2)}) collective-permute-start(f32[16,1280]{1,0:T(8,128)S(1)} %get-tuple-element.56), channel_id=1, source_target_pairs={{0,7},{1,6},{2,5},{3,4},{4,3},{5,2},{6,1},{7,0},{8,15},{9,14},{10,... | collective-permute-start | bytes 245768 | tf_op jit(solution)/shard_map/ppermute | solution.py:250
  31.9 12.9 %collective-permute-start.15 = (f32[16,1280]{1,0:T(8,128)S(1)}, f32[16,1280]{1,0:T(8,128)S(1)}, u32[]{:S(2)}, u32[]{:S(2)}) collective-permute-start(f32[16,1280]{1,0:T(8,128)S(1)} %get-tuple-element.57), channel_id=1, source_target_pairs={{0,24},{1,25},{2,26},{3,27},{4,28},{5,29},{6,30},{7,31},{8,16},{9,... | collective-permute-start | bytes 245768 | tf_op jit(solution)/shard_map/ppermute | solution.py:250
  38.9 6.6 %collective-permute-start.16 = (f32[16,1280]{1,0:T(8,128)S(1)}, f32[16,1280]{1,0:T(8,128)S(1)}, u32[]{:S(2)}, u32[]{:S(2)}) collective-permute-start(f32[16,1280]{1,0:T(8,128)S(1)} %get-tuple-element.58), channel_id=1, source_target_pairs={{0,8},{1,9},{2,10},{3,11},{4,12},{5,13},{6,14},{7,15},{8,0},{9,1},... | collective-permute-start | bytes 245768 | tf_op jit(solution)/shard_map/ppermute | solution.py:250
  38.9 8.8 %collective-permute-start.17 = (f32[16,1280]{1,0:T(8,128)S(1)}, f32[16,1280]{1,0:T(8,128)S(1)}, u32[]{:S(2)}, u32[]{:S(2)}) collective-permute-start(f32[16,1280]{1,0:T(8,128)S(1)} %get-tuple-element.59), channel_id=1, source_target_pairs={{0,25},{1,24},{2,27},{3,26},{4,29},{5,28},{6,31},{7,30},{8,17},{9,... | collective-permute-start | bytes 245768 | tf_op jit(solution)/shard_map/ppermute | solution.py:250
  39.6 8.6 %collective-permute-start.18 = (f32[16,1280]{1,0:T(8,128)S(1)}, f32[16,1280]{1,0:T(8,128)S(1)}, u32[]{:S(2)}, u32[]{:S(2)}) collective-permute-start(f32[16,1280]{1,0:T(8,128)S(1)} %get-tuple-element.60), channel_id=1, source_target_pairs={{0,9},{1,8},{2,11},{3,10},{4,13},{5,12},{6,15},{7,14},{8,1},{9,0},... | collective-permute-start | bytes 245768 | tf_op jit(solution)/shard_map/ppermute | solution.py:250
  41.3 9.7 %collective-permute-start.19 = (f32[16,1280]{1,0:T(8,128)S(1)}, f32[16,1280]{1,0:T(8,128)S(1)}, u32[]{:S(2)}, u32[]{:S(2)}) collective-permute-start(f32[16,1280]{1,0:T(8,128)S(1)} %get-tuple-element.61), channel_id=1, source_target_pairs={{0,26},{1,27},{2,24},{3,25},{4,30},{5,31},{6,28},{7,29},{8,18},{9,... | collective-permute-start | bytes 245768 | tf_op jit(solution)/shard_map/ppermute | solution.py:250
  44.7 7.7 %collective-permute-start.20 = (f32[16,1280]{1,0:T(8,128)S(1)}, f32[16,1280]{1,0:T(8,128)S(1)}, u32[]{:S(2)}, u32[]{:S(2)}) collective-permute-start(f32[16,1280]{1,0:T(8,128)S(1)} %get-tuple-element.62), channel_id=1, source_target_pairs={{0,10},{1,11},{2,8},{3,9},{4,14},{5,15},{6,12},{7,13},{8,2},{9,3},... | collective-permute-start | bytes 245768 | tf_op jit(solution)/shard_map/ppermute | solution.py:250
  45.6 9.0 %collective-permute-start.21 = (f32[16,1280]{1,0:T(8,128)S(1)}, f32[16,1280]{1,0:T(8,128)S(1)}, u32[]{:S(2)}, u32[]{:S(2)}) collective-permute-start(f32[16,1280]{1,0:T(8,128)S(1)} %get-tuple-element.63), channel_id=1, source_target_pairs={{0,27},{1,26},{2,25},{3,24},{4,31},{5,30},{6,29},{7,28},{8,19},{9,... | collective-permute-start | bytes 245768 | tf_op jit(solution)/shard_map/ppermute | solution.py:250
  47.7 8.0 %collective-permute-start.22 = (f32[16,1280]{1,0:T(8,128)S(1)}, f32[16,1280]{1,0:T(8,128)S(1)}, u32[]{:S(2)}, u32[]{:S(2)}) collective-permute-start(f32[16,1280]{1,0:T(8,128)S(1)} %get-tuple-element.64), channel_id=1, source_target_pairs={{0,11},{1,10},{2,9},{3,8},{4,15},{5,14},{6,13},{7,12},{8,3},{9,2},... | collective-permute-start | bytes 245768 | tf_op jit(solution)/shard_map/ppermute | solution.py:250
  48.2 10.9 %collective-permute-start.23 = (f32[16,1280]{1,0:T(8,128)S(1)}, f32[16,1280]{1,0:T(8,128)S(1)}, u32[]{:S(2)}, u32[]{:S(2)}) collective-permute-start(f32[16,1280]{1,0:T(8,128)S(1)} %get-tuple-element.65), channel_id=1, source_target_pairs={{0,28},{1,29},{2,30},{3,31},{4,24},{5,25},{6,26},{7,27},{8,20},{9,... | collective-permute-start | bytes 245768 | tf_op jit(solution)/shard_map/ppermute | solution.py:250
  51.0 9.8 %collective-permute-start.24 = (f32[16,1280]{1,0:T(8,128)S(1)}, f32[16,1280]{1,0:T(8,128)S(1)}, u32[]{:S(2)}, u32[]{:S(2)}) collective-permute-start(f32[16,1280]{1,0:T(8,128)S(1)} %get-tuple-element.66), channel_id=1, source_target_pairs={{0,12},{1,13},{2,14},{3,15},{4,8},{5,9},{6,10},{7,11},{8,4},{9,5},... | collective-permute-start | bytes 245768 | tf_op jit(solution)/shard_map/ppermute | solution.py:250
  52.4 10.0 %collective-permute-start.25 = (f32[16,1280]{1,0:T(8,128)S(1)}, f32[16,1280]{1,0:T(8,128)S(1)}, u32[]{:S(2)}, u32[]{:S(2)}) collective-permute-start(f32[16,1280]{1,0:T(8,128)S(1)} %get-tuple-element.67), channel_id=1, source_target_pairs={{0,29},{1,28},{2,31},{3,30},{4,25},{5,24},{6,27},{7,26},{8,21},{9,... | collective-permute-start | bytes 245768 | tf_op jit(solution)/shard_map/ppermute | solution.py:250
  54.5 11.8 %collective-permute-start.26 = (f32[16,1280]{1,0:T(8,128)S(1)}, f32[16,1280]{1,0:T(8,128)S(1)}, u32[]{:S(2)}, u32[]{:S(2)}) collective-permute-start(f32[16,1280]{1,0:T(8,128)S(1)} %get-tuple-element.68), channel_id=1, source_target_pairs={{0,13},{1,12},{2,15},{3,14},{4,9},{5,8},{6,11},{7,10},{8,5},{9,4},... | collective-permute-start | bytes 245768 | tf_op jit(solution)/shard_map/ppermute | solution.py:250
  55.7 10.7 %collective-permute-start.27 = (f32[16,1280]{1,0:T(8,128)S(1)}, f32[16,1280]{1,0:T(8,128)S(1)}, u32[]{:S(2)}, u32[]{:S(2)}) collective-permute-start(f32[16,1280]{1,0:T(8,128)S(1)} %get-tuple-element.69), channel_id=1, source_target_pairs={{0,30},{1,31},{2,28},{3,29},{4,26},{5,27},{6,24},{7,25},{8,22},{9,... | collective-permute-start | bytes 245768 | tf_op jit(solution)/shard_map/ppermute | solution.py:250
  59.1 7.5 %collective-permute-start.28 = (f32[16,1280]{1,0:T(8,128)S(1)}, f32[16,1280]{1,0:T(8,128)S(1)}, u32[]{:S(2)}, u32[]{:S(2)}) collective-permute-start(f32[16,1280]{1,0:T(8,128)S(1)} %get-tuple-element.70), channel_id=1, source_target_pairs={{0,14},{1,15},{2,12},{3,13},{4,10},{5,11},{6,8},{7,9},{8,6},{9,7},... | collective-permute-start | bytes 245768 | tf_op jit(solution)/shard_map/ppermute | solution.py:250
  60.8 8.4 %collective-permute-start.29 = (f32[16,1280]{1,0:T(8,128)S(1)}, f32[16,1280]{1,0:T(8,128)S(1)}, u32[]{:S(2)}, u32[]{:S(2)}) collective-permute-start(f32[16,1280]{1,0:T(8,128)S(1)} %get-tuple-element.71), channel_id=1, source_target_pairs={{0,31},{1,30},{2,29},{3,28},{4,27},{5,26},{6,25},{7,24},{8,23},{9,... | collective-permute-start | bytes 245768 | tf_op jit(solution)/shard_map/ppermute | solution.py:250
  62.4 7.9 %collective-permute-start.30 = (f32[16,1280]{1,0:T(8,128)S(1)}, f32[16,1280]{1,0:T(8,128)S(1)}, u32[]{:S(2)}, u32[]{:S(2)}) collective-permute-start(f32[16,1280]{1,0:T(8,128)S(1)} %get-tuple-element.72), channel_id=1, source_target_pairs={{0,15},{1,14},{2,13},{3,12},{4,11},{5,10},{6,9},{7,8},{8,7},{9,6},... | collective-permute-start | bytes 245768 | tf_op jit(solution)/shard_map/ppermute | solution.py:250

commit v2 on v1

v2 whole, which is shorter than its diff:
```python
import functools

import jax
import jax.numpy as jnp
from jax import lax
from jax.experimental import pallas as pl
from jax.experimental.pallas import tpu as pltpu
from jax.sharding import PartitionSpec as P


BAND = 24
SUBLANES = 8
VMEM_BYTES = 67043328
KERNEL_BYTES = 20 << 20
ROOM = 256 << 10
FIRST, SECOND = 2, 2
LAST_ROWS = 64
WIDTH = 256
STEPS = 8
AHEAD = 2
VMEM = pltpu.VMEM
SMEM = pltpu.SMEM


def message_order(devices):
    half = devices // 2
    across = [half ^ low for low in range(half)]
    within = list(range(half // 2, half)) + list(range(1, half // 2))
    order = across[:AHEAD]
    for pair in zip(within, across[AHEAD:]):
        order.extend(pair)
    return order + within[half - AHEAD :]


def filter_tile(me, tap, above, here, below, tile, tiles, rows):
    row = lax.broadcasted_iota(jnp.int32, here.shape, 0)
    column = lax.broadcasted_iota(jnp.int32, here.shape, 1)
    columns = here.shape[1]
    above = jnp.where(tile > 0, above, 0.0)
    below = jnp.where(tile < tiles - 1, below, 0.0)
    over = pltpu.roll(jnp.where(row == SUBLANES - 1, above, here), 1, 0)
    under = pltpu.roll(jnp.where(row == 0, below, here), SUBLANES - 1, 0)
    left, center, right = (
        tap[0][b] * over + tap[1][b] * here + tap[2][b] * under for b in range(3)
    )
    left = jnp.where(column == 0, 0.0, pltpu.roll(left, 1, 1))
    right = jnp.where(column == columns - 1, 0.0, pltpu.roll(right, columns - 1, 1))
    value = left + center + right
    step = rows
    while step < SUBLANES:
        swapped = jnp.where(
            (row & step) == 0,
            pltpu.roll(value, SUBLANES - step, 0),
            pltpu.roll(value, step, 0),
        )
        value = jnp.where((me * rows) & step == 0, value, swapped)
        step *= 2
    return value


def tile_rows(tile, tiles):
    spots = (jnp.maximum(tile - 1, 0), tile, jnp.minimum(tile + 1, tiles - 1))
    return [pl.ds(pl.multiple_of(spot * SUBLANES, SUBLANES), SUBLANES) for spot in spots]


def stencil_kernel(kernel_ref, frames_ref, *refs, groups, rows, direct):
    count, height, _ = frames_ref.shape
    strips = SUBLANES // rows
    tiles = height // SUBLANES
    outs = len(groups) * strips
    out_refs, (tap_ref, tap_sem), scratch = refs[:outs], refs[outs : outs + 2], refs[outs + 2 :]
    me = lax.axis_index("blk")
    copies = [pltpu.make_async_copy(kernel_ref, tap_ref, tap_sem)]
    if direct:
        near_ref, near_sem = scratch
        for place, group in enumerate(groups):
            spans = tile_rows((me // strips) ^ group, tiles)
            for part, span in enumerate(spans):
                copies.append(
                    pltpu.make_async_copy(
                        frames_ref.at[:, span, :],
                        near_ref.at[place, part],
                        near_sem.at[place, part],
                    )
                )
    for copy in copies:
        copy.start()
    for copy in copies:
        copy.wait()
    tap = [[tap_ref[a, b] for b in range(3)] for a in range(3)]
    for place, group in enumerate(groups):
        tile = (me // strips) ^ group
        spans = tile_rows(tile, tiles)
        for frame in range(count):
            if direct:
                parts = [near_ref[place, part, frame] for part in range(3)]
            else:
                parts = [frames_ref[frame, span, :] for span in spans]
            value = filter_tile(me, tap, *parts, tile, tiles, rows)
            for strip in range(strips):
                out_refs[place * strips + strip][frame * rows : (frame + 1) * rows, :] = value[
                    strip * rows : (strip + 1) * rows, :
                ]


def stencil(kernel, frames, groups, rows, direct):
    count, _, columns = frames.shape
    strips = SUBLANES // rows
    outs = len(groups) * strips
    size = count * rows * columns
    scratch = [SMEM(kernel.shape, jnp.float32), pltpu.SemaphoreType.DMA]
    if direct:
        scratch += [
            VMEM((len(groups), 3, count, SUBLANES, columns), jnp.float32),
            pltpu.SemaphoreType.DMA((len(groups), 3)),
        ]
    return pl.pallas_call(
        functools.partial(stencil_kernel, groups=groups, rows=rows, direct=direct),
        in_specs=[
            pl.BlockSpec(memory_space=pltpu.HBM),
            pl.BlockSpec(memory_space=pltpu.HBM if direct else VMEM),
        ],
        out_specs=[pl.BlockSpec(memory_space=VMEM)] * outs,
        out_shape=[jax.ShapeDtypeStruct((count * rows, columns), jnp.float32)] * outs,
        scratch_shapes=scratch,
        cost_estimate=pl.CostEstimate(
            flops=18 * size * outs, bytes_accessed=8 * size * outs, transcendentals=0
        ),
        compiler_params=pltpu.CompilerParams(
            vmem_limit_bytes=VMEM_BYTES - 4 * size * outs - ROOM if direct else KERNEL_BYTES
        ),
        name="stencil",
    )(kernel, frames)


def weights_kernel(
    widths_ref, partner_ref, high_ref, low_ref, last_ref, *, count, rows
):
    length = widths_ref.shape[1]
    size = length * rows
    tail = last_ref.shape[1] // 3
    square = (length, length)

    def iota(shape, axis):
        return lax.broadcasted_iota(jnp.int32, shape, axis)

    frame = lax.rem(iota(square, 1), count)
    source = count * (lax.axis_index("blk") ^ partner_ref[...]) + frame
    spread = jnp.broadcast_to(widths_ref[...], square).T
    offset = (iota(square, 0) - source).astype(jnp.float32)
    values = jnp.where(
        jnp.abs(offset) <= BAND, jnp.exp(-offset * offset / (2.0 * spread * spread)), 0.0
    )
    matrix = values / jnp.sum(values, axis=1, keepdims=True)
    high = matrix.astype(jnp.bfloat16)
    low = (matrix - high.astype(jnp.float32)).astype(jnp.bfloat16)

    tall, wide, full = (size, length), (length, size), (size, size)
    down = (iota(tall, 0) // rows == iota(tall, 1)).astype(jnp.bfloat16)
    along = (iota(wide, 0) == iota(wide, 1) // rows).astype(jnp.bfloat16)
    same = lax.rem(iota(full, 0), rows) == lax.rem(iota(full, 1), rows)
    dot = functools.partial(jnp.dot, preferred_element_type=jnp.float32)
    for piece, out_ref in ((high, high_ref), (low, low_ref)):
        wider = dot(down, dot(piece, along).astype(jnp.bfloat16))
        out_ref[...] = jnp.where(same, wider, 0.0).astype(jnp.bfloat16)

    wide, full = (length, 3 * tail), (size, 3 * tail)
    column = size - tail + lax.rem(iota(wide, 1), tail)
    along = iota(wide, 0) == column // rows
    is_high = iota(wide, 1) < 2 * tail
    picked = dot(high, (along & is_high).astype(jnp.bfloat16)) + dot(
        low, (along & ~is_high).astype(jnp.bfloat16)
    )
    same = lax.rem(iota(full, 0), rows) == lax.rem(iota(full, 1), rows)
    wider = dot(down, picked.astype(jnp.bfloat16))
    last_ref[...] = jnp.where(same, wider, 0.0).astype(jnp.bfloat16)


def spread_weights(widths, partners, count, rows):
    size = widths.shape[0] * rows
    columns = [partner for partner in partners for _ in range(count)]
    shapes = [(size, size), (size, size), (size, 3 * LAST_ROWS)]
    return pl.pallas_call(
        functools.partial(weights_kernel, count=count, rows=rows),
        in_specs=[pl.BlockSpec(memory_space=VMEM)] * 2,
        out_specs=[pl.BlockSpec(memory_space=VMEM)] * 3,
        out_shape=[jax.ShapeDtypeStruct(shape, jnp.bfloat16) for shape in shapes],
        cost_estimate=pl.CostEstimate(
            flops=2 * size**3, bytes_accessed=4 * size**2, transcendentals=size
        ),
        compiler_params=pltpu.CompilerParams(vmem_limit_bytes=KERNEL_BYTES),
        name="weights",
    )(widths[None, :], jnp.array([columns], jnp.int32))


def split(part):
    high = part.astype(jnp.bfloat16)
    return high, (part - high.astype(jnp.float32)).astype(jnp.bfloat16)


def gather_kernel(high_ref, low_ref, *refs, begin, end, first):
    parts, out_ref = refs[:-1], refs[-1]
    if not first:
        so_far, parts = parts[0], parts[1:]
    dot = functools.partial(jnp.dot, preferred_element_type=jnp.float32)
    high, low = high_ref[:, begin:end], low_ref[:, begin:end]
    for start in range(0, out_ref.shape[1], WIDTH):
        span = slice(start, start + WIDTH)
        part_high, part_low = split(jnp.concatenate([ref[:, span] for ref in parts], axis=0))
        value = dot(high, part_high) + dot(high, part_low) + dot(low, part_high)
        out_ref[:, span] = value if first else so_far[:, span] + value


def gather(high, low, so_far, parts, begin, end):
    size, columns = high.shape[0], parts[0].shape[1]
    ins = ([] if so_far is None else [so_far]) + list(parts)
    return pl.pallas_call(
        functools.partial(gather_kernel, begin=begin, end=end, first=so_far is None),
        in_specs=[pl.BlockSpec(memory_space=VMEM)] * (2 + len(ins)),
        out_specs=pl.BlockSpec(memory_space=VMEM),
        out_shape=jax.ShapeDtypeStruct((size, columns), jnp.float32),
        cost_estimate=pl.CostEstimate(
            flops=6 * size * (end - begin) * columns,
            bytes_accessed=8 * size * columns,
            transcendentals=0,
        ),
        compiler_params=pltpu.CompilerParams(vmem_limit_bytes=KERNEL_BYTES),
        name="temporal",
    )(high, low, *ins)


def finish_kernel(weights_ref, so_far, *refs, steps):
    parts, (out_ref, done_ref, semaphores) = refs[:-3], refs[-3:]
    times, rows, columns = out_ref.shape
    step = times // steps
    part_high, part_low = split(jnp.concatenate([ref[...] for ref in parts], axis=0))
    part = jnp.concatenate([part_high, part_low, part_high], axis=0)
    copies = []
    for at in range(steps):
        span = slice(at * step * rows, (at + 1) * step * rows)
        value = jnp.dot(weights_ref[span, :], part, preferred_element_type=jnp.float32)
        done_ref[at] = (so_far[span, :] + value).reshape(step, rows, columns)
        copies.append(
            pltpu.make_async_copy(
                done_ref.at[at], out_ref.at[at * step : (at + 1) * step], semaphores.at[at]
            )
        )
        copies[-1].start()
    for copy in copies:
        copy.wait()


def finish(weights, so_far, parts, rows):
    size, columns = so_far.shape
    shape = (size // rows, rows, columns)
    return pl.pallas_call(
        functools.partial(finish_kernel, steps=STEPS),
        in_specs=[pl.BlockSpec(memory_space=VMEM)] * (2 + len(parts)),
        out_specs=pl.BlockSpec(memory_space=pltpu.HBM),
        out_shape=jax.ShapeDtypeStruct(shape, jnp.float32),
        scratch_shapes=[
            VMEM((STEPS, shape[0] // STEPS, rows, columns), jnp.float32),
            pltpu.SemaphoreType.DMA((STEPS,)),
        ],
        cost_estimate=pl.CostEstimate(
            flops=2 * size * weights.shape[1] * columns,
            bytes_accessed=8 * size * columns,
            transcendentals=0,
        ),
        compiler_params=pltpu.CompilerParams(vmem_limit_bytes=KERNEL_BYTES),
        name="finish",
    )(weights, so_far, *parts)


def local(frames, widths, kernel, *, devices):
    count, height, _ = frames.shape
    rows = height // devices
    strips = SUBLANES // rows
    order = message_order(devices)
    partners = [0] + order
    every = list(dict.fromkeys(k // strips for k in order))
    messages = {}
    ends = stencil_ends(len(every))
    for stage, (begin, end) in enumerate(zip((0,) + ends[:-1], ends)):
        groups = tuple(every[begin:end])
        outs = stencil(kernel, frames, groups, rows, stage == 0)
        for place, group in enumerate(groups):
            for strip in range(strips):
                messages[group * strips + strip] = outs[place * strips + strip]
    arrived = [messages[0]]
    for k in order:
        pairs = [(i, i ^ k) for i in range(devices)]
        arrived.append(lax.ppermute(messages[k], "blk", pairs))
    high, low, last = spread_weights(widths, partners, count, rows)
    total = None
    each = count * rows
    cuts = temporal_cuts(devices, each)
    for begin, end in zip(cuts[:-1], cuts[1:]):
        part = arrived[begin:end]
        total = gather(high, low, total, part, begin * each, end * each)
    return finish(last, total, arrived[cuts[-1] :], rows)


def stencil_ends(groups):
    return (FIRST, FIRST + SECOND, groups)


def temporal_cuts(devices, each):
    return [0, devices // 2, devices - LAST_ROWS // each]


def solution(mesh):
    devices = mesh.shape["blk"]
    return jax.shard_map(
        functools.partial(local, devices=devices),
        mesh=mesh,
        in_specs=(P("blk", None, None), P(), P()),
        out_specs=P(None, "blk", None),
        check_vma=False,
    )
```

time: 73.4 us -> 76.6 us (1.044)
  local copies, waits for them, and re-layouts: 2.43 us -> 4.18 us
  Pallas kernels: 9.91 us -> 11.6 us
  starting transfers between devices: 55 us -> 53.9 us
    pallas_call x2 -> x3, Pallas kernels: 3.73 us -> 6.16 us  [stencil(): pl.pallas_call(functools.partial(stencil_kernel, groups=groups, rows=rows...]
    unnamed x8 -> x16, local copies, waits for them, and re-layouts: 2.43 us -> 4.18 us
    pallas_call x3, Pallas kernels: 5.3 us -> 4.2 us  [the longest x2 2.37 us: gather(): pl.pallas_call(functools.partial(gather_kernel, begin=begin, end=end, fir...]
    ppermute x31, starting transfers between devices: 55 us -> 53.9 us  [local(): arrived.append(lax.ppermute(messages[k], 'blk', pairs))]
  transfers between devices with their start and end apart: 31 -> 31, of which waited for: 5 -> 7; matrix products, arithmetic and copies ran while one was open for 0% -> 0% of each run, Pallas kernels for 8% -> 11%
where the time goes in v2:
time: 76.6 us; the launch traced here: 76.2 us
  starting transfers between devices  53.9 us (70%)
  Pallas kernels  11.6 us (15%)
  waiting for transfers between devices  6.36 us (8%)
  local copies, waits for them, and re-layouts  4.18 us (5%)
    ppermute x31, starting transfers between devices, local(): arrived.append(lax.ppermute(messages[k], 'blk', pairs))  53.9 us
    ppermute x31, waiting for transfers between devices, local(): arrived.append(lax.ppermute(messages[k], 'blk', pairs))  6.36 us
    pallas_call x3, Pallas kernels, stencil(): pl.pallas_call(functools.partial(stencil_kernel, groups=groups, rows=rows...  6.16 us
    unnamed x16, local copies, waits for them, and re-layouts  4.18 us
    pallas_call x2, Pallas kernels, gather(): pl.pallas_call(functools.partial(gather_kernel, begin=begin, end=end, fir...  2.37 us
    pallas_call x1, Pallas kernels, finish(): pl.pallas_call(functools.partial(finish_kernel, steps=STEPS), in_specs=[p...  1.83 us
  transfers between devices with their start and end apart: 31, of which 7 were waited for; matrix products, arithmetic and copies ran while one was open for 0% of the time, Pallas kernels for 11%

profile of v2, /device:TPU:0, one launch (start us, length us, event | category | flops | bytes accessed | tf_op | source)
XLA Modules:
  0.0 76.2 jit_solution(10418927947873146621)
XLA Ops:
  0.0 1.7 %copy-done = f32[4,128,1280]{2,1,0:T(8,128)S(1)} copy-done((f32[4,128,1280]{2,1,0:T(8,128)S(1)}, f32[4,128,1280]{2,1,0:T(8,128)}, u32[]{:S(2)}) %copy-start) | copy-done | bytes 2621464
  1.7 0.7 copy-done.2
  2.4 1.4 %stencil.5 = (f32[16,1280]{1,0:T(8,128)}, f32[16,1280]{1,0:T(8,128)S(1)}, f32[16,1280]{1,0:T(8,128)S(1)}, f32[16,1280]{1,0:T(8,128)S(1)}) custom-call(f32[3,3]{1,0:T(4,128)S(1)} %copy-done.2, f32[4,128,1280]{2,1,0:T(8,128)S(1)} %copy-done), custom_call_target="tpu_custom_call" | custom-call | flops 1474560 | bytes 655360 | tf_op jit(solution)/shard_map/stencil/pallas_call | solution.py:117
  3.9 5.1 %collective-permute-start.3 = (f32[16,1280]{1,0:T(8,128)}, f32[16,1280]{1,0:T(8,128)S(1)}, u32[]{:S(2)}, u32[]{:S(2)}) collective-permute-start(f32[16,1280]{1,0:T(8,128)} %get-tuple-element.47), channel_id=1, source_target_pairs={{0,18},{1,19},{2,16},{3,17},{4,22},{5,23},{6,20},{7,21},{8,26},{9,... | collective-permute-start | bytes 245768 | tf_op jit(solution)/shard_map/ppermute | solution.py:293
  8.9 0.0 collective-permute-start.5
  8.9 2.0 %collective-permute-start.6 = (f32[16,1280]{1,0:T(8,128)S(1)}, f32[16,1280]{1,0:T(8,128)S(1)}, u32[]{:S(2)}, u32[]{:S(2)}) collective-permute-start(f32[16,1280]{1,0:T(8,128)S(1)} %get-tuple-element.50), channel_id=1, source_target_pairs={{0,10},{1,11},{2,8},{3,9},{4,14},{5,15},{6,12},{7,13},{8,2},{9,3},... | collective-permute-start | bytes 245768 | tf_op jit(solution)/shard_map/ppermute | solution.py:293
  10.9 0.6 collective-permute-start.8
  11.5 2.3 %stencil.4 = (f32[16,1280]{1,0:T(8,128)}, f32[16,1280]{1,0:T(8,128)}, f32[16,1280]{1,0:T(8,128)}, f32[16,1280]{1,0:T(8,128)}) custom-call(f32[3,3]{1,0:T(4,128)} %kernel_ref.5, f32[4,128,1280]{2,1,0:T(8,128)} %frames_ref.5), custom_call_target="tpu_custom_call" | custom-call | flops 1474560 | bytes 655360 | tf_op jit(solution)/shard_map/stencil/pallas_call | solution.py:117
  13.8 2.8 %collective-permute-start = (f32[16,1280]{1,0:T(8,128)}, f32[16,1280]{1,0:T(8,128)S(1)}, u32[]{:S(2)}, u32[]{:S(2)}) collective-permute-start(f32[16,1280]{1,0:T(8,128)} %get-tuple-element.44), channel_id=1, source_target_pairs={{0,16},{1,17},{2,18},{3,19},{4,20},{5,21},{6,22},{7,23},{8,24},{9,... | collective-permute-start | bytes 245768 | tf_op jit(solution)/shard_map/ppermute | solution.py:293
  16.6 0.0 collective-permute-done.3.refs_4_
  16.6 0.0 collective-permute-start.1
  16.6 1.7 %copy-done.1 = f32[4,128,1280]{2,1,0:T(8,128)S(1)} copy-done((f32[4,128,1280]{2,1,0:T(8,128)S(1)}, f32[4,128,1280]{2,1,0:T(8,128)}, u32[]{:S(2)}) %copy-start.1) | copy-done | bytes 2621464
  18.4 2.4 %stencil.3 = (f32[16,1280]{1,0:T(8,128)S(1)}, f32[16,1280]{1,0:T(8,128)S(1)}, f32[16,1280]{1,0:T(8,128)S(1)}, f32[16,1280]{1,0:T(8,128)S(1)}, f32[16,1280]{1,0:T...) custom-call(f32[3,3]{1,0:T(4,128)S(1)} %copy-done.3, ...), custom_call_target="tpu_custom_call" | custom-call | flops 8847360 | bytes 3932160 | tf_op jit(solution)/shard_map/stencil/pallas_call | solution.py:117
  20.8 0.0 collective-permute-done.5.refs_6_
  20.8 2.1 %collective-permute-start.2 = (f32[16,1280]{1,0:T(8,128)S(1)}, f32[16,1280]{1,0:T(8,128)S(1)}, u32[]{:S(2)}, u32[]{:S(2)}) collective-permute-start(f32[16,1280]{1,0:T(8,128)S(1)} %copy-done.7), channel_id=1, source_target_pairs={{0,8},{1,9},{2,10},{3,11},{4,12},{5,13},{6,14},{7,15},{8,0},{9,1},... | collective-permute-start | bytes 245768 | tf_op jit(solution)/shard_map/ppermute | solution.py:293
  22.9 0.0 collective-permute-done.6.refs_7_
  22.9 0.7 collective-permute-start.4
  23.6 0.0 collective-permute-done.8.refs_9_
  23.6 2.6 %collective-permute-start.7 = (f32[16,1280]{1,0:T(8,128)S(1)}, f32[16,1280]{1,0:T(8,128)S(1)}, u32[]{:S(2)}, u32[]{:S(2)}) collective-permute-start(f32[16,1280]{1,0:T(8,128)S(1)} %get-tuple-element.51), channel_id=1, source_target_pairs={{0,20},{1,21},{2,22},{3,23},{4,16},{5,17},{6,18},{7,19},{8,28},{9,... | collective-permute-start | bytes 245768 | tf_op jit(solution)/shard_map/ppermute | solution.py:293
  26.2 0.0 collective-permute-done.refs_1_
  26.2 0.6 collective-permute-start.9
  26.8 0.0 collective-permute-done.1.refs_2_
  26.9 2.3 %collective-permute-start.10 = (f32[16,1280]{1,0:T(8,128)S(1)}, f32[16,1280]{1,0:T(8,128)S(1)}, u32[]{:S(2)}, u32[]{:S(2)}) collective-permute-start(f32[16,1280]{1,0:T(8,128)S(1)} %get-tuple-element.54), channel_id=1, source_target_pairs={{0,12},{1,13},{2,14},{3,15},{4,8},{5,9},{6,10},{7,11},{8,4},{9,5},... | collective-permute-start | bytes 245768 | tf_op jit(solution)/shard_map/ppermute | solution.py:293
  29.1 0.0 collective-permute-done.2.refs_3_
  29.1 2.5 %collective-permute-start.11 = (f32[16,1280]{1,0:T(8,128)S(1)}, f32[16,1280]{1,0:T(8,128)S(1)}, u32[]{:S(2)}, u32[]{:S(2)}) collective-permute-start(f32[16,1280]{1,0:T(8,128)S(1)} %get-tuple-element.55), channel_id=1, source_target_pairs={{0,22},{1,23},{2,20},{3,21},{4,18},{5,19},{6,16},{7,17},{8,30},{9,... | collective-permute-start | bytes 245768 | tf_op jit(solution)/shard_map/ppermute | solution.py:293
  31.6 1.4 %collective-permute-start.12 = (f32[16,1280]{1,0:T(8,128)S(1)}, f32[16,1280]{1,0:T(8,128)S(1)}, u32[]{:S(2)}, u32[]{:S(2)}) collective-permute-start(f32[16,1280]{1,0:T(8,128)S(1)} %get-tuple-element.56), channel_id=1, source_target_pairs={{0,13},{1,12},{2,15},{3,14},{4,9},{5,8},{6,11},{7,10},{8,5},{9,4},... | collective-permute-start | bytes 245768 | tf_op jit(solution)/shard_map/ppermute | solution.py:293
  33.1 1.8 %collective-permute-start.13 = (f32[16,1280]{1,0:T(8,128)S(1)}, f32[16,1280]{1,0:T(8,128)S(1)}, u32[]{:S(2)}, u32[]{:S(2)}) collective-permute-start(f32[16,1280]{1,0:T(8,128)S(1)} %get-tuple-element.57), channel_id=1, source_target_pairs={{0,23},{1,22},{2,21},{3,20},{4,19},{5,18},{6,17},{7,16},{8,31},{9,... | collective-permute-start | bytes 245768 | tf_op jit(solution)/shard_map/ppermute | solution.py:293
  34.8 0.8 %collective-permute-done.9.refs_10_ = f32[16,1280]{1,0:T(8,128)S(1)} collective-permute-done((f32[16,1280]{1,0:T(8,128)S(1)}, f32[16,1280]{1,0:T(8,128)S(1)}, u32[]{:S(2)}, u32[]{:S(2)}) %collective-permute-start.9) | collective-permute-done | bytes 81952 | tf_op jit(solution)/shard_map/ppermute | solution.py:293
  35.7 2.0 %collective-permute-start.14 = (f32[16,1280]{1,0:T(8,128)S(1)}, f32[16,1280]{1,0:T(8,128)S(1)}, u32[]{:S(2)}, u32[]{:S(2)}) collective-permute-start(f32[16,1280]{1,0:T(8,128)S(1)} %get-tuple-element.58), channel_id=1, source_target_pairs={{0,14},{1,15},{2,12},{3,13},{4,10},{5,11},{6,8},{7,9},{8,6},{9,7},... | collective-permute-start | bytes 245768 | tf_op jit(solution)/shard_map/ppermute | solution.py:293
  37.6 0.0 collective-permute-done.10.refs_11_
  37.6 1.5 %collective-permute-start.15 = (f32[16,1280]{1,0:T(8,128)S(1)}, f32[16,1280]{1,0:T(8,128)S(1)}, u32[]{:S(2)}, u32[]{:S(2)}) collective-permute-start(f32[16,1280]{1,0:T(8,128)S(1)} %get-tuple-element.59), channel_id=1, source_target_pairs={{0,24},{1,25},{2,26},{3,27},{4,28},{5,29},{6,30},{7,31},{8,16},{9,... | collective-permute-start | bytes 245768 | tf_op jit(solution)/shard_map/ppermute | solution.py:293
  39.2 0.9 %collective-permute-done.11.refs_12_ = f32[16,1280]{1,0:T(8,128)S(1)} collective-permute-done((f32[16,1280]{1,0:T(8,128)S(1)}, f32[16,1280]{1,0:T(8,128)S(1)}, u32[]{:S(2)}, u32[]{:S(2)}) %collective-permute-start.11) | collective-permute-done | bytes 81952 | tf_op jit(solution)/shard_map/ppermute | solution.py:293
  40.1 0.7 collective-permute-done.12.refs_13_
  40.8 1.4 %collective-permute-start.17 = (f32[16,1280]{1,0:T(8,128)S(1)}, f32[16,1280]{1,0:T(8,128)S(1)}, u32[]{:S(2)}, u32[]{:S(2)}) collective-permute-start(f32[16,1280]{1,0:T(8,128)S(1)} %get-tuple-element.61), channel_id=1, source_target_pairs={{0,25},{1,24},{2,27},{3,26},{4,29},{5,28},{6,31},{7,30},{8,17},{9,... | collective-permute-start | bytes 245768 | tf_op jit(solution)/shard_map/ppermute | solution.py:293
  42.1 1.6 %collective-permute-done.13.refs_14_ = f32[16,1280]{1,0:T(8,128)S(1)} collective-permute-done((f32[16,1280]{1,0:T(8,128)S(1)}, f32[16,1280]{1,0:T(8,128)S(1)}, u32[]{:S(2)}, u32[]{:S(2)}) %collective-permute-start.13) | collective-permute-done | bytes 81952 | tf_op jit(solution)/shard_map/ppermute | solution.py:293
  43.8 0.0 collective-permute-start.18
  43.8 0.0 collective-permute-done.14.refs_15_
  43.8 2.3 %collective-permute-start.19 = (f32[16,1280]{1,0:T(8,128)S(1)}, f32[16,1280]{1,0:T(8,128)S(1)}, u32[]{:S(2)}, u32[]{:S(2)}) collective-permute-start(f32[16,1280]{1,0:T(8,128)S(1)} %get-tuple-element.63), channel_id=1, source_target_pairs={{0,26},{1,27},{2,24},{3,25},{4,30},{5,31},{6,28},{7,29},{8,18},{9,... | collective-permute-start | bytes 245768 | tf_op jit(solution)/shard_map/ppermute | solution.py:293
  46.0 1.3 %collective-permute-start.20 = (f32[16,1280]{1,0:T(8,128)S(1)}, f32[16,1280]{1,0:T(8,128)S(1)}, u32[]{:S(2)}, u32[]{:S(2)}) collective-permute-start(f32[16,1280]{1,0:T(8,128)S(1)} %get-tuple-element.64), channel_id=1, source_target_pairs={{0,2},{1,3},{2,0},{3,1},{4,6},{5,7},{6,4},{7,5},{8,10},{9,11},{10,... | collective-permute-start | bytes 245768 | tf_op jit(solution)/shard_map/ppermute | solution.py:293
  47.4 0.8 %collective-permute-done.16.refs_2_ = f32[16,1280]{1,0:T(8,128)S(1)} collective-permute-done((f32[16,1280]{1,0:T(8,128)S(1)}, f32[16,1280]{1,0:T(8,128)S(1)}, u32[]{:S(2)}, u32[]{:S(2)}) %collective-permute-start.16) | collective-permute-done | bytes 81952 | tf_op jit(solution)/shard_map/ppermute | solution.py:293
  48.2 2.4 %collective-permute-start.21 = (f32[16,1280]{1,0:T(8,128)S(1)}, f32[16,1280]{1,0:T(8,128)S(1)}, u32[]{:S(2)}, u32[]{:S(2)}) collective-permute-start(f32[16,1280]{1,0:T(8,128)S(1)} %get-tuple-element.65), channel_id=1, source_target_pairs={{0,27},{1,26},{2,25},{3,24},{4,31},{5,30},{6,29},{7,28},{8,19},{9,... | collective-permute-start | bytes 245768 | tf_op jit(solution)/shard_map/ppermute | solution.py:293
  50.5 0.8 %collective-permute-start.22 = (f32[16,1280]{1,0:T(8,128)S(1)}, f32[16,1280]{1,0:T(8,128)S(1)}, u32[]{:S(2)}, u32[]{:S(2)}) collective-permute-start(f32[16,1280]{1,0:T(8,128)S(1)} %get-tuple-element.66), channel_id=1, source_target_pairs={{0,3},{1,2},{2,1},{3,0},{4,7},{5,6},{6,5},{7,4},{8,11},{9,10},{10,... | collective-permute-start | bytes 245768 | tf_op jit(solution)/shard_map/ppermute | solution.py:293
  51.3 0.0 collective-permute-done.18.refs_4_
  51.3 3.4 %collective-permute-start.23 = (f32[16,1280]{1,0:T(8,128)S(1)}, f32[16,1280]{1,0:T(8,128)S(1)}, u32[]{:S(2)}, u32[]{:S(2)}) collective-permute-start(f32[16,1280]{1,0:T(8,128)S(1)} %get-tuple-element.67), channel_id=1, source_target_pairs={{0,28},{1,29},{2,30},{3,31},{4,24},{5,25},{6,26},{7,27},{8,20},{9,... | collective-permute-start | bytes 245768 | tf_op jit(solution)/shard_map/ppermute | solution.py:293
  54.7 0.0 collective-permute-done.19.refs_5_
  54.7 1.7 %collective-permute-start.24 = (f32[16,1280]{1,0:T(8,128)S(1)}, f32[16,1280]{1,0:T(8,128)S(1)}, u32[]{:S(2)}, u32[]{:S(2)}) collective-permute-start(f32[16,1280]{1,0:T(8,128)S(1)} %get-tuple-element.68), channel_id=1, source_target_pairs={{0,4},{1,5},{2,6},{3,7},{4,0},{5,1},{6,2},{7,3},{8,12},{9,13},{10,... | collective-permute-start | bytes 245768 | tf_op jit(solution)/shard_map/ppermute | solution.py:293
  56.4 3.1 %collective-permute-start.25 = (f32[16,1280]{1,0:T(8,128)S(1)}, f32[16,1280]{1,0:T(8,128)S(1)}, u32[]{:S(2)}, u32[]{:S(2)}) collective-permute-start(f32[16,1280]{1,0:T(8,128)S(1)} %get-tuple-element.69), channel_id=1, source_target_pairs={{0,29},{1,28},{2,31},{3,30},{4,25},{5,24},{6,27},{7,26},{8,21},{9,... | collective-permute-start | bytes 245768 | tf_op jit(solution)/shard_map/ppermute | solution.py:293
  59.5 1.2 %weights.1 = (bf16[512,512]{1,0:T(8,128)(2,1)S(1)}, bf16[512,512]{1,0:T(8,128)(2,1)S(1)}, bf16[512,192]{1,0:T(8,128)(2,1)S(1)}) custom-call(f32[1,128]{1,0:T(1,128)S(1)} %bitcast.1, s32[1,128]{1,0:T(1,128)S(1)} %copy-done.5), custom_call_target="tpu_custom_call" | custom-call | flops 268435456 | bytes 1048576 | tf_op jit(solution)/shard_map/weights/pallas_call | solution.py:183
  60.8 1.4 %collective-permute-start.26 = (f32[16,1280]{1,0:T(8,128)S(1)}, f32[16,1280]{1,0:T(8,128)S(1)}, u32[]{:S(2)}, u32[]{:S(2)}) collective-permute-start(f32[16,1280]{1,0:T(8,128)S(1)} %get-tuple-element.70), channel_id=1, source_target_pairs={{0,5},{1,4},{2,7},{3,6},{4,1},{5,0},{6,3},{7,2},{8,13},{9,12},{10,... | collective-permute-start | bytes 245768 | tf_op jit(solution)/shard_map/ppermute | solution.py:293
  62.2 0.0 collective-permute-done.22.refs_8_
  62.2 0.7 collective-permute-start.27
  62.9 0.0 collective-permute-done.23.refs_9_
  62.9 2.2 %collective-permute-start.28 = (f32[16,1280]{1,0:T(8,128)S(1)}, f32[16,1280]{1,0:T(8,128)S(1)}, u32[]{:S(2)}, u32[]{:S(2)}) collective-permute-start(f32[16,1280]{1,0:T(8,128)S(1)} %get-tuple-element.72), channel_id=1, source_target_pairs={{0,6},{1,7},{2,4},{3,5},{4,2},{5,3},{6,0},{7,1},{8,14},{9,15},{10,... | collective-permute-start | bytes 245768 | tf_op jit(solution)/shard_map/ppermute | solution.py:293
  65.1 0.0 collective-permute-done.24.refs_10_
  65.1 3.0 %collective-permute-start.29 = (f32[16,1280]{1,0:T(8,128)S(1)}, f32[16,1280]{1,0:T(8,128)S(1)}, u32[]{:S(2)}, u32[]{:S(2)}) collective-permute-start(f32[16,1280]{1,0:T(8,128)S(1)} %get-tuple-element.73), channel_id=1, source_target_pairs={{0,31},{1,30},{2,29},{3,28},{4,27},{5,26},{6,25},{7,24},{8,23},{9,... | collective-permute-start | bytes 245768 | tf_op jit(solution)/shard_map/ppermute | solution.py:293
  68.2 2.3 %collective-permute-start.30 = (f32[16,1280]{1,0:T(8,128)S(1)}, f32[16,1280]{1,0:T(8,128)S(1)}, u32[]{:S(2)}, u32[]{:S(2)}) collective-permute-start(f32[16,1280]{1,0:T(8,128)S(1)} %get-tuple-element.74), channel_id=1, source_target_pairs={{0,7},{1,6},{2,5},{3,4},{4,3},{5,2},{6,1},{7,0},{8,15},{9,14},{10,... | collective-permute-start | bytes 245768 | tf_op jit(solution)/shard_map/ppermute | solution.py:293
  70.5 1.2 %temporal.2.refs_0_ = f32[512,1280]{1,0:T(8,128)S(1)} custom-call(bf16[512,512]{1,0:T(8,128)(2,1)S(1)} %get-tuple-element.41.high_ref, bf16[512,512]{1,0:T(8,128)(2,1)S(1)} %get-tuple-element.42.low_ref, f32[16,1280]{1,0:T(8,128)S(1)} %get-tuple-element.43.refs_0_, f32[16,1280]{1,0:T(8,128)S(1)} %collective-permute-done.refs_1_, ...), custom_call_target="tpu_custom_call" | custom-call | flops 1006632960 | bytes 5242880 | tf_op jit(solution)/shard_map/temporal/pallas_call | solution.py:217
  71.7 0.0 collective-permute-done.26.refs_12_
  71.7 1.2 %temporal.3.so_far = f32[512,1280]{1,0:T(8,128)S(1)} custom-call(bf16[512,512]{1,0:T(8,128)(2,1)S(1)} %get-tuple-element.41.high_ref, bf16[512,512]{1,0:T(8,128)(2,1)S(1)} %get-tuple-element.42.low_ref, f32[512,1280]{1,0:T(8,128)S(1)} %temporal.2.refs_0_, f32[16,1280]{1,0:T(8,128)S(1)} %collective-permute-done.15.refs_1_, ...), custom_call_target="tpu_custom_call" | custom-call | flops 754974720 | bytes 5242880 | tf_op jit(solution)/shard_map/temporal/pallas_call | solution.py:217
  72.9 0.0 collective-permute-done.27.refs_0_
  72.9 0.0 collective-permute-done.28.refs_1_
  72.9 0.7 collective-permute-done.29.refs_2_
  73.6 0.8 %collective-permute-done.30.refs_3_ = f32[16,1280]{1,0:T(8,128)S(1)} collective-permute-done((f32[16,1280]{1,0:T(8,128)S(1)}, f32[16,1280]{1,0:T(8,128)S(1)}, u32[]{:S(2)}, u32[]{:S(2)}) %collective-permute-start.30) | collective-permute-done | bytes 81952 | tf_op jit(solution)/shard_map/ppermute | solution.py:293
  74.3 1.8 %finish.1 = f32[128,4,1280]{2,1,0:T(4,128)} custom-call(bf16[512,192]{1,0:T(8,128)(2,1)S(1)} %get-tuple-element.40.weights_ref, f32[512,1280]{1,0:T(8,128)S(1)} %temporal.3.so_far, f32[16,1280]{1,0:T(8,128)S(1)} %collective-permute-done.27.refs_0_, f32[16,1280]{1,0:T(8,128)S(1)} %collective-permute-done.28.refs_1_, ...), custom_call_target="tpu_custom_call" | custom-call | flops 251658240 | bytes 5242880 | tf_op jit(solution)/shard_map/finish/pallas_call | solution.py:256
  (21 shorter events, 0.0 us)
Async XLA Ops:
  0.0 1.7 %copy-start = (f32[4,128,1280]{2,1,0:T(8,128)S(1)}, f32[4,128,1280]{2,1,0:T(8,128)}, u32[]{:S(2)}) copy-start(f32[4,128,1280]{2,1,0:T(8,128)} %frames_ref.5) | copy-start | bytes 7864324
  1.7 0.7 copy-start.2
  2.4 14.2 %copy-start.3 = (f32[3,3]{1,0:T(4,128)S(1)}, f32[3,3]{1,0:T(4,128)}, u32[]{:S(2)}) copy-start(f32[3,3]{1,0:T(4,128)} %kernel_ref.5) | copy-start | bytes 112
  3.9 12.7 %collective-permute-start.3 = (f32[16,1280]{1,0:T(8,128)}, f32[16,1280]{1,0:T(8,128)S(1)}, u32[]{:S(2)}, u32[]{:S(2)}) collective-permute-start(f32[16,1280]{1,0:T(8,128)} %get-tuple-element.47), channel_id=1, source_target_pairs={{0,18},{1,19},{2,16},{3,17},{4,22},{5,23},{6,20},{7,21},{8,26},{9,... | collective-permute-start | bytes 245768 | tf_op jit(solution)/shard_map/ppermute | solution.py:293
  8.9 11.9 %collective-permute-start.5 = (f32[16,1280]{1,0:T(8,128)S(1)}, f32[16,1280]{1,0:T(8,128)S(1)}, u32[]{:S(2)}, u32[]{:S(2)}) collective-permute-start(f32[16,1280]{1,0:T(8,128)S(1)} %get-tuple-element.49), channel_id=1, source_target_pairs={{0,19},{1,18},{2,17},{3,16},{4,23},{5,22},{6,21},{7,20},{8,27},{9,... | collective-permute-start | bytes 245768 | tf_op jit(solution)/shard_map/ppermute | solution.py:293
  8.9 14.0 %collective-permute-start.6 = (f32[16,1280]{1,0:T(8,128)S(1)}, f32[16,1280]{1,0:T(8,128)S(1)}, u32[]{:S(2)}, u32[]{:S(2)}) collective-permute-start(f32[16,1280]{1,0:T(8,128)S(1)} %get-tuple-element.50), channel_id=1, source_target_pairs={{0,10},{1,11},{2,8},{3,9},{4,14},{5,15},{6,12},{7,13},{8,2},{9,3},... | collective-permute-start | bytes 245768 | tf_op jit(solution)/shard_map/ppermute | solution.py:293
  10.9 48.6 %copy-start.4 = (f32[128]{0:T(128)S(1)}, f32[128]{0:T(128)}, u32[]{:S(2)}) copy-start(f32[128]{0:T(128)} %param.5) | copy-start | bytes 1540
  10.9 48.6 %copy-start.5 = (s32[1,128]{1,0:T(1,128)S(1)}, s32[1,128]{1,0:T(1,128)}, u32[]{:S(2)}) copy-start(s32[1,128]{1,0:T(1,128)} %constant.2.clone.partner_ref) | copy-start | bytes 1540
  10.9 12.7 %collective-permute-start.8 = (f32[16,1280]{1,0:T(8,128)S(1)}, f32[16,1280]{1,0:T(8,128)S(1)}, u32[]{:S(2)}, u32[]{:S(2)}) collective-permute-start(f32[16,1280]{1,0:T(8,128)S(1)} %get-tuple-element.52), channel_id=1, source_target_pairs={{0,11},{1,10},{2,9},{3,8},{4,15},{5,14},{6,13},{7,12},{8,3},{9,2},... | collective-permute-start | bytes 245768 | tf_op jit(solution)/shard_map/ppermute | solution.py:293
  13.8 12.4 %collective-permute-start = (f32[16,1280]{1,0:T(8,128)}, f32[16,1280]{1,0:T(8,128)S(1)}, u32[]{:S(2)}, u32[]{:S(2)}) collective-permute-start(f32[16,1280]{1,0:T(8,128)} %get-tuple-element.44), channel_id=1, source_target_pairs={{0,16},{1,17},{2,18},{3,19},{4,20},{5,21},{6,22},{7,23},{8,24},{9,... | collective-permute-start | bytes 245768 | tf_op jit(solution)/shard_map/ppermute | solution.py:293
  16.6 10.3 %collective-permute-start.1 = (f32[16,1280]{1,0:T(8,128)}, f32[16,1280]{1,0:T(8,128)S(1)}, u32[]{:S(2)}, u32[]{:S(2)}) collective-permute-start(f32[16,1280]{1,0:T(8,128)} %get-tuple-element.45), channel_id=1, source_target_pairs={{0,17},{1,16},{2,19},{3,18},{4,21},{5,20},{6,23},{7,22},{8,25},{9,... | collective-permute-start | bytes 245768 | tf_op jit(solution)/shard_map/ppermute | solution.py:293
  16.6 1.7 %copy-start.1 = (f32[4,128,1280]{2,1,0:T(8,128)S(1)}, f32[4,128,1280]{2,1,0:T(8,128)}, u32[]{:S(2)}) copy-start(f32[4,128,1280]{2,1,0:T(8,128)} %frames_ref.5) | copy-start | bytes 7864324
  18.4 2.4 %copy-start.7 = (f32[16,1280]{1,0:T(8,128)S(1)}, f32[16,1280]{1,0:T(8,128)}, u32[]{:S(2)}) copy-start(f32[16,1280]{1,0:T(8,128)} %get-tuple-element.46) | copy-start | bytes 245764
  18.4 4.5 %copy-start.6 = (f32[16,1280]{1,0:T(8,128)S(1)}, f32[16,1280]{1,0:T(8,128)}, u32[]{:S(2)}) copy-start(f32[16,1280]{1,0:T(8,128)} %get-tuple-element.48) | copy-start | bytes 245764
  20.8 8.3 %collective-permute-start.2 = (f32[16,1280]{1,0:T(8,128)S(1)}, f32[16,1280]{1,0:T(8,128)S(1)}, u32[]{:S(2)}, u32[]{:S(2)}) collective-permute-start(f32[16,1280]{1,0:T(8,128)S(1)} %copy-done.7), channel_id=1, source_target_pairs={{0,8},{1,9},{2,10},{3,11},{4,12},{5,13},{6,14},{7,15},{8,0},{9,1},... | collective-permute-start | bytes 245768 | tf_op jit(solution)/shard_map/ppermute | solution.py:293
  22.9 8.8 %collective-permute-start.4 = (f32[16,1280]{1,0:T(8,128)S(1)}, f32[16,1280]{1,0:T(8,128)S(1)}, u32[]{:S(2)}, u32[]{:S(2)}) collective-permute-start(f32[16,1280]{1,0:T(8,128)S(1)} %copy-done.6), channel_id=1, source_target_pairs={{0,9},{1,8},{2,11},{3,10},{4,13},{5,12},{6,15},{7,14},{8,1},{9,0},... | collective-permute-start | bytes 245768 | tf_op jit(solution)/shard_map/ppermute | solution.py:293
  23.6 9.5 %collective-permute-start.7 = (f32[16,1280]{1,0:T(8,128)S(1)}, f32[16,1280]{1,0:T(8,128)S(1)}, u32[]{:S(2)}, u32[]{:S(2)}) collective-permute-start(f32[16,1280]{1,0:T(8,128)S(1)} %get-tuple-element.51), channel_id=1, source_target_pairs={{0,20},{1,21},{2,22},{3,23},{4,16},{5,17},{6,18},{7,19},{8,28},{9,... | collective-permute-start | bytes 245768 | tf_op jit(solution)/shard_map/ppermute | solution.py:293
  26.2 9.5 %collective-permute-start.9 = (f32[16,1280]{1,0:T(8,128)S(1)}, f32[16,1280]{1,0:T(8,128)S(1)}, u32[]{:S(2)}, u32[]{:S(2)}) collective-permute-start(f32[16,1280]{1,0:T(8,128)S(1)} %get-tuple-element.53), channel_id=1, source_target_pairs={{0,21},{1,20},{2,23},{3,22},{4,17},{5,16},{6,19},{7,18},{8,29},{9,... | collective-permute-start | bytes 245768 | tf_op jit(solution)/shard_map/ppermute | solution.py:293
  26.9 10.8 %collective-permute-start.10 = (f32[16,1280]{1,0:T(8,128)S(1)}, f32[16,1280]{1,0:T(8,128)S(1)}, u32[]{:S(2)}, u32[]{:S(2)}) collective-permute-start(f32[16,1280]{1,0:T(8,128)S(1)} %get-tuple-element.54), channel_id=1, source_target_pairs={{0,12},{1,13},{2,14},{3,15},{4,8},{5,9},{6,10},{7,11},{8,4},{9,5},... | collective-permute-start | bytes 245768 | tf_op jit(solution)/shard_map/ppermute | solution.py:293
  29.1 11.0 %collective-permute-start.11 = (f32[16,1280]{1,0:T(8,128)S(1)}, f32[16,1280]{1,0:T(8,128)S(1)}, u32[]{:S(2)}, u32[]{:S(2)}) collective-permute-start(f32[16,1280]{1,0:T(8,128)S(1)} %get-tuple-element.55), channel_id=1, source_target_pairs={{0,22},{1,23},{2,20},{3,21},{4,18},{5,19},{6,16},{7,17},{8,30},{9,... | collective-permute-start | bytes 245768 | tf_op jit(solution)/shard_map/ppermute | solution.py:293
  31.6 9.1 %collective-permute-start.12 = (f32[16,1280]{1,0:T(8,128)S(1)}, f32[16,1280]{1,0:T(8,128)S(1)}, u32[]{:S(2)}, u32[]{:S(2)}) collective-permute-start(f32[16,1280]{1,0:T(8,128)S(1)} %get-tuple-element.56), channel_id=1, source_target_pairs={{0,13},{1,12},{2,15},{3,14},{4,9},{5,8},{6,11},{7,10},{8,5},{9,4},... | collective-permute-start | bytes 245768 | tf_op jit(solution)/shard_map/ppermute | solution.py:293
  33.1 10.7 %collective-permute-start.13 = (f32[16,1280]{1,0:T(8,128)S(1)}, f32[16,1280]{1,0:T(8,128)S(1)}, u32[]{:S(2)}, u32[]{:S(2)}) collective-permute-start(f32[16,1280]{1,0:T(8,128)S(1)} %get-tuple-element.57), channel_id=1, source_target_pairs={{0,23},{1,22},{2,21},{3,20},{4,19},{5,18},{6,17},{7,16},{8,31},{9,... | collective-permute-start | bytes 245768 | tf_op jit(solution)/shard_map/ppermute | solution.py:293
  35.7 8.1 %collective-permute-start.14 = (f32[16,1280]{1,0:T(8,128)S(1)}, f32[16,1280]{1,0:T(8,128)S(1)}, u32[]{:S(2)}, u32[]{:S(2)}) collective-permute-start(f32[16,1280]{1,0:T(8,128)S(1)} %get-tuple-element.58), channel_id=1, source_target_pairs={{0,14},{1,15},{2,12},{3,13},{4,10},{5,11},{6,8},{7,9},{8,6},{9,7},... | collective-permute-start | bytes 245768 | tf_op jit(solution)/shard_map/ppermute | solution.py:293
  37.6 8.4 %collective-permute-start.15 = (f32[16,1280]{1,0:T(8,128)S(1)}, f32[16,1280]{1,0:T(8,128)S(1)}, u32[]{:S(2)}, u32[]{:S(2)}) collective-permute-start(f32[16,1280]{1,0:T(8,128)S(1)} %get-tuple-element.59), channel_id=1, source_target_pairs={{0,24},{1,25},{2,26},{3,27},{4,28},{5,29},{6,30},{7,31},{8,16},{9,... | collective-permute-start | bytes 245768 | tf_op jit(solution)/shard_map/ppermute | solution.py:293
  40.1 8.1 %collective-permute-start.16 = (f32[16,1280]{1,0:T(8,128)S(1)}, f32[16,1280]{1,0:T(8,128)S(1)}, u32[]{:S(2)}, u32[]{:S(2)}) collective-permute-start(f32[16,1280]{1,0:T(8,128)S(1)} %get-tuple-element.60), channel_id=1, source_target_pairs={{0,15},{1,14},{2,13},{3,12},{4,11},{5,10},{6,9},{7,8},{8,7},{9,6},... | collective-permute-start | bytes 245768 | tf_op jit(solution)/shard_map/ppermute | solution.py:293
  40.8 9.8 %collective-permute-start.17 = (f32[16,1280]{1,0:T(8,128)S(1)}, f32[16,1280]{1,0:T(8,128)S(1)}, u32[]{:S(2)}, u32[]{:S(2)}) collective-permute-start(f32[16,1280]{1,0:T(8,128)S(1)} %get-tuple-element.61), channel_id=1, source_target_pairs={{0,25},{1,24},{2,27},{3,26},{4,29},{5,28},{6,31},{7,30},{8,17},{9,... | collective-permute-start | bytes 245768 | tf_op jit(solution)/shard_map/ppermute | solution.py:293
  43.8 7.5 %collective-permute-start.18 = (f32[16,1280]{1,0:T(8,128)S(1)}, f32[16,1280]{1,0:T(8,128)S(1)}, u32[]{:S(2)}, u32[]{:S(2)}) collective-permute-start(f32[16,1280]{1,0:T(8,128)S(1)} %get-tuple-element.62), channel_id=1, source_target_pairs={{0,1},{1,0},{2,3},{3,2},{4,5},{5,4},{6,7},{7,6},{8,9},{9,8},{10,11... | collective-permute-start | bytes 245768 | tf_op jit(solution)/shard_map/ppermute | solution.py:293
  43.8 10.9 %collective-permute-start.19 = (f32[16,1280]{1,0:T(8,128)S(1)}, f32[16,1280]{1,0:T(8,128)S(1)}, u32[]{:S(2)}, u32[]{:S(2)}) collective-permute-start(f32[16,1280]{1,0:T(8,128)S(1)} %get-tuple-element.63), channel_id=1, source_target_pairs={{0,26},{1,27},{2,24},{3,25},{4,30},{5,31},{6,28},{7,29},{8,18},{9,... | collective-permute-start | bytes 245768 | tf_op jit(solution)/shard_map/ppermute | solution.py:293
  46.0 10.4 %collective-permute-start.20 = (f32[16,1280]{1,0:T(8,128)S(1)}, f32[16,1280]{1,0:T(8,128)S(1)}, u32[]{:S(2)}, u32[]{:S(2)}) collective-permute-start(f32[16,1280]{1,0:T(8,128)S(1)} %get-tuple-element.64), channel_id=1, source_target_pairs={{0,2},{1,3},{2,0},{3,1},{4,6},{5,7},{6,4},{7,5},{8,10},{9,11},{10,... | collective-permute-start | bytes 245768 | tf_op jit(solution)/shard_map/ppermute | solution.py:293
  48.2 12.6 %collective-permute-start.21 = (f32[16,1280]{1,0:T(8,128)S(1)}, f32[16,1280]{1,0:T(8,128)S(1)}, u32[]{:S(2)}, u32[]{:S(2)}) collective-permute-start(f32[16,1280]{1,0:T(8,128)S(1)} %get-tuple-element.65), channel_id=1, source_target_pairs={{0,27},{1,26},{2,25},{3,24},{4,31},{5,30},{6,29},{7,28},{8,19},{9,... | collective-permute-start | bytes 245768 | tf_op jit(solution)/shard_map/ppermute | solution.py:293
  50.5 11.7 %collective-permute-start.22 = (f32[16,1280]{1,0:T(8,128)S(1)}, f32[16,1280]{1,0:T(8,128)S(1)}, u32[]{:S(2)}, u32[]{:S(2)}) collective-permute-start(f32[16,1280]{1,0:T(8,128)S(1)} %get-tuple-element.66), channel_id=1, source_target_pairs={{0,3},{1,2},{2,1},{3,0},{4,7},{5,6},{6,5},{7,4},{8,11},{9,10},{10,... | collective-permute-start | bytes 245768 | tf_op jit(solution)/shard_map/ppermute | solution.py:293
  51.3 11.6 %collective-permute-start.23 = (f32[16,1280]{1,0:T(8,128)S(1)}, f32[16,1280]{1,0:T(8,128)S(1)}, u32[]{:S(2)}, u32[]{:S(2)}) collective-permute-start(f32[16,1280]{1,0:T(8,128)S(1)} %get-tuple-element.67), channel_id=1, source_target_pairs={{0,28},{1,29},{2,30},{3,31},{4,24},{5,25},{6,26},{7,27},{8,20},{9,... | collective-permute-start | bytes 245768 | tf_op jit(solution)/shard_map/ppermute | solution.py:293
  54.7 10.4 %collective-permute-start.24 = (f32[16,1280]{1,0:T(8,128)S(1)}, f32[16,1280]{1,0:T(8,128)S(1)}, u32[]{:S(2)}, u32[]{:S(2)}) collective-permute-start(f32[16,1280]{1,0:T(8,128)S(1)} %get-tuple-element.68), channel_id=1, source_target_pairs={{0,4},{1,5},{2,6},{3,7},{4,0},{5,1},{6,2},{7,3},{8,12},{9,13},{10,... | collective-permute-start | bytes 245768 | tf_op jit(solution)/shard_map/ppermute | solution.py:293
  56.4 11.7 %collective-permute-start.25 = (f32[16,1280]{1,0:T(8,128)S(1)}, f32[16,1280]{1,0:T(8,128)S(1)}, u32[]{:S(2)}, u32[]{:S(2)}) collective-permute-start(f32[16,1280]{1,0:T(8,128)S(1)} %get-tuple-element.69), channel_id=1, source_target_pairs={{0,29},{1,28},{2,31},{3,30},{4,25},{5,24},{6,27},{7,26},{8,21},{9,... | collective-permute-start | bytes 245768 | tf_op jit(solution)/shard_map/ppermute | solution.py:293
  60.8 10.9 %collective-permute-start.26 = (f32[16,1280]{1,0:T(8,128)S(1)}, f32[16,1280]{1,0:T(8,128)S(1)}, u32[]{:S(2)}, u32[]{:S(2)}) collective-permute-start(f32[16,1280]{1,0:T(8,128)S(1)} %get-tuple-element.70), channel_id=1, source_target_pairs={{0,5},{1,4},{2,7},{3,6},{4,1},{5,0},{6,3},{7,2},{8,13},{9,12},{10,... | collective-permute-start | bytes 245768 | tf_op jit(solution)/shard_map/ppermute | solution.py:293
  62.2 10.7 %collective-permute-start.27 = (f32[16,1280]{1,0:T(8,128)S(1)}, f32[16,1280]{1,0:T(8,128)S(1)}, u32[]{:S(2)}, u32[]{:S(2)}) collective-permute-start(f32[16,1280]{1,0:T(8,128)S(1)} %get-tuple-element.71), channel_id=1, source_target_pairs={{0,30},{1,31},{2,28},{3,29},{4,26},{5,27},{6,24},{7,25},{8,22},{9,... | collective-permute-start | bytes 245768 | tf_op jit(solution)/shard_map/ppermute | solution.py:293
  62.9 10.0 %collective-permute-start.28 = (f32[16,1280]{1,0:T(8,128)S(1)}, f32[16,1280]{1,0:T(8,128)S(1)}, u32[]{:S(2)}, u32[]{:S(2)}) collective-permute-start(f32[16,1280]{1,0:T(8,128)S(1)} %get-tuple-element.72), channel_id=1, source_target_pairs={{0,6},{1,7},{2,4},{3,5},{4,2},{5,3},{6,0},{7,1},{8,14},{9,15},{10,... | collective-permute-start | bytes 245768 | tf_op jit(solution)/shard_map/ppermute | solution.py:293
  65.1 8.4 %collective-permute-start.29 = (f32[16,1280]{1,0:T(8,128)S(1)}, f32[16,1280]{1,0:T(8,128)S(1)}, u32[]{:S(2)}, u32[]{:S(2)}) collective-permute-start(f32[16,1280]{1,0:T(8,128)S(1)} %get-tuple-element.73), channel_id=1, source_target_pairs={{0,31},{1,30},{2,29},{3,28},{4,27},{5,26},{6,25},{7,24},{8,23},{9,... | collective-permute-start | bytes 245768 | tf_op jit(solution)/shard_map/ppermute | solution.py:293
  68.2 6.2 %collective-permute-start.30 = (f32[16,1280]{1,0:T(8,128)S(1)}, f32[16,1280]{1,0:T(8,128)S(1)}, u32[]{:S(2)}, u32[]{:S(2)}) collective-permute-start(f32[16,1280]{1,0:T(8,128)S(1)} %get-tuple-element.74), channel_id=1, source_target_pairs={{0,7},{1,6},{2,5},{3,4},{4,3},{5,2},{6,1},{7,0},{8,15},{9,14},{10,... | collective-permute-start | bytes 245768 | tf_op jit(solution)/shard_map/ppermute | solution.py:293

commit v3 on v2

v3 whole, which is shorter than its diff:
```python
import functools

import jax
import jax.numpy as jnp
from jax import lax
from jax.experimental import pallas as pl
from jax.experimental.pallas import tpu as pltpu
from jax.sharding import PartitionSpec as P


BAND = 24
SUBLANES = 8
VMEM = pltpu.VMEM
SMEM = pltpu.SMEM
KERNEL_BYTES = 20 << 20
WIDTH = 256
STAGES = (1,)
AHEAD = 4


def message_order(devices):
    half = devices // 2
    across = [half ^ low for low in range(half)]
    within = list(range(half // 2, half)) + list(range(1, half // 2))
    order, rest = across[:AHEAD], across[AHEAD:]
    done = 0
    for at, k in enumerate(rest):
        upto = -(-(at + 1) * len(within) // len(rest))
        order += within[done:upto] + [k]
        done = upto
    return order


def filter_tile(me, tap, above, here, below, tile, tiles, rows):
    row = lax.broadcasted_iota(jnp.int32, here.shape, 0)
    column = lax.broadcasted_iota(jnp.int32, here.shape, 1)
    columns = here.shape[1]
    above = jnp.where(tile > 0, above, 0.0)
    below = jnp.where(tile < tiles - 1, below, 0.0)
    over = pltpu.roll(jnp.where(row == SUBLANES - 1, above, here), 1, 0)
    under = pltpu.roll(jnp.where(row == 0, below, here), SUBLANES - 1, 0)
    left, center, right = (
        tap[0][b] * over + tap[1][b] * here + tap[2][b] * under for b in range(3)
    )
    left = jnp.where(column == 0, 0.0, pltpu.roll(left, 1, 1))
    right = jnp.where(column == columns - 1, 0.0, pltpu.roll(right, columns - 1, 1))
    value = left + center + right
    step = rows
    while step < SUBLANES:
        swapped = jnp.where(
            (row & step) == 0,
            pltpu.roll(value, SUBLANES - step, 0),
            pltpu.roll(value, step, 0),
        )
        value = jnp.where((me * rows) & step == 0, value, swapped)
        step *= 2
    return value


def tile_rows(tile, tiles):
    spots = (jnp.maximum(tile - 1, 0), tile, jnp.minimum(tile + 1, tiles - 1))
    return [pl.ds(pl.multiple_of(spot * SUBLANES, SUBLANES), SUBLANES) for spot in spots]


def stencil_kernel(kernel_ref, frames_ref, *refs, groups, rows, direct):
    count, height, _ = frames_ref.shape
    strips = SUBLANES // rows
    tiles = height // SUBLANES
    me = lax.axis_index("blk")
    chosen = [(me // strips) ^ group for group in groups]
    spans = [tile_rows(tile, tiles) for tile in chosen]
    tap_ref, tap_sem, *near = refs[len(groups) * strips :]
    tap_copy = pltpu.make_async_copy(kernel_ref, tap_ref, tap_sem)
    tap_copy.start()
    copies = []
    if direct:
        near_ref, near_sem = near
        for place, parts in enumerate(spans):
            for part, span in enumerate(parts):
                copies.append(
                    pltpu.make_async_copy(
                        frames_ref.at[:, span, :],
                        near_ref.at[place, part],
                        near_sem.at[place, part],
                    )
                )
                copies[-1].start()
    tap_copy.wait()
    tap = [[tap_ref[a, b] for b in range(3)] for a in range(3)]
    for place, tile in enumerate(chosen):
        for copy in copies[3 * place : 3 * place + 3]:
            copy.wait()
        for frame in range(count):
            if direct:
                parts = [near_ref[place, part, frame] for part in range(3)]
            else:
                parts = [frames_ref[frame, span, :] for span in spans[place]]
            value = filter_tile(me, tap, *parts, tile, tiles, rows)
            for strip in range(strips):
                refs[place * strips + strip][frame * rows : (frame + 1) * rows, :] = value[
                    strip * rows : (strip + 1) * rows, :
                ]


def far(array):
    return pltpu.with_memory_space_constraint(array, pltpu.HBM)


def stencil(kernel, frames, groups, rows, direct):
    count, _, columns = frames.shape
    outs = len(groups) * (SUBLANES // rows)
    total = 4 * outs * count * rows * columns
    scratch = [SMEM(kernel.shape, jnp.float32), pltpu.SemaphoreType.DMA]
    if direct:
        near = (len(groups), 3, count, SUBLANES, columns)
        scratch += [VMEM(near, jnp.float32), pltpu.SemaphoreType.DMA(near[:2])]
    return pl.pallas_call(
        functools.partial(stencil_kernel, groups=groups, rows=rows, direct=direct),
        in_specs=[
            pl.BlockSpec(memory_space=pltpu.HBM),
            pl.BlockSpec(memory_space=pltpu.HBM if direct else VMEM),
        ],
        out_specs=[pl.BlockSpec(memory_space=VMEM)] * outs,
        out_shape=[jax.ShapeDtypeStruct((count * rows, columns), jnp.float32)] * outs,
        scratch_shapes=scratch,
        cost_estimate=pl.CostEstimate(
            flops=5 * total, bytes_accessed=2 * total, transcendentals=0
        ),
        compiler_params=pltpu.CompilerParams(vmem_limit_bytes=KERNEL_BYTES),
        name="stencil",
    )(far(kernel), far(frames) if direct else frames)


def weights_kernel(
    widths_ref, partner_ref, high_ref, low_ref, last_ref, *, count, rows
):
    length = widths_ref.shape[1]
    size = length * rows
    tail = last_ref.shape[1] // 3
    square = (length, length)

    def iota(shape, axis):
        return lax.broadcasted_iota(jnp.int32, shape, axis)

    frame = lax.rem(iota(square, 1), count)
    source = count * (lax.axis_index("blk") ^ partner_ref[...]) + frame
    spread = jnp.broadcast_to(widths_ref[...], square).T
    offset = (iota(square, 0) - source).astype(jnp.float32)
    values = jnp.where(
        jnp.abs(offset) <= BAND, jnp.exp(-offset * offset / (2.0 * spread * spread)), 0.0
    )
    matrix = values / jnp.sum(values, axis=1, keepdims=True)
    high = matrix.astype(jnp.bfloat16)
    low = (matrix - high.astype(jnp.float32)).astype(jnp.bfloat16)

    tall, wide, full = (size, length), (length, size), (size, size)
    down = (iota(tall, 0) // rows == iota(tall, 1)).astype(jnp.bfloat16)
    along = (iota(wide, 0) == iota(wide, 1) // rows).astype(jnp.bfloat16)
    same = lax.rem(iota(full, 0), rows) == lax.rem(iota(full, 1), rows)
    dot = functools.partial(jnp.dot, preferred_element_type=jnp.float32)
    for piece, out_ref in ((high, high_ref), (low, low_ref)):
        wider = dot(down, dot(piece, along).astype(jnp.bfloat16))
        out_ref[...] = jnp.where(same, wider, 0.0).astype(jnp.bfloat16)

    wide, full = (length, 3 * tail), (size, 3 * tail)
    column = size - tail + lax.rem(iota(wide, 1), tail)
    along = iota(wide, 0) == column // rows
    is_high = iota(wide, 1) < 2 * tail
    picked = dot(high, (along & is_high).astype(jnp.bfloat16)) + dot(
        low, (along & ~is_high).astype(jnp.bfloat16)
    )
    same = lax.rem(iota(full, 0), rows) == lax.rem(iota(full, 1), rows)
    wider = dot(down, picked.astype(jnp.bfloat16))
    last_ref[...] = jnp.where(same, wider, 0.0).astype(jnp.bfloat16)


def spread_weights(widths, partners, count, rows, tail):
    size = widths.shape[0] * rows
    columns = [partner for partner in partners for _ in range(count)]
    shapes = [(size, size), (size, size), (size, 3 * tail)]
    return pl.pallas_call(
        functools.partial(weights_kernel, count=count, rows=rows),
        in_specs=[pl.BlockSpec(memory_space=VMEM)] * 2,
        out_specs=[pl.BlockSpec(memory_space=VMEM)] * 3,
        out_shape=[jax.ShapeDtypeStruct(shape, jnp.bfloat16) for shape in shapes],
        cost_estimate=pl.CostEstimate(
            flops=2 * size**3, bytes_accessed=4 * size**2, transcendentals=size
        ),
        compiler_params=pltpu.CompilerParams(vmem_limit_bytes=KERNEL_BYTES),
        name="weights",
    )(widths[None, :], jnp.array([columns], jnp.int32))


def split(part):
    high = part.astype(jnp.bfloat16)
    return high, (part - high.astype(jnp.float32)).astype(jnp.bfloat16)


def stacked(refs, span):
    return split(jnp.concatenate([ref[:, span] for ref in refs], axis=0))


def spans_of(columns):
    return [slice(start, start + WIDTH) for start in range(0, columns, WIDTH)]


def gather_kernel(high_ref, low_ref, *refs, begin, end):
    parts, total_ref = refs[:-1], refs[-1]
    dot = functools.partial(jnp.dot, preferred_element_type=jnp.float32)
    high, low = high_ref[:, begin:end], low_ref[:, begin:end]
    for span in spans_of(total_ref.shape[1]):
        part_high, part_low = stacked(parts, span)
        total_ref[:, span] = dot(high, part_high) + dot(high, part_low) + dot(low, part_high)


def write_kernel(high_ref, low_ref, so_far_ref, *refs, begin, end):
    parts, (total_ref, out_ref, done_ref, semaphores) = refs[:-4], refs[-4:]
    dot = functools.partial(jnp.dot, preferred_element_type=jnp.float32)
    high, low = high_ref[:, begin:end], low_ref[:, begin:end]
    copies = []
    for at, span in enumerate(spans_of(total_ref.shape[1])):
        part_high, part_low = stacked(parts, span)
        value = dot(high, part_high) + dot(high, part_low) + dot(low, part_high)
        value += so_far_ref[:, span]
        total_ref[:, span] = value
        done_ref[:, :, span] = value.reshape(*done_ref.shape[:2], WIDTH)
        copies.append(
            pltpu.make_async_copy(
                done_ref.at[:, :, span], out_ref.at[:, :, span], semaphores.at[at]
            )
        )
        copies[-1].start()
    for copy in copies:
        copy.wait()


def gather(high, low, so_far, parts, begin, end, rows):
    size, columns = high.shape[0], parts[0].shape[1]
    spec = pl.BlockSpec(memory_space=VMEM)
    total = jax.ShapeDtypeStruct((size, columns), jnp.float32)
    strip = (size // rows, rows, columns)
    first = so_far is None
    if first:
        ins, outs = [high, low] + parts, dict(out_specs=spec, out_shape=total)
    else:
        ins = [high, low, so_far] + parts
        outs = dict(
            out_specs=[spec, pl.BlockSpec(memory_space=pltpu.HBM)],
            out_shape=[total, jax.ShapeDtypeStruct(strip, jnp.float32)],
            scratch_shapes=[
                VMEM(strip, jnp.float32),
                pltpu.SemaphoreType.DMA((columns // WIDTH,)),
            ],
        )
    return pl.pallas_call(
        functools.partial(gather_kernel if first else write_kernel, begin=begin, end=end),
        in_specs=[spec] * len(ins),
        cost_estimate=pl.CostEstimate(
            flops=6 * size * (end - begin) * columns,
            bytes_accessed=8 * size * columns,
            transcendentals=0,
        ),
        compiler_params=pltpu.CompilerParams(vmem_limit_bytes=KERNEL_BYTES),
        name="temporal",
        **outs,
    )(*ins)


def reach(sources):
    exact = sources % SUBLANES == 0 and BAND % SUBLANES == 0
    reached = sources + 2 * BAND + (0 if exact else SUBLANES)
    return -(-reached // SUBLANES) * SUBLANES


def finish_kernel(weights_ref, so_far_ref, _, *refs, group, sources):
    parts, (out_ref, done_ref, semaphores) = refs[:-3], refs[-3:]
    times, rows, columns = out_ref.shape
    window = done_ref.shape[0]
    strips = SUBLANES // rows
    first = ((lax.axis_index("blk") // strips) ^ group) * sources
    start = jnp.maximum(first - BAND, 0) // SUBLANES * SUBLANES
    start = jnp.minimum(start, times - window)
    block = pl.ds(pl.multiple_of(start * rows, SUBLANES * rows), window * rows)
    weights = weights_ref[block, :]
    copies = []
    for at, span in enumerate(spans_of(columns)):
        high, low = stacked(parts, span)
        part = jnp.concatenate([high, low, high], axis=0)
        value = so_far_ref[block, span] + jnp.dot(
            weights, part, preferred_element_type=jnp.float32
        )
        done_ref[:, :, span] = value.reshape(window, rows, WIDTH)
        copies.append(
            pltpu.make_async_copy(
                done_ref.at[:, :, span],
                out_ref.at[pl.ds(start, window), :, span],
                semaphores.at[at],
            )
        )
        copies[-1].start()
    for copy in copies:
        copy.wait()


def finish(weights, so_far, out, parts, group, sources):
    times, rows, columns = out.shape
    window = min(times, reach(sources))
    spec = pl.BlockSpec(memory_space=VMEM)
    far = pl.BlockSpec(memory_space=pltpu.HBM)
    return pl.pallas_call(
        functools.partial(finish_kernel, group=group, sources=sources),
        in_specs=[spec, spec, far] + [spec] * len(parts),
        out_specs=far,
        out_shape=jax.ShapeDtypeStruct(out.shape, jnp.float32),
        input_output_aliases={2: 0},
        scratch_shapes=[
            VMEM((window, rows, columns), jnp.float32),
            pltpu.SemaphoreType.DMA((columns // WIDTH,)),
        ],
        cost_estimate=pl.CostEstimate(
            flops=2 * window * rows * weights.shape[1] * columns,
            bytes_accessed=8 * window * rows * columns,
            transcendentals=0,
        ),
        compiler_params=pltpu.CompilerParams(vmem_limit_bytes=KERNEL_BYTES),
        name="finish",
    )(weights, so_far, out, *parts)


def local(frames, widths, kernel, *, devices):
    count, height, _ = frames.shape
    rows = height // devices
    strips = SUBLANES // rows
    each = count * rows
    order = message_order(devices)

    tiles = list(dict.fromkeys(k // strips for k in order))
    made = {}
    for stage, (begin, end) in enumerate(zip((0,) + STAGES, STAGES + (len(tiles),))):
        groups = tiles[begin:end]
        outs = stencil(kernel, frames, groups, rows, stage == 0)
        made.update(zip((group * strips + at for group in groups for at in range(strips)), outs))

    arrived = {0: made[0]}
    for k in order:
        arrived[k] = lax.ppermute(made[k], "blk", [(i, i ^ k) for i in range(devices)])

    group = (devices - 1) // strips
    end = [group * strips + at for at in range(strips)]
    partners = [k for k in [0] + order if k not in end] + end
    middle, tail = devices // 2, devices - strips
    high, low, final = spread_weights(widths, partners, count, rows, strips * each)
    part = [arrived[k] for k in partners]
    total = gather(high, low, None, part[:middle], 0, middle * each, rows)
    total, out = gather(high, low, total, part[middle:tail], middle * each, tail * each, rows)
    return finish(final, total, out, part[tail:], group, strips * count)


def solution(mesh):
    devices = mesh.shape["blk"]
    return jax.shard_map(
        functools.partial(local, devices=devices),
        mesh=mesh,
        in_specs=(P("blk", None, None), P(), P()),
        out_specs=P(None, "blk", None),
        check_vma=False,
    )
```

time: 76.6 us -> 75 us (0.979)
  starting transfers between devices: 53.9 us -> 59.2 us
  local copies, waits for them, and re-layouts: 4.18 us -> 0.01 us
  Pallas kernels: 11.6 us -> 10.1 us
  waiting for transfers between devices: 6.36 us -> 5.43 us
    ppermute x31, starting transfers between devices: 53.9 us -> 59.2 us  [local(): lax.ppermute(made[k], 'blk', [(i, i ^ k) for i in range(devices)])]
    unnamed x16 -> x6, local copies, waits for them, and re-layouts: 4.18 us -> 0.01 us
    pallas_call x3 -> x2, Pallas kernels: 6.16 us -> 4.33 us  [stencil(): pl.pallas_call(functools.partial(stencil_kernel, groups=groups, rows=rows...]
    ppermute x31, waiting for transfers between devices: 6.36 us -> 5.43 us  [local(): lax.ppermute(made[k], 'blk', [(i, i ^ k) for i in range(devices)])]
  transfers between devices with their start and end apart: 31 -> 31, of which waited for: 7 -> 3; matrix products, arithmetic and copies ran while one was open for 0% -> 0% of each run, Pallas kernels for 11% -> 10%
where the time goes in v3:
time: 75 us; the launch traced here: 74.8 us
  starting transfers between devices  59.2 us (79%)
  Pallas kernels  10.1 us (13%)
  waiting for transfers between devices  5.43 us (7%)
    ppermute x31, starting transfers between devices, local(): lax.ppermute(made[k], 'blk', [(i, i ^ k) for i in range(devices)])  59.2 us
    ppermute x31, waiting for transfers between devices, local(): lax.ppermute(made[k], 'blk', [(i, i ^ k) for i in range(devices)])  5.43 us
    pallas_call x2, Pallas kernels, stencil(): pl.pallas_call(functools.partial(stencil_kernel, groups=groups, rows=rows...  4.33 us
    pallas_call x2, Pallas kernels, gather(): pl.pallas_call(functools.partial(gather_kernel if first else write_kernel...  3.43 us
  transfers between devices with their start and end apart: 31, of which 3 were waited for; matrix products, arithmetic and copies ran while one was open for 0% of the time, Pallas kernels for 10%

profile of v3, /device:TPU:0, one launch (start us, length us, event | category | flops | bytes accessed | tf_op | source)
XLA Modules:
  0.0 74.8 jit_solution(11858941771241849437)
XLA Ops:
  0.0 1.4 %stencil.3 = (f32[16,1280]{1,0:T(8,128)S(1)}, f32[16,1280]{1,0:T(8,128)S(1)}) custom-call(f32[3,3]{1,0:T(4,128)} %kernel_ref.3, f32[4,128,1280]{2,1,0:T(8,128)} %frames_ref.3), custom_call_target="tpu_custom_call" | custom-call | flops 819200 | bytes 327680 | tf_op jit(solution)/shard_map/stencil/pallas_call | solution.py:117
  1.4 4.2 %collective-permute-start = (f32[16,1280]{1,0:T(8,128)S(1)}, f32[16,1280]{1,0:T(8,128)S(1)}, u32[]{:S(2)}, u32[]{:S(2)}) collective-permute-start(f32[16,1280]{1,0:T(8,128)S(1)} %get-tuple-element.46), channel_id=1, source_target_pairs={{0,16},{1,17},{2,18},{3,19},{4,20},{5,21},{6,22},{7,23},{8,24},{9,... | collective-permute-start | bytes 245768 | tf_op jit(solution)/shard_map/ppermute | solution.py:346
  5.6 0.0 collective-permute-start.1
  5.6 2.9 %stencil.2 = (f32[16,1280]{1,0:T(8,128)S(1)}, f32[16,1280]{1,0:T(8,128)S(1)}, f32[16,1280]{1,0:T(8,128)S(1)}, f32[16,1280]{1,0:T(8,128)S(1)}, f32[16,1280]{1,0:T...) custom-call(f32[3,3]{1,0:T(4,128)} %kernel_ref.3, ...), custom_call_target="tpu_custom_call" | custom-call | flops 12288000 | bytes 4915200 | tf_op jit(solution)/shard_map/stencil/pallas_call | solution.py:117
  8.5 3.1 %collective-permute-start.2 = (f32[16,1280]{1,0:T(8,128)S(1)}, f32[16,1280]{1,0:T(8,128)S(1)}, u32[]{:S(2)}, u32[]{:S(2)}) collective-permute-start(f32[16,1280]{1,0:T(8,128)S(1)} %get-tuple-element.48), channel_id=1, source_target_pairs={{0,18},{1,19},{2,16},{3,17},{4,22},{5,23},{6,20},{7,21},{8,26},{9,... | collective-permute-start | bytes 245768 | tf_op jit(solution)/shard_map/ppermute | solution.py:346
  11.6 0.6 collective-permute-start.3
  12.2 1.6 %collective-permute-start.4 = (f32[16,1280]{1,0:T(8,128)S(1)}, f32[16,1280]{1,0:T(8,128)S(1)}, u32[]{:S(2)}, u32[]{:S(2)}) collective-permute-start(f32[16,1280]{1,0:T(8,128)S(1)} %get-tuple-element.50), channel_id=1, source_target_pairs={{0,8},{1,9},{2,10},{3,11},{4,12},{5,13},{6,14},{7,15},{8,0},{9,1},... | collective-permute-start | bytes 245768 | tf_op jit(solution)/shard_map/ppermute | solution.py:346
  13.8 0.0 collective-permute-done.refs_1_
  13.8 0.1 collective-permute-start.5
  13.9 0.0 collective-permute-done.1.refs_2_
  13.9 3.5 %collective-permute-start.6 = (f32[16,1280]{1,0:T(8,128)S(1)}, f32[16,1280]{1,0:T(8,128)S(1)}, u32[]{:S(2)}, u32[]{:S(2)}) collective-permute-start(f32[16,1280]{1,0:T(8,128)S(1)} %get-tuple-element.52), channel_id=1, source_target_pairs={{0,20},{1,21},{2,22},{3,23},{4,16},{5,17},{6,18},{7,19},{8,28},{9,... | collective-permute-start | bytes 245768 | tf_op jit(solution)/shard_map/ppermute | solution.py:346
  17.4 2.9 %collective-permute-done.2.refs_3_ = f32[16,1280]{1,0:T(8,128)S(1)} collective-permute-done((f32[16,1280]{1,0:T(8,128)S(1)}, f32[16,1280]{1,0:T(8,128)S(1)}, u32[]{:S(2)}, u32[]{:S(2)}) %collective-permute-start.2) | collective-permute-done | bytes 81952 | tf_op jit(solution)/shard_map/ppermute | solution.py:346
  20.3 2.5 %collective-permute-start.7 = (f32[16,1280]{1,0:T(8,128)S(1)}, f32[16,1280]{1,0:T(8,128)S(1)}, u32[]{:S(2)}, u32[]{:S(2)}) collective-permute-start(f32[16,1280]{1,0:T(8,128)S(1)} %get-tuple-element.53), channel_id=1, source_target_pairs={{0,10},{1,11},{2,8},{3,9},{4,14},{5,15},{6,12},{7,13},{8,2},{9,3},... | collective-permute-start | bytes 245768 | tf_op jit(solution)/shard_map/ppermute | solution.py:346
  22.8 0.0 collective-permute-done.3.refs_4_
  22.8 1.3 %collective-permute-start.8 = (f32[16,1280]{1,0:T(8,128)S(1)}, f32[16,1280]{1,0:T(8,128)S(1)}, u32[]{:S(2)}, u32[]{:S(2)}) collective-permute-start(f32[16,1280]{1,0:T(8,128)S(1)} %get-tuple-element.54), channel_id=1, source_target_pairs={{0,21},{1,20},{2,23},{3,22},{4,17},{5,16},{6,19},{7,18},{8,29},{9,... | collective-permute-start | bytes 245768 | tf_op jit(solution)/shard_map/ppermute | solution.py:346
  24.1 0.0 collective-permute-done.4.refs_5_
  24.1 2.1 %collective-permute-start.9 = (f32[16,1280]{1,0:T(8,128)S(1)}, f32[16,1280]{1,0:T(8,128)S(1)}, u32[]{:S(2)}, u32[]{:S(2)}) collective-permute-start(f32[16,1280]{1,0:T(8,128)S(1)} %get-tuple-element.55), channel_id=1, source_target_pairs={{0,11},{1,10},{2,9},{3,8},{4,15},{5,14},{6,13},{7,12},{8,3},{9,2},... | collective-permute-start | bytes 245768 | tf_op jit(solution)/shard_map/ppermute | solution.py:346
  26.2 0.0 collective-permute-done.5.refs_6_
  26.2 2.6 %collective-permute-start.10 = (f32[16,1280]{1,0:T(8,128)S(1)}, f32[16,1280]{1,0:T(8,128)S(1)}, u32[]{:S(2)}, u32[]{:S(2)}) collective-permute-start(f32[16,1280]{1,0:T(8,128)S(1)} %get-tuple-element.56), channel_id=1, source_target_pairs={{0,22},{1,23},{2,20},{3,21},{4,18},{5,19},{6,16},{7,17},{8,30},{9,... | collective-permute-start | bytes 245768 | tf_op jit(solution)/shard_map/ppermute | solution.py:346
  28.8 0.0 collective-permute-done.6.refs_7_
  28.8 0.4 collective-permute-start.11
  29.2 0.0 collective-permute-done.7.refs_8_
  29.2 2.8 %collective-permute-start.12 = (f32[16,1280]{1,0:T(8,128)S(1)}, f32[16,1280]{1,0:T(8,128)S(1)}, u32[]{:S(2)}, u32[]{:S(2)}) collective-permute-start(f32[16,1280]{1,0:T(8,128)S(1)} %get-tuple-element.58), channel_id=1, source_target_pairs={{0,23},{1,22},{2,21},{3,20},{4,19},{5,18},{6,17},{7,16},{8,31},{9,... | collective-permute-start | bytes 245768 | tf_op jit(solution)/shard_map/ppermute | solution.py:346
  32.0 0.0 collective-permute-done.8.refs_9_
  32.0 1.6 %collective-permute-start.13 = (f32[16,1280]{1,0:T(8,128)S(1)}, f32[16,1280]{1,0:T(8,128)S(1)}, u32[]{:S(2)}, u32[]{:S(2)}) collective-permute-start(f32[16,1280]{1,0:T(8,128)S(1)} %get-tuple-element.59), channel_id=1, source_target_pairs={{0,13},{1,12},{2,15},{3,14},{4,9},{5,8},{6,11},{7,10},{8,5},{9,4},... | collective-permute-start | bytes 245768 | tf_op jit(solution)/shard_map/ppermute | solution.py:346
  33.6 0.0 collective-permute-done.9.refs_10_
  33.6 2.6 %collective-permute-start.14 = (f32[16,1280]{1,0:T(8,128)S(1)}, f32[16,1280]{1,0:T(8,128)S(1)}, u32[]{:S(2)}, u32[]{:S(2)}) collective-permute-start(f32[16,1280]{1,0:T(8,128)S(1)} %get-tuple-element.60), channel_id=1, source_target_pairs={{0,14},{1,15},{2,12},{3,13},{4,10},{5,11},{6,8},{7,9},{8,6},{9,7},... | collective-permute-start | bytes 245768 | tf_op jit(solution)/shard_map/ppermute | solution.py:346
  36.2 0.0 collective-permute-done.10.refs_11_
  36.2 1.5 %collective-permute-start.15 = (f32[16,1280]{1,0:T(8,128)S(1)}, f32[16,1280]{1,0:T(8,128)S(1)}, u32[]{:S(2)}, u32[]{:S(2)}) collective-permute-start(f32[16,1280]{1,0:T(8,128)S(1)} %get-tuple-element.61), channel_id=1, source_target_pairs={{0,24},{1,25},{2,26},{3,27},{4,28},{5,29},{6,30},{7,31},{8,16},{9,... | collective-permute-start | bytes 245768 | tf_op jit(solution)/shard_map/ppermute | solution.py:346
  37.7 0.0 collective-permute-done.11.refs_12_
  37.7 0.6 collective-permute-start.16
  38.3 0.0 collective-permute-done.12.refs_13_
  38.3 4.2 %collective-permute-start.17 = (f32[16,1280]{1,0:T(8,128)S(1)}, f32[16,1280]{1,0:T(8,128)S(1)}, u32[]{:S(2)}, u32[]{:S(2)}) collective-permute-start(f32[16,1280]{1,0:T(8,128)S(1)} %get-tuple-element.63), channel_id=1, source_target_pairs={{0,25},{1,24},{2,27},{3,26},{4,29},{5,28},{6,31},{7,30},{8,17},{9,... | collective-permute-start | bytes 245768 | tf_op jit(solution)/shard_map/ppermute | solution.py:346
  42.5 0.0 collective-permute-done.13.refs_14_
  42.5 0.7 collective-permute-start.18
  43.2 0.0 collective-permute-done.14.refs_15_
  43.2 1.6 %collective-permute-start.19 = (f32[16,1280]{1,0:T(8,128)S(1)}, f32[16,1280]{1,0:T(8,128)S(1)}, u32[]{:S(2)}, u32[]{:S(2)}) collective-permute-start(f32[16,1280]{1,0:T(8,128)S(1)} %get-tuple-element.65), channel_id=1, source_target_pairs={{0,26},{1,27},{2,24},{3,25},{4,30},{5,31},{6,28},{7,29},{8,18},{9,... | collective-permute-start | bytes 245768 | tf_op jit(solution)/shard_map/ppermute | solution.py:346
  44.8 0.0 collective-permute-done.15.refs_0_
  44.8 3.9 %collective-permute-start.20 = (f32[16,1280]{1,0:T(8,128)S(1)}, f32[16,1280]{1,0:T(8,128)S(1)}, u32[]{:S(2)}, u32[]{:S(2)}) collective-permute-start(f32[16,1280]{1,0:T(8,128)S(1)} %get-tuple-element.66), channel_id=1, source_target_pairs={{0,2},{1,3},{2,0},{3,1},{4,6},{5,7},{6,4},{7,5},{8,10},{9,11},{10,... | collective-permute-start | bytes 245768 | tf_op jit(solution)/shard_map/ppermute | solution.py:346
  48.8 0.0 collective-permute-done.16.refs_1_
  48.8 0.0 collective-permute-start.21
  48.8 0.0 collective-permute-done.17.refs_2_
  48.8 1.6 %collective-permute-start.22 = (f32[16,1280]{1,0:T(8,128)S(1)}, f32[16,1280]{1,0:T(8,128)S(1)}, u32[]{:S(2)}, u32[]{:S(2)}) collective-permute-start(f32[16,1280]{1,0:T(8,128)S(1)} %get-tuple-element.68), channel_id=1, source_target_pairs={{0,3},{1,2},{2,1},{3,0},{4,7},{5,6},{6,5},{7,4},{8,11},{9,10},{10,... | collective-permute-start | bytes 245768 | tf_op jit(solution)/shard_map/ppermute | solution.py:346
  50.4 0.0 collective-permute-done.18.refs_3_
  50.4 1.0 %collective-permute-start.23 = (f32[16,1280]{1,0:T(8,128)S(1)}, f32[16,1280]{1,0:T(8,128)S(1)}, u32[]{:S(2)}, u32[]{:S(2)}) collective-permute-start(f32[16,1280]{1,0:T(8,128)S(1)} %get-tuple-element.69), channel_id=1, source_target_pairs={{0,4},{1,5},{2,6},{3,7},{4,0},{5,1},{6,2},{7,3},{8,12},{9,13},{10,... | collective-permute-start | bytes 245768 | tf_op jit(solution)/shard_map/ppermute | solution.py:346
  51.3 1.1 %weights.1 = (bf16[512,512]{1,0:T(8,128)(2,1)S(1)}, bf16[512,512]{1,0:T(8,128)(2,1)S(1)}, bf16[512,96]{1,0:T(8,128)(2,1)S(1)}) custom-call(f32[1,128]{1,0:T(1,128)S(1)} %bitcast.1, s32[1,128]{1,0:T(1,128)S(1)} %copy-done.2), custom_call_target="tpu_custom_call" | custom-call | flops 268435456 | bytes 1048576 | tf_op jit(solution)/shard_map/weights/pallas_call | solution.py:181
  52.4 0.0 collective-permute-done.19.refs_4_
  52.5 4.0 %collective-permute-start.24 = (f32[16,1280]{1,0:T(8,128)S(1)}, f32[16,1280]{1,0:T(8,128)S(1)}, u32[]{:S(2)}, u32[]{:S(2)}) collective-permute-start(f32[16,1280]{1,0:T(8,128)S(1)} %get-tuple-element.70), channel_id=1, source_target_pairs={{0,28},{1,29},{2,30},{3,31},{4,24},{5,25},{6,26},{7,27},{8,20},{9,... | collective-permute-start | bytes 245768 | tf_op jit(solution)/shard_map/ppermute | solution.py:346
  56.4 0.0 collective-permute-done.20.refs_5_
  56.4 0.0 collective-permute-start.25
  56.4 0.0 collective-permute-done.21.refs_6_
  56.4 1.6 %collective-permute-start.26 = (f32[16,1280]{1,0:T(8,128)S(1)}, f32[16,1280]{1,0:T(8,128)S(1)}, u32[]{:S(2)}, u32[]{:S(2)}) collective-permute-start(f32[16,1280]{1,0:T(8,128)S(1)} %get-tuple-element.72), channel_id=1, source_target_pairs={{0,29},{1,28},{2,31},{3,30},{4,25},{5,24},{6,27},{7,26},{8,21},{9,... | collective-permute-start | bytes 245768 | tf_op jit(solution)/shard_map/ppermute | solution.py:346
  58.0 2.4 %collective-permute-start.27 = (f32[16,1280]{1,0:T(8,128)S(1)}, f32[16,1280]{1,0:T(8,128)S(1)}, u32[]{:S(2)}, u32[]{:S(2)}) collective-permute-start(f32[16,1280]{1,0:T(8,128)S(1)} %get-tuple-element.73), channel_id=1, source_target_pairs={{0,6},{1,7},{2,4},{3,5},{4,2},{5,3},{6,0},{7,1},{8,14},{9,15},{10,... | collective-permute-start | bytes 245768 | tf_op jit(solution)/shard_map/ppermute | solution.py:346
  60.4 0.0 collective-permute-done.23.refs_8_
  60.4 1.4 %collective-permute-start.28 = (f32[16,1280]{1,0:T(8,128)S(1)}, f32[16,1280]{1,0:T(8,128)S(1)}, u32[]{:S(2)}, u32[]{:S(2)}) collective-permute-start(f32[16,1280]{1,0:T(8,128)S(1)} %get-tuple-element.74), channel_id=1, source_target_pairs={{0,7},{1,6},{2,5},{3,4},{4,3},{5,2},{6,1},{7,0},{8,15},{9,14},{10,... | collective-permute-start | bytes 245768 | tf_op jit(solution)/shard_map/ppermute | solution.py:346
  61.7 1.2 %temporal.2.so_far_ref = f32[512,1280]{1,0:T(8,128)S(1)} custom-call(bf16[512,512]{1,0:T(8,128)(2,1)S(1)} %get-tuple-element.43.high_ref, bf16[512,512]{1,0:T(8,128)(2,1)S(1)} %get-tuple-element.44.low_ref, f32[16,1280]{1,0:T(8,128)S(1)} %get-tuple-element.45.refs_0_, f32[16,1280]{1,0:T(8,128)S(1)} %collective-permute-done.refs_1_, ...), custom_call_target="tpu_custom_call" | custom-call | flops 1006632960 | bytes 5242880 | tf_op jit(solution)/shard_map/temporal/pallas_call | solution.py:255
  62.9 0.0 collective-permute-done.24.refs_9_
  62.9 2.1 %collective-permute-start.29 = (f32[16,1280]{1,0:T(8,128)S(1)}, f32[16,1280]{1,0:T(8,128)S(1)}, u32[]{:S(2)}, u32[]{:S(2)}) collective-permute-start(f32[16,1280]{1,0:T(8,128)S(1)} %get-tuple-element.77), channel_id=1, source_target_pairs={{0,30},{1,31},{2,28},{3,29},{4,26},{5,27},{6,24},{7,25},{8,22},{9,... | collective-permute-start | bytes 245768 | tf_op jit(solution)/shard_map/ppermute | solution.py:346
  65.1 0.7 collective-permute-done.25.refs_10_
  65.8 3.8 %collective-permute-start.30 = (f32[16,1280]{1,0:T(8,128)S(1)}, f32[16,1280]{1,0:T(8,128)S(1)}, u32[]{:S(2)}, u32[]{:S(2)}) collective-permute-start(f32[16,1280]{1,0:T(8,128)S(1)} %get-tuple-element.78), channel_id=1, source_target_pairs={{0,31},{1,30},{2,29},{3,28},{4,27},{5,26},{6,25},{7,24},{8,23},{9,... | collective-permute-start | bytes 245768 | tf_op jit(solution)/shard_map/ppermute | solution.py:346
  69.6 2.2 %temporal.3 = (f32[512,1280]{1,0:T(8,128)S(1)}, f32[128,4,1280]{2,1,0:T(4,128)}) custom-call(bf16[512,512]{1,0:T(8,128)(2,1)S(1)} %get-tuple-element.43.high_ref, bf16[512,512]{1,0:T(8,128)(2,1)S(1)} %get-tuple-element.44.low_ref, f32[512,1280]{1,0:T(8,128)S(1)} %temporal.2.so_far_ref, f32[16,1280]{1,0:T(8,128)S(1)} %collective-permute-done.15.refs_0_, ...), custom_call_target="tpu_custom_call" | custom-call | flops 880803840 | bytes 5242880 | tf_op jit(solution)/shard_map/temporal/pallas_call | solution.py:255
  71.8 0.0 collective-permute-done.29.refs_0_
  71.9 1.7 %collective-permute-done.30.refs_1_ = f32[16,1280]{1,0:T(8,128)S(1)} collective-permute-done((f32[16,1280]{1,0:T(8,128)S(1)}, f32[16,1280]{1,0:T(8,128)S(1)}, u32[]{:S(2)}, u32[]{:S(2)}) %collective-permute-start.30) | collective-permute-done | bytes 81952 | tf_op jit(solution)/shard_map/ppermute | solution.py:346
  73.6 1.2 %finish.1 = f32[128,4,1280]{2,1,0:T(4,128)} custom-call(bf16[512,96]{1,0:T(8,128)(2,1)S(1)} %get-tuple-element.42.weights_ref, f32[512,1280]{1,0:T(8,128)S(1)} %get-tuple-element.75.so_far_ref, f32[128,4,1280]{2,1,0:T(4,128)} %get-tuple-element.76._, f32[16,1280]{1,0:T(8,128)S(1)} %collective-permute-done.29.refs_0_, ...), custom_call_target="tpu_custom_call", output_to_operand_aliasing={{}: (2, {})} | custom-call | flops 55050240 | bytes 2293760 | tf_op jit(solution)/shard_map/finish/pallas_call | solution.py:310
  (10 shorter events, 0.0 us)
Async XLA Ops:
  0.0 51.3 %copy-start.2 = (s32[1,128]{1,0:T(1,128)S(1)}, s32[1,128]{1,0:T(1,128)}, u32[]{:S(2)}) copy-start(s32[1,128]{1,0:T(1,128)} %constant.2.clone.partner_ref) | copy-start | bytes 1540
  0.0 5.6 %copy-start = (f32[4,128,1280]{2,1,0:T(8,128)S(1)}, f32[4,128,1280]{2,1,0:T(8,128)}, u32[]{:S(2)}) copy-start(f32[4,128,1280]{2,1,0:T(8,128)} %frames_ref.3) | copy-start | bytes 7864324
  0.0 51.3 %copy-start.1 = (f32[128]{0:T(128)S(1)}, f32[128]{0:T(128)}, u32[]{:S(2)}) copy-start(f32[128]{0:T(128)} %param.5) | copy-start | bytes 1540
  1.4 12.4 %collective-permute-start = (f32[16,1280]{1,0:T(8,128)S(1)}, f32[16,1280]{1,0:T(8,128)S(1)}, u32[]{:S(2)}, u32[]{:S(2)}) collective-permute-start(f32[16,1280]{1,0:T(8,128)S(1)} %get-tuple-element.46), channel_id=1, source_target_pairs={{0,16},{1,17},{2,18},{3,19},{4,20},{5,21},{6,22},{7,23},{8,24},{9,... | collective-permute-start | bytes 245768 | tf_op jit(solution)/shard_map/ppermute | solution.py:346
  5.6 8.3 %collective-permute-start.1 = (f32[16,1280]{1,0:T(8,128)S(1)}, f32[16,1280]{1,0:T(8,128)S(1)}, u32[]{:S(2)}, u32[]{:S(2)}) collective-permute-start(f32[16,1280]{1,0:T(8,128)S(1)} %get-tuple-element.47), channel_id=1, source_target_pairs={{0,17},{1,16},{2,19},{3,18},{4,21},{5,20},{6,23},{7,22},{8,25},{9,... | collective-permute-start | bytes 245768 | tf_op jit(solution)/shard_map/ppermute | solution.py:346
  8.5 11.8 %collective-permute-start.2 = (f32[16,1280]{1,0:T(8,128)S(1)}, f32[16,1280]{1,0:T(8,128)S(1)}, u32[]{:S(2)}, u32[]{:S(2)}) collective-permute-start(f32[16,1280]{1,0:T(8,128)S(1)} %get-tuple-element.48), channel_id=1, source_target_pairs={{0,18},{1,19},{2,16},{3,17},{4,22},{5,23},{6,20},{7,21},{8,26},{9,... | collective-permute-start | bytes 245768 | tf_op jit(solution)/shard_map/ppermute | solution.py:346
  11.6 11.2 %collective-permute-start.3 = (f32[16,1280]{1,0:T(8,128)S(1)}, f32[16,1280]{1,0:T(8,128)S(1)}, u32[]{:S(2)}, u32[]{:S(2)}) collective-permute-start(f32[16,1280]{1,0:T(8,128)S(1)} %get-tuple-element.49), channel_id=1, source_target_pairs={{0,19},{1,18},{2,17},{3,16},{4,23},{5,22},{6,21},{7,20},{8,27},{9,... | collective-permute-start | bytes 245768 | tf_op jit(solution)/shard_map/ppermute | solution.py:346
  12.2 11.9 %collective-permute-start.4 = (f32[16,1280]{1,0:T(8,128)S(1)}, f32[16,1280]{1,0:T(8,128)S(1)}, u32[]{:S(2)}, u32[]{:S(2)}) collective-permute-start(f32[16,1280]{1,0:T(8,128)S(1)} %get-tuple-element.50), channel_id=1, source_target_pairs={{0,8},{1,9},{2,10},{3,11},{4,12},{5,13},{6,14},{7,15},{8,0},{9,1},... | collective-permute-start | bytes 245768 | tf_op jit(solution)/shard_map/ppermute | solution.py:346
  13.8 12.4 %collective-permute-start.5 = (f32[16,1280]{1,0:T(8,128)S(1)}, f32[16,1280]{1,0:T(8,128)S(1)}, u32[]{:S(2)}, u32[]{:S(2)}) collective-permute-start(f32[16,1280]{1,0:T(8,128)S(1)} %get-tuple-element.51), channel_id=1, source_target_pairs={{0,9},{1,8},{2,11},{3,10},{4,13},{5,12},{6,15},{7,14},{8,1},{9,0},... | collective-permute-start | bytes 245768 | tf_op jit(solution)/shard_map/ppermute | solution.py:346
  13.9 15.0 %collective-permute-start.6 = (f32[16,1280]{1,0:T(8,128)S(1)}, f32[16,1280]{1,0:T(8,128)S(1)}, u32[]{:S(2)}, u32[]{:S(2)}) collective-permute-start(f32[16,1280]{1,0:T(8,128)S(1)} %get-tuple-element.52), channel_id=1, source_target_pairs={{0,20},{1,21},{2,22},{3,23},{4,16},{5,17},{6,18},{7,19},{8,28},{9,... | collective-permute-start | bytes 245768 | tf_op jit(solution)/shard_map/ppermute | solution.py:346
  20.3 8.9 %collective-permute-start.7 = (f32[16,1280]{1,0:T(8,128)S(1)}, f32[16,1280]{1,0:T(8,128)S(1)}, u32[]{:S(2)}, u32[]{:S(2)}) collective-permute-start(f32[16,1280]{1,0:T(8,128)S(1)} %get-tuple-element.53), channel_id=1, source_target_pairs={{0,10},{1,11},{2,8},{3,9},{4,14},{5,15},{6,12},{7,13},{8,2},{9,3},... | collective-permute-start | bytes 245768 | tf_op jit(solution)/shard_map/ppermute | solution.py:346
  22.8 9.2 %collective-permute-start.8 = (f32[16,1280]{1,0:T(8,128)S(1)}, f32[16,1280]{1,0:T(8,128)S(1)}, u32[]{:S(2)}, u32[]{:S(2)}) collective-permute-start(f32[16,1280]{1,0:T(8,128)S(1)} %get-tuple-element.54), channel_id=1, source_target_pairs={{0,21},{1,20},{2,23},{3,22},{4,17},{5,16},{6,19},{7,18},{8,29},{9,... | collective-permute-start | bytes 245768 | tf_op jit(solution)/shard_map/ppermute | solution.py:346
  24.1 9.5 %collective-permute-start.9 = (f32[16,1280]{1,0:T(8,128)S(1)}, f32[16,1280]{1,0:T(8,128)S(1)}, u32[]{:S(2)}, u32[]{:S(2)}) collective-permute-start(f32[16,1280]{1,0:T(8,128)S(1)} %get-tuple-element.55), channel_id=1, source_target_pairs={{0,11},{1,10},{2,9},{3,8},{4,15},{5,14},{6,13},{7,12},{8,3},{9,2},... | collective-permute-start | bytes 245768 | tf_op jit(solution)/shard_map/ppermute | solution.py:346
  26.2 10.0 %collective-permute-start.10 = (f32[16,1280]{1,0:T(8,128)S(1)}, f32[16,1280]{1,0:T(8,128)S(1)}, u32[]{:S(2)}, u32[]{:S(2)}) collective-permute-start(f32[16,1280]{1,0:T(8,128)S(1)} %get-tuple-element.56), channel_id=1, source_target_pairs={{0,22},{1,23},{2,20},{3,21},{4,18},{5,19},{6,16},{7,17},{8,30},{9,... | collective-permute-start | bytes 245768 | tf_op jit(solution)/shard_map/ppermute | solution.py:346
  28.8 8.8 %collective-permute-start.11 = (f32[16,1280]{1,0:T(8,128)S(1)}, f32[16,1280]{1,0:T(8,128)S(1)}, u32[]{:S(2)}, u32[]{:S(2)}) collective-permute-start(f32[16,1280]{1,0:T(8,128)S(1)} %get-tuple-element.57), channel_id=1, source_target_pairs={{0,12},{1,13},{2,14},{3,15},{4,8},{5,9},{6,10},{7,11},{8,4},{9,5},... | collective-permute-start | bytes 245768 | tf_op jit(solution)/shard_map/ppermute | solution.py:346
  29.2 9.1 %collective-permute-start.12 = (f32[16,1280]{1,0:T(8,128)S(1)}, f32[16,1280]{1,0:T(8,128)S(1)}, u32[]{:S(2)}, u32[]{:S(2)}) collective-permute-start(f32[16,1280]{1,0:T(8,128)S(1)} %get-tuple-element.58), channel_id=1, source_target_pairs={{0,23},{1,22},{2,21},{3,20},{4,19},{5,18},{6,17},{7,16},{8,31},{9,... | collective-permute-start | bytes 245768 | tf_op jit(solution)/shard_map/ppermute | solution.py:346
  32.0 10.4 %collective-permute-start.13 = (f32[16,1280]{1,0:T(8,128)S(1)}, f32[16,1280]{1,0:T(8,128)S(1)}, u32[]{:S(2)}, u32[]{:S(2)}) collective-permute-start(f32[16,1280]{1,0:T(8,128)S(1)} %get-tuple-element.59), channel_id=1, source_target_pairs={{0,13},{1,12},{2,15},{3,14},{4,9},{5,8},{6,11},{7,10},{8,5},{9,4},... | collective-permute-start | bytes 245768 | tf_op jit(solution)/shard_map/ppermute | solution.py:346
  33.6 9.6 %collective-permute-start.14 = (f32[16,1280]{1,0:T(8,128)S(1)}, f32[16,1280]{1,0:T(8,128)S(1)}, u32[]{:S(2)}, u32[]{:S(2)}) collective-permute-start(f32[16,1280]{1,0:T(8,128)S(1)} %get-tuple-element.60), channel_id=1, source_target_pairs={{0,14},{1,15},{2,12},{3,13},{4,10},{5,11},{6,8},{7,9},{8,6},{9,7},... | collective-permute-start | bytes 245768 | tf_op jit(solution)/shard_map/ppermute | solution.py:346
  36.2 8.6 %collective-permute-start.15 = (f32[16,1280]{1,0:T(8,128)S(1)}, f32[16,1280]{1,0:T(8,128)S(1)}, u32[]{:S(2)}, u32[]{:S(2)}) collective-permute-start(f32[16,1280]{1,0:T(8,128)S(1)} %get-tuple-element.61), channel_id=1, source_target_pairs={{0,24},{1,25},{2,26},{3,27},{4,28},{5,29},{6,30},{7,31},{8,16},{9,... | collective-permute-start | bytes 245768 | tf_op jit(solution)/shard_map/ppermute | solution.py:346
  37.7 11.1 %collective-permute-start.16 = (f32[16,1280]{1,0:T(8,128)S(1)}, f32[16,1280]{1,0:T(8,128)S(1)}, u32[]{:S(2)}, u32[]{:S(2)}) collective-permute-start(f32[16,1280]{1,0:T(8,128)S(1)} %get-tuple-element.62), channel_id=1, source_target_pairs={{0,15},{1,14},{2,13},{3,12},{4,11},{5,10},{6,9},{7,8},{8,7},{9,6},... | collective-permute-start | bytes 245768 | tf_op jit(solution)/shard_map/ppermute | solution.py:346
  38.3 10.5 %collective-permute-start.17 = (f32[16,1280]{1,0:T(8,128)S(1)}, f32[16,1280]{1,0:T(8,128)S(1)}, u32[]{:S(2)}, u32[]{:S(2)}) collective-permute-start(f32[16,1280]{1,0:T(8,128)S(1)} %get-tuple-element.63), channel_id=1, source_target_pairs={{0,25},{1,24},{2,27},{3,26},{4,29},{5,28},{6,31},{7,30},{8,17},{9,... | collective-permute-start | bytes 245768 | tf_op jit(solution)/shard_map/ppermute | solution.py:346
  42.5 7.9 %collective-permute-start.18 = (f32[16,1280]{1,0:T(8,128)S(1)}, f32[16,1280]{1,0:T(8,128)S(1)}, u32[]{:S(2)}, u32[]{:S(2)}) collective-permute-start(f32[16,1280]{1,0:T(8,128)S(1)} %get-tuple-element.64), channel_id=1, source_target_pairs={{0,1},{1,0},{2,3},{3,2},{4,5},{5,4},{6,7},{7,6},{8,9},{9,8},{10,11... | collective-permute-start | bytes 245768 | tf_op jit(solution)/shard_map/ppermute | solution.py:346
  43.2 9.3 %collective-permute-start.19 = (f32[16,1280]{1,0:T(8,128)S(1)}, f32[16,1280]{1,0:T(8,128)S(1)}, u32[]{:S(2)}, u32[]{:S(2)}) collective-permute-start(f32[16,1280]{1,0:T(8,128)S(1)} %get-tuple-element.65), channel_id=1, source_target_pairs={{0,26},{1,27},{2,24},{3,25},{4,30},{5,31},{6,28},{7,29},{8,18},{9,... | collective-permute-start | bytes 245768 | tf_op jit(solution)/shard_map/ppermute | solution.py:346
  44.8 11.6 %collective-permute-start.20 = (f32[16,1280]{1,0:T(8,128)S(1)}, f32[16,1280]{1,0:T(8,128)S(1)}, u32[]{:S(2)}, u32[]{:S(2)}) collective-permute-start(f32[16,1280]{1,0:T(8,128)S(1)} %get-tuple-element.66), channel_id=1, source_target_pairs={{0,2},{1,3},{2,0},{3,1},{4,6},{5,7},{6,4},{7,5},{8,10},{9,11},{10,... | collective-permute-start | bytes 245768 | tf_op jit(solution)/shard_map/ppermute | solution.py:346
  48.8 7.7 %collective-permute-start.21 = (f32[16,1280]{1,0:T(8,128)S(1)}, f32[16,1280]{1,0:T(8,128)S(1)}, u32[]{:S(2)}, u32[]{:S(2)}) collective-permute-start(f32[16,1280]{1,0:T(8,128)S(1)} %get-tuple-element.67), channel_id=1, source_target_pairs={{0,27},{1,26},{2,25},{3,24},{4,31},{5,30},{6,29},{7,28},{8,19},{9,... | collective-permute-start | bytes 245768 | tf_op jit(solution)/shard_map/ppermute | solution.py:346
  48.8 9.3 %collective-permute-start.22 = (f32[16,1280]{1,0:T(8,128)S(1)}, f32[16,1280]{1,0:T(8,128)S(1)}, u32[]{:S(2)}, u32[]{:S(2)}) collective-permute-start(f32[16,1280]{1,0:T(8,128)S(1)} %get-tuple-element.68), channel_id=1, source_target_pairs={{0,3},{1,2},{2,1},{3,0},{4,7},{5,6},{6,5},{7,4},{8,11},{9,10},{10,... | collective-permute-start | bytes 245768 | tf_op jit(solution)/shard_map/ppermute | solution.py:346
  50.4 10.0 %collective-permute-start.23 = (f32[16,1280]{1,0:T(8,128)S(1)}, f32[16,1280]{1,0:T(8,128)S(1)}, u32[]{:S(2)}, u32[]{:S(2)}) collective-permute-start(f32[16,1280]{1,0:T(8,128)S(1)} %get-tuple-element.69), channel_id=1, source_target_pairs={{0,4},{1,5},{2,6},{3,7},{4,0},{5,1},{6,2},{7,3},{8,12},{9,13},{10,... | collective-permute-start | bytes 245768 | tf_op jit(solution)/shard_map/ppermute | solution.py:346
  52.5 10.5 %collective-permute-start.24 = (f32[16,1280]{1,0:T(8,128)S(1)}, f32[16,1280]{1,0:T(8,128)S(1)}, u32[]{:S(2)}, u32[]{:S(2)}) collective-permute-start(f32[16,1280]{1,0:T(8,128)S(1)} %get-tuple-element.70), channel_id=1, source_target_pairs={{0,28},{1,29},{2,30},{3,31},{4,24},{5,25},{6,26},{7,27},{8,20},{9,... | collective-permute-start | bytes 245768 | tf_op jit(solution)/shard_map/ppermute | solution.py:346
  56.4 9.3 %collective-permute-start.25 = (f32[16,1280]{1,0:T(8,128)S(1)}, f32[16,1280]{1,0:T(8,128)S(1)}, u32[]{:S(2)}, u32[]{:S(2)}) collective-permute-start(f32[16,1280]{1,0:T(8,128)S(1)} %get-tuple-element.71), channel_id=1, source_target_pairs={{0,5},{1,4},{2,7},{3,6},{4,1},{5,0},{6,3},{7,2},{8,13},{9,12},{10,... | collective-permute-start | bytes 245768 | tf_op jit(solution)/shard_map/ppermute | solution.py:346
  56.4 13.1 %collective-permute-start.26 = (f32[16,1280]{1,0:T(8,128)S(1)}, f32[16,1280]{1,0:T(8,128)S(1)}, u32[]{:S(2)}, u32[]{:S(2)}) collective-permute-start(f32[16,1280]{1,0:T(8,128)S(1)} %get-tuple-element.72), channel_id=1, source_target_pairs={{0,29},{1,28},{2,31},{3,30},{4,25},{5,24},{6,27},{7,26},{8,21},{9,... | collective-permute-start | bytes 245768 | tf_op jit(solution)/shard_map/ppermute | solution.py:346
  58.0 11.6 %collective-permute-start.27 = (f32[16,1280]{1,0:T(8,128)S(1)}, f32[16,1280]{1,0:T(8,128)S(1)}, u32[]{:S(2)}, u32[]{:S(2)}) collective-permute-start(f32[16,1280]{1,0:T(8,128)S(1)} %get-tuple-element.73), channel_id=1, source_target_pairs={{0,6},{1,7},{2,4},{3,5},{4,2},{5,3},{6,0},{7,1},{8,14},{9,15},{10,... | collective-permute-start | bytes 245768 | tf_op jit(solution)/shard_map/ppermute | solution.py:346
  60.4 9.2 %collective-permute-start.28 = (f32[16,1280]{1,0:T(8,128)S(1)}, f32[16,1280]{1,0:T(8,128)S(1)}, u32[]{:S(2)}, u32[]{:S(2)}) collective-permute-start(f32[16,1280]{1,0:T(8,128)S(1)} %get-tuple-element.74), channel_id=1, source_target_pairs={{0,7},{1,6},{2,5},{3,4},{4,3},{5,2},{6,1},{7,0},{8,15},{9,14},{10,... | collective-permute-start | bytes 245768 | tf_op jit(solution)/shard_map/ppermute | solution.py:346
  62.9 8.9 %collective-permute-start.29 = (f32[16,1280]{1,0:T(8,128)S(1)}, f32[16,1280]{1,0:T(8,128)S(1)}, u32[]{:S(2)}, u32[]{:S(2)}) collective-permute-start(f32[16,1280]{1,0:T(8,128)S(1)} %get-tuple-element.77), channel_id=1, source_target_pairs={{0,30},{1,31},{2,28},{3,29},{4,26},{5,27},{6,24},{7,25},{8,22},{9,... | collective-permute-start | bytes 245768 | tf_op jit(solution)/shard_map/ppermute | solution.py:346
  65.8 7.8 %collective-permute-start.30 = (f32[16,1280]{1,0:T(8,128)S(1)}, f32[16,1280]{1,0:T(8,128)S(1)}, u32[]{:S(2)}, u32[]{:S(2)}) collective-permute-start(f32[16,1280]{1,0:T(8,128)S(1)} %get-tuple-element.78), channel_id=1, source_target_pairs={{0,31},{1,30},{2,29},{3,28},{4,27},{5,26},{6,25},{7,24},{8,23},{9,... | collective-permute-start | bytes 245768 | tf_op jit(solution)/shard_map/ppermute | solution.py:346

commit v4 on v3

--- a/solution.py
+++ b/solution.py
@@ -1,4 +1,5 @@
 import functools
+import math
 
 import jax
 import jax.numpy as jnp
@@ -15,17 +16,24 @@
 KERNEL_BYTES = 20 << 20
 WIDTH = 256
 STAGES = (1,)
+LATER = 1.15
 AHEAD = 4
 
 
-def message_order(devices):
+def gray_order(count, strips):
+    tiles = [tile ^ (tile >> 1) for tile in range(count // strips)]
+    return [tile * strips + strip for tile in tiles for strip in range(strips)]
+
+
+def message_order(devices, strips):
     half = devices // 2
-    across = [half ^ low for low in range(half)]
-    within = list(range(half // 2, half)) + list(range(1, half // 2))
+    lows = gray_order(half, strips)
+    across = [half ^ low for low in lows]
+    within = [low for low in lows if low >= half // 2] + [k for k in lows if 0 < k < half // 2]
     order, rest = across[:AHEAD], across[AHEAD:]
     done = 0
     for at, k in enumerate(rest):
-        upto = -(-(at + 1) * len(within) // len(rest))
+        upto = math.ceil(len(within) * ((at + 1) / len(rest)) ** LATER)
         order += within[done:upto] + [k]
         done = upto
     return order
@@ -332,7 +340,7 @@
     rows = height // devices
     strips = SUBLANES // rows
     each = count * rows
-    order = message_order(devices)
+    order = message_order(devices, strips)
 
     tiles = list(dict.fromkeys(k // strips for k in order))
     made = {}
@@ -345,7 +353,7 @@
     for k in order:
         arrived[k] = lax.ppermute(made[k], "blk", [(i, i ^ k) for i in range(devices)])
 
-    group = (devices - 1) // strips
+    group = order[-1] // strips
     end = [group * strips + at for at in range(strips)]
     partners = [k for k in [0] + order if k not in end] + end
     middle, tail = devices // 2, devices - strips

time: 75 us -> 73.8 us (0.984)
  starting transfers between devices: 59.2 us -> 55.6 us
  waiting for transfers between devices: 5.43 us -> 7.87 us
    ppermute x31, starting transfers between devices: 59.2 us -> 55.6 us  [local(): lax.ppermute(made[k], 'blk', [(i, i ^ k) for i in range(devices)])]
    ppermute x31, waiting for transfers between devices: 5.43 us -> 7.87 us  [local(): lax.ppermute(made[k], 'blk', [(i, i ^ k) for i in range(devices)])]
  transfers between devices with their start and end apart: 31 -> 31, of which waited for: 3 -> 6; matrix products, arithmetic and copies ran while one was open for 0% -> 0% of each run, Pallas kernels for 10% -> 10%
where the time goes in v4:
time: 73.8 us; the launch traced here: 73.7 us
  starting transfers between devices  55.6 us (75%)
  Pallas kernels  10.1 us (14%)
  waiting for transfers between devices  7.87 us (11%)
    ppermute x31, starting transfers between devices, local(): lax.ppermute(made[k], 'blk', [(i, i ^ k) for i in range(devices)])  55.6 us
    ppermute x31, waiting for transfers between devices, local(): lax.ppermute(made[k], 'blk', [(i, i ^ k) for i in range(devices)])  7.87 us
    pallas_call x2, Pallas kernels, stencil(): pl.pallas_call(functools.partial(stencil_kernel, groups=groups, rows=rows...  4.33 us
    pallas_call x2, Pallas kernels, gather(): pl.pallas_call(functools.partial(gather_kernel if first else write_kernel...  3.44 us
  transfers between devices with their start and end apart: 31, of which 6 were waited for; matrix products, arithmetic and copies ran while one was open for 0% of the time, Pallas kernels for 10%

profile of v4, /device:TPU:0, one launch (start us, length us, event | category | flops | bytes accessed | tf_op | source)
XLA Modules:
  0.0 73.7 jit_solution(13464702815210670409)
XLA Ops:
  0.0 1.4 %stencil.3 = (f32[16,1280]{1,0:T(8,128)S(1)}, f32[16,1280]{1,0:T(8,128)S(1)}) custom-call(f32[3,3]{1,0:T(4,128)} %kernel_ref.3, f32[4,128,1280]{2,1,0:T(8,128)} %frames_ref.3), custom_call_target="tpu_custom_call" | custom-call | flops 819200 | bytes 327680 | tf_op jit(solution)/shard_map/stencil/pallas_call | solution.py:125
  1.4 4.2 %collective-permute-start = (f32[16,1280]{1,0:T(8,128)S(1)}, f32[16,1280]{1,0:T(8,128)S(1)}, u32[]{:S(2)}, u32[]{:S(2)}) collective-permute-start(f32[16,1280]{1,0:T(8,128)S(1)} %get-tuple-element.46), channel_id=1, source_target_pairs={{0,16},{1,17},{2,18},{3,19},{4,20},{5,21},{6,22},{7,23},{8,24},{9,... | collective-permute-start | bytes 245768 | tf_op jit(solution)/shard_map/ppermute | solution.py:354
  5.6 0.0 collective-permute-start.1
  5.6 2.9 %stencil.2 = (f32[16,1280]{1,0:T(8,128)S(1)}, f32[16,1280]{1,0:T(8,128)S(1)}, f32[16,1280]{1,0:T(8,128)S(1)}, f32[16,1280]{1,0:T(8,128)S(1)}, f32[16,1280]{1,0:T...) custom-call(f32[3,3]{1,0:T(4,128)} %kernel_ref.3, ...), custom_call_target="tpu_custom_call" | custom-call | flops 12288000 | bytes 4915200 | tf_op jit(solution)/shard_map/stencil/pallas_call | solution.py:125
  8.5 3.1 %collective-permute-start.2 = (f32[16,1280]{1,0:T(8,128)S(1)}, f32[16,1280]{1,0:T(8,128)S(1)}, u32[]{:S(2)}, u32[]{:S(2)}) collective-permute-start(f32[16,1280]{1,0:T(8,128)S(1)} %get-tuple-element.48), channel_id=1, source_target_pairs={{0,18},{1,19},{2,16},{3,17},{4,22},{5,23},{6,20},{7,21},{8,26},{9,... | collective-permute-start | bytes 245768 | tf_op jit(solution)/shard_map/ppermute | solution.py:354
  11.6 0.6 collective-permute-start.3
  12.2 2.5 %collective-permute-start.4 = (f32[16,1280]{1,0:T(8,128)S(1)}, f32[16,1280]{1,0:T(8,128)S(1)}, u32[]{:S(2)}, u32[]{:S(2)}) collective-permute-start(f32[16,1280]{1,0:T(8,128)S(1)} %get-tuple-element.50), channel_id=1, source_target_pairs={{0,12},{1,13},{2,14},{3,15},{4,8},{5,9},{6,10},{7,11},{8,4},{9,5},... | collective-permute-start | bytes 245768 | tf_op jit(solution)/shard_map/ppermute | solution.py:354
  14.8 0.0 collective-permute-done.refs_1_
  14.8 3.4 %collective-permute-start.5 = (f32[16,1280]{1,0:T(8,128)S(1)}, f32[16,1280]{1,0:T(8,128)S(1)}, u32[]{:S(2)}, u32[]{:S(2)}) collective-permute-start(f32[16,1280]{1,0:T(8,128)S(1)} %get-tuple-element.51), channel_id=1, source_target_pairs={{0,22},{1,23},{2,20},{3,21},{4,18},{5,19},{6,16},{7,17},{8,30},{9,... | collective-permute-start | bytes 245768 | tf_op jit(solution)/shard_map/ppermute | solution.py:354
  18.2 0.0 collective-permute-done.1.refs_2_
  18.2 0.3 collective-permute-start.6
  18.5 1.7 %collective-permute-done.2.refs_3_ = f32[16,1280]{1,0:T(8,128)S(1)} collective-permute-done((f32[16,1280]{1,0:T(8,128)S(1)}, f32[16,1280]{1,0:T(8,128)S(1)}, u32[]{:S(2)}, u32[]{:S(2)}) %collective-permute-start.2) | collective-permute-done | bytes 81952 | tf_op jit(solution)/shard_map/ppermute | solution.py:354
  20.2 2.3 %collective-permute-start.7 = (f32[16,1280]{1,0:T(8,128)S(1)}, f32[16,1280]{1,0:T(8,128)S(1)}, u32[]{:S(2)}, u32[]{:S(2)}) collective-permute-start(f32[16,1280]{1,0:T(8,128)S(1)} %get-tuple-element.53), channel_id=1, source_target_pairs={{0,23},{1,22},{2,21},{3,20},{4,19},{5,18},{6,17},{7,16},{8,31},{9,... | collective-permute-start | bytes 245768 | tf_op jit(solution)/shard_map/ppermute | solution.py:354
  22.5 0.0 collective-permute-done.3.refs_4_
  22.5 4.4 %collective-permute-start.8 = (f32[16,1280]{1,0:T(8,128)S(1)}, f32[16,1280]{1,0:T(8,128)S(1)}, u32[]{:S(2)}, u32[]{:S(2)}) collective-permute-start(f32[16,1280]{1,0:T(8,128)S(1)} %get-tuple-element.54), channel_id=1, source_target_pairs={{0,14},{1,15},{2,12},{3,13},{4,10},{5,11},{6,8},{7,9},{8,6},{9,7},... | collective-permute-start | bytes 245768 | tf_op jit(solution)/shard_map/ppermute | solution.py:354
  26.8 0.0 collective-permute-done.4.refs_5_
  26.8 0.3 collective-permute-start.9
  27.1 1.1 %collective-permute-done.5.refs_6_ = f32[16,1280]{1,0:T(8,128)S(1)} collective-permute-done((f32[16,1280]{1,0:T(8,128)S(1)}, f32[16,1280]{1,0:T(8,128)S(1)}, u32[]{:S(2)}, u32[]{:S(2)}) %collective-permute-start.5) | collective-permute-done | bytes 81952 | tf_op jit(solution)/shard_map/ppermute | solution.py:354
  28.2 0.1 collective-permute-start.10
  28.3 0.0 collective-permute-done.6.refs_7_
  28.3 3.4 %collective-permute-start.11 = (f32[16,1280]{1,0:T(8,128)S(1)}, f32[16,1280]{1,0:T(8,128)S(1)}, u32[]{:S(2)}, u32[]{:S(2)}) collective-permute-start(f32[16,1280]{1,0:T(8,128)S(1)} %get-tuple-element.57), channel_id=1, source_target_pairs={{0,10},{1,11},{2,8},{3,9},{4,14},{5,15},{6,12},{7,13},{8,2},{9,3},... | collective-permute-start | bytes 245768 | tf_op jit(solution)/shard_map/ppermute | solution.py:354
  31.7 0.0 collective-permute-done.7.refs_8_
  31.7 1.5 %collective-permute-start.12 = (f32[16,1280]{1,0:T(8,128)S(1)}, f32[16,1280]{1,0:T(8,128)S(1)}, u32[]{:S(2)}, u32[]{:S(2)}) collective-permute-start(f32[16,1280]{1,0:T(8,128)S(1)} %get-tuple-element.58), channel_id=1, source_target_pairs={{0,21},{1,20},{2,23},{3,22},{4,17},{5,16},{6,19},{7,18},{8,29},{9,... | collective-permute-start | bytes 245768 | tf_op jit(solution)/shard_map/ppermute | solution.py:354
  33.2 0.0 collective-permute-done.8.refs_9_
  33.2 1.5 %collective-permute-start.13 = (f32[16,1280]{1,0:T(8,128)S(1)}, f32[16,1280]{1,0:T(8,128)S(1)}, u32[]{:S(2)}, u32[]{:S(2)}) collective-permute-start(f32[16,1280]{1,0:T(8,128)S(1)} %get-tuple-element.59), channel_id=1, source_target_pairs={{0,11},{1,10},{2,9},{3,8},{4,15},{5,14},{6,13},{7,12},{8,3},{9,2},... | collective-permute-start | bytes 245768 | tf_op jit(solution)/shard_map/ppermute | solution.py:354
  34.7 0.9 %collective-permute-done.9.refs_10_ = f32[16,1280]{1,0:T(8,128)S(1)} collective-permute-done((f32[16,1280]{1,0:T(8,128)S(1)}, f32[16,1280]{1,0:T(8,128)S(1)}, u32[]{:S(2)}, u32[]{:S(2)}) %collective-permute-start.9) | collective-permute-done | bytes 81952 | tf_op jit(solution)/shard_map/ppermute | solution.py:354
  35.6 4.6 %collective-permute-start.14 = (f32[16,1280]{1,0:T(8,128)S(1)}, f32[16,1280]{1,0:T(8,128)S(1)}, u32[]{:S(2)}, u32[]{:S(2)}) collective-permute-start(f32[16,1280]{1,0:T(8,128)S(1)} %get-tuple-element.60), channel_id=1, source_target_pairs={{0,28},{1,29},{2,30},{3,31},{4,24},{5,25},{6,26},{7,27},{8,20},{9,... | collective-permute-start | bytes 245768 | tf_op jit(solution)/shard_map/ppermute | solution.py:354
  40.3 0.0 collective-permute-done.10.refs_11_
  40.3 0.0 collective-permute-start.15
  40.3 0.0 collective-permute-done.11.refs_12_
  40.3 1.1 %collective-permute-start.16 = (f32[16,1280]{1,0:T(8,128)S(1)}, f32[16,1280]{1,0:T(8,128)S(1)}, u32[]{:S(2)}, u32[]{:S(2)}) collective-permute-start(f32[16,1280]{1,0:T(8,128)S(1)} %get-tuple-element.62), channel_id=1, source_target_pairs={{0,29},{1,28},{2,31},{3,30},{4,25},{5,24},{6,27},{7,26},{8,21},{9,... | collective-permute-start | bytes 245768 | tf_op jit(solution)/shard_map/ppermute | solution.py:354
  41.4 0.0 collective-permute-done.12.refs_13_
  41.4 1.5 %collective-permute-start.17 = (f32[16,1280]{1,0:T(8,128)S(1)}, f32[16,1280]{1,0:T(8,128)S(1)}, u32[]{:S(2)}, u32[]{:S(2)}) collective-permute-start(f32[16,1280]{1,0:T(8,128)S(1)} %get-tuple-element.63), channel_id=1, source_target_pairs={{0,9},{1,8},{2,11},{3,10},{4,13},{5,12},{6,15},{7,14},{8,1},{9,0},... | collective-permute-start | bytes 245768 | tf_op jit(solution)/shard_map/ppermute | solution.py:354
  42.8 0.0 collective-permute-done.13.refs_14_
  42.9 0.0 collective-permute-start.18
  42.9 1.9 %collective-permute-done.14.refs_15_ = f32[16,1280]{1,0:T(8,128)S(1)} collective-permute-done((f32[16,1280]{1,0:T(8,128)S(1)}, f32[16,1280]{1,0:T(8,128)S(1)}, u32[]{:S(2)}, u32[]{:S(2)}) %collective-permute-start.14) | collective-permute-done | bytes 81952 | tf_op jit(solution)/shard_map/ppermute | solution.py:354
  44.8 2.6 %collective-permute-start.19 = (f32[16,1280]{1,0:T(8,128)S(1)}, f32[16,1280]{1,0:T(8,128)S(1)}, u32[]{:S(2)}, u32[]{:S(2)}) collective-permute-start(f32[16,1280]{1,0:T(8,128)S(1)} %get-tuple-element.65), channel_id=1, source_target_pairs={{0,30},{1,31},{2,28},{3,29},{4,26},{5,27},{6,24},{7,25},{8,22},{9,... | collective-permute-start | bytes 245768 | tf_op jit(solution)/shard_map/ppermute | solution.py:354
  47.4 0.0 collective-permute-done.15.refs_0_
  47.4 2.0 %collective-permute-start.20 = (f32[16,1280]{1,0:T(8,128)S(1)}, f32[16,1280]{1,0:T(8,128)S(1)}, u32[]{:S(2)}, u32[]{:S(2)}) collective-permute-start(f32[16,1280]{1,0:T(8,128)S(1)} %get-tuple-element.66), channel_id=1, source_target_pairs={{0,2},{1,3},{2,0},{3,1},{4,6},{5,7},{6,4},{7,5},{8,10},{9,11},{10,... | collective-permute-start | bytes 245768 | tf_op jit(solution)/shard_map/ppermute | solution.py:354
  49.4 0.0 collective-permute-done.16.refs_1_
  49.4 1.0 %collective-permute-start.21 = (f32[16,1280]{1,0:T(8,128)S(1)}, f32[16,1280]{1,0:T(8,128)S(1)}, u32[]{:S(2)}, u32[]{:S(2)}) collective-permute-start(f32[16,1280]{1,0:T(8,128)S(1)} %get-tuple-element.67), channel_id=1, source_target_pairs={{0,31},{1,30},{2,29},{3,28},{4,27},{5,26},{6,25},{7,24},{8,23},{9,... | collective-permute-start | bytes 245768 | tf_op jit(solution)/shard_map/ppermute | solution.py:354
  50.3 0.5 collective-permute-done.17.refs_2_
  50.8 2.6 %collective-permute-start.22 = (f32[16,1280]{1,0:T(8,128)S(1)}, f32[16,1280]{1,0:T(8,128)S(1)}, u32[]{:S(2)}, u32[]{:S(2)}) collective-permute-start(f32[16,1280]{1,0:T(8,128)S(1)} %get-tuple-element.68), channel_id=1, source_target_pairs={{0,3},{1,2},{2,1},{3,0},{4,7},{5,6},{6,5},{7,4},{8,11},{9,10},{10,... | collective-permute-start | bytes 245768 | tf_op jit(solution)/shard_map/ppermute | solution.py:354
  53.4 0.0 collective-permute-done.18.refs_3_
  53.4 0.0 collective-permute-start.23
  53.5 1.1 %weights.1 = (bf16[512,512]{1,0:T(8,128)(2,1)S(1)}, bf16[512,512]{1,0:T(8,128)(2,1)S(1)}, bf16[512,96]{1,0:T(8,128)(2,1)S(1)}) custom-call(f32[1,128]{1,0:T(1,128)S(1)} %bitcast.1, s32[1,128]{1,0:T(1,128)S(1)} %copy-done.2), custom_call_target="tpu_custom_call" | custom-call | flops 268435456 | bytes 1048576 | tf_op jit(solution)/shard_map/weights/pallas_call | solution.py:189
  54.6 0.0 collective-permute-done.19.refs_4_
  54.6 3.4 %collective-permute-start.24 = (f32[16,1280]{1,0:T(8,128)S(1)}, f32[16,1280]{1,0:T(8,128)S(1)}, u32[]{:S(2)}, u32[]{:S(2)}) collective-permute-start(f32[16,1280]{1,0:T(8,128)S(1)} %get-tuple-element.70), channel_id=1, source_target_pairs={{0,6},{1,7},{2,4},{3,5},{4,2},{5,3},{6,0},{7,1},{8,14},{9,15},{10,... | collective-permute-start | bytes 245768 | tf_op jit(solution)/shard_map/ppermute | solution.py:354
  57.9 0.0 collective-permute-done.20.refs_5_
  57.9 0.0 collective-permute-start.25
  57.9 0.0 collective-permute-done.21.refs_6_
  58.0 4.1 %collective-permute-start.26 = (f32[16,1280]{1,0:T(8,128)S(1)}, f32[16,1280]{1,0:T(8,128)S(1)}, u32[]{:S(2)}, u32[]{:S(2)}) collective-permute-start(f32[16,1280]{1,0:T(8,128)S(1)} %get-tuple-element.72), channel_id=1, source_target_pairs={{0,27},{1,26},{2,25},{3,24},{4,31},{5,30},{6,29},{7,28},{8,19},{9,... | collective-permute-start | bytes 245768 | tf_op jit(solution)/shard_map/ppermute | solution.py:354
  62.0 0.0 collective-permute-done.22.refs_7_
  62.0 0.0 collective-permute-start.27
  62.0 0.1 collective-permute-start.28
  62.1 1.2 %temporal.2.so_far_ref = f32[512,1280]{1,0:T(8,128)S(1)} custom-call(bf16[512,512]{1,0:T(8,128)(2,1)S(1)} %get-tuple-element.43.high_ref, bf16[512,512]{1,0:T(8,128)(2,1)S(1)} %get-tuple-element.44.low_ref, f32[16,1280]{1,0:T(8,128)S(1)} %get-tuple-element.45.refs_0_, f32[16,1280]{1,0:T(8,128)S(1)} %collective-permute-done.refs_1_, ...), custom_call_target="tpu_custom_call" | custom-call | flops 1006632960 | bytes 5242880 | tf_op jit(solution)/shard_map/temporal/pallas_call | solution.py:263
  63.3 2.4 %collective-permute-start.29 = (f32[16,1280]{1,0:T(8,128)S(1)}, f32[16,1280]{1,0:T(8,128)S(1)}, u32[]{:S(2)}, u32[]{:S(2)}) collective-permute-start(f32[16,1280]{1,0:T(8,128)S(1)} %get-tuple-element.77), channel_id=1, source_target_pairs={{0,24},{1,25},{2,26},{3,27},{4,28},{5,29},{6,30},{7,31},{8,16},{9,... | collective-permute-start | bytes 245768 | tf_op jit(solution)/shard_map/ppermute | solution.py:354
  65.7 0.0 collective-permute-done.25.refs_10_
  65.7 2.9 %collective-permute-start.30 = (f32[16,1280]{1,0:T(8,128)S(1)}, f32[16,1280]{1,0:T(8,128)S(1)}, u32[]{:S(2)}, u32[]{:S(2)}) collective-permute-start(f32[16,1280]{1,0:T(8,128)S(1)} %get-tuple-element.78), channel_id=1, source_target_pairs={{0,25},{1,24},{2,27},{3,26},{4,29},{5,28},{6,31},{7,30},{8,17},{9,... | collective-permute-start | bytes 245768 | tf_op jit(solution)/shard_map/ppermute | solution.py:354
  68.6 0.0 collective-permute-done.27.refs_12_
  68.6 0.0 collective-permute-done.28.refs_13_
  68.6 2.2 %temporal.3 = (f32[512,1280]{1,0:T(8,128)S(1)}, f32[128,4,1280]{2,1,0:T(4,128)}) custom-call(bf16[512,512]{1,0:T(8,128)(2,1)S(1)} %get-tuple-element.43.high_ref, bf16[512,512]{1,0:T(8,128)(2,1)S(1)} %get-tuple-element.44.low_ref, f32[512,1280]{1,0:T(8,128)S(1)} %temporal.2.so_far_ref, f32[16,1280]{1,0:T(8,128)S(1)} %collective-permute-done.15.refs_0_, ...), custom_call_target="tpu_custom_call" | custom-call | flops 880803840 | bytes 5242880 | tf_op jit(solution)/shard_map/temporal/pallas_call | solution.py:263
  70.9 1.6 %collective-permute-done.30.refs_1_ = f32[16,1280]{1,0:T(8,128)S(1)} collective-permute-done((f32[16,1280]{1,0:T(8,128)S(1)}, f32[16,1280]{1,0:T(8,128)S(1)}, u32[]{:S(2)}, u32[]{:S(2)}) %collective-permute-start.30) | collective-permute-done | bytes 81952 | tf_op jit(solution)/shard_map/ppermute | solution.py:354
  72.5 1.2 %finish.1 = f32[128,4,1280]{2,1,0:T(4,128)} custom-call(bf16[512,96]{1,0:T(8,128)(2,1)S(1)} %get-tuple-element.42.weights_ref, f32[512,1280]{1,0:T(8,128)S(1)} %get-tuple-element.75.so_far_ref, f32[128,4,1280]{2,1,0:T(4,128)} %get-tuple-element.76._, f32[16,1280]{1,0:T(8,128)S(1)} %collective-permute-done.29.refs_0_, ...), custom_call_target="tpu_custom_call", output_to_operand_aliasing={{}: (2, {})} | custom-call | flops 55050240 | bytes 2293760 | tf_op jit(solution)/shard_map/finish/pallas_call | solution.py:318
  (10 shorter events, 0.0 us)
Async XLA Ops:
  0.0 53.4 %copy-start.2 = (s32[1,128]{1,0:T(1,128)S(1)}, s32[1,128]{1,0:T(1,128)}, u32[]{:S(2)}) copy-start(s32[1,128]{1,0:T(1,128)} %constant.2.clone.partner_ref) | copy-start | bytes 1540
  0.0 5.6 %copy-start = (f32[4,128,1280]{2,1,0:T(8,128)S(1)}, f32[4,128,1280]{2,1,0:T(8,128)}, u32[]{:S(2)}) copy-start(f32[4,128,1280]{2,1,0:T(8,128)} %frames_ref.3) | copy-start | bytes 7864324
  0.0 53.4 %copy-start.1 = (f32[128]{0:T(128)S(1)}, f32[128]{0:T(128)}, u32[]{:S(2)}) copy-start(f32[128]{0:T(128)} %param.5) | copy-start | bytes 1540
  1.4 13.3 %collective-permute-start = (f32[16,1280]{1,0:T(8,128)S(1)}, f32[16,1280]{1,0:T(8,128)S(1)}, u32[]{:S(2)}, u32[]{:S(2)}) collective-permute-start(f32[16,1280]{1,0:T(8,128)S(1)} %get-tuple-element.46), channel_id=1, source_target_pairs={{0,16},{1,17},{2,18},{3,19},{4,20},{5,21},{6,22},{7,23},{8,24},{9,... | collective-permute-start | bytes 245768 | tf_op jit(solution)/shard_map/ppermute | solution.py:354
  5.6 12.6 %collective-permute-start.1 = (f32[16,1280]{1,0:T(8,128)S(1)}, f32[16,1280]{1,0:T(8,128)S(1)}, u32[]{:S(2)}, u32[]{:S(2)}) collective-permute-start(f32[16,1280]{1,0:T(8,128)S(1)} %get-tuple-element.47), channel_id=1, source_target_pairs={{0,17},{1,16},{2,19},{3,18},{4,21},{5,20},{6,23},{7,22},{8,25},{9,... | collective-permute-start | bytes 245768 | tf_op jit(solution)/shard_map/ppermute | solution.py:354
  8.5 11.7 %collective-permute-start.2 = (f32[16,1280]{1,0:T(8,128)S(1)}, f32[16,1280]{1,0:T(8,128)S(1)}, u32[]{:S(2)}, u32[]{:S(2)}) collective-permute-start(f32[16,1280]{1,0:T(8,128)S(1)} %get-tuple-element.48), channel_id=1, source_target_pairs={{0,18},{1,19},{2,16},{3,17},{4,22},{5,23},{6,20},{7,21},{8,26},{9,... | collective-permute-start | bytes 245768 | tf_op jit(solution)/shard_map/ppermute | solution.py:354
  11.6 10.9 %collective-permute-start.3 = (f32[16,1280]{1,0:T(8,128)S(1)}, f32[16,1280]{1,0:T(8,128)S(1)}, u32[]{:S(2)}, u32[]{:S(2)}) collective-permute-start(f32[16,1280]{1,0:T(8,128)S(1)} %get-tuple-element.49), channel_id=1, source_target_pairs={{0,19},{1,18},{2,17},{3,16},{4,23},{5,22},{6,21},{7,20},{8,27},{9,... | collective-permute-start | bytes 245768 | tf_op jit(solution)/shard_map/ppermute | solution.py:354
  12.2 14.6 %collective-permute-start.4 = (f32[16,1280]{1,0:T(8,128)S(1)}, f32[16,1280]{1,0:T(8,128)S(1)}, u32[]{:S(2)}, u32[]{:S(2)}) collective-permute-start(f32[16,1280]{1,0:T(8,128)S(1)} %get-tuple-element.50), channel_id=1, source_target_pairs={{0,12},{1,13},{2,14},{3,15},{4,8},{5,9},{6,10},{7,11},{8,4},{9,5},... | collective-permute-start | bytes 245768 | tf_op jit(solution)/shard_map/ppermute | solution.py:354
  14.8 13.5 %collective-permute-start.5 = (f32[16,1280]{1,0:T(8,128)S(1)}, f32[16,1280]{1,0:T(8,128)S(1)}, u32[]{:S(2)}, u32[]{:S(2)}) collective-permute-start(f32[16,1280]{1,0:T(8,128)S(1)} %get-tuple-element.51), channel_id=1, source_target_pairs={{0,22},{1,23},{2,20},{3,21},{4,18},{5,19},{6,16},{7,17},{8,30},{9,... | collective-permute-start | bytes 245768 | tf_op jit(solution)/shard_map/ppermute | solution.py:354
  18.2 10.1 %collective-permute-start.6 = (f32[16,1280]{1,0:T(8,128)S(1)}, f32[16,1280]{1,0:T(8,128)S(1)}, u32[]{:S(2)}, u32[]{:S(2)}) collective-permute-start(f32[16,1280]{1,0:T(8,128)S(1)} %get-tuple-element.52), channel_id=1, source_target_pairs={{0,13},{1,12},{2,15},{3,14},{4,9},{5,8},{6,11},{7,10},{8,5},{9,4},... | collective-permute-start | bytes 245768 | tf_op jit(solution)/shard_map/ppermute | solution.py:354
  20.2 11.5 %collective-permute-start.7 = (f32[16,1280]{1,0:T(8,128)S(1)}, f32[16,1280]{1,0:T(8,128)S(1)}, u32[]{:S(2)}, u32[]{:S(2)}) collective-permute-start(f32[16,1280]{1,0:T(8,128)S(1)} %get-tuple-element.53), channel_id=1, source_target_pairs={{0,23},{1,22},{2,21},{3,20},{4,19},{5,18},{6,17},{7,16},{8,31},{9,... | collective-permute-start | bytes 245768 | tf_op jit(solution)/shard_map/ppermute | solution.py:354
  22.5 10.7 %collective-permute-start.8 = (f32[16,1280]{1,0:T(8,128)S(1)}, f32[16,1280]{1,0:T(8,128)S(1)}, u32[]{:S(2)}, u32[]{:S(2)}) collective-permute-start(f32[16,1280]{1,0:T(8,128)S(1)} %get-tuple-element.54), channel_id=1, source_target_pairs={{0,14},{1,15},{2,12},{3,13},{4,10},{5,11},{6,8},{7,9},{8,6},{9,7},... | collective-permute-start | bytes 245768 | tf_op jit(solution)/shard_map/ppermute | solution.py:354
  26.8 8.8 %collective-permute-start.9 = (f32[16,1280]{1,0:T(8,128)S(1)}, f32[16,1280]{1,0:T(8,128)S(1)}, u32[]{:S(2)}, u32[]{:S(2)}) collective-permute-start(f32[16,1280]{1,0:T(8,128)S(1)} %get-tuple-element.55), channel_id=1, source_target_pairs={{0,15},{1,14},{2,13},{3,12},{4,11},{5,10},{6,9},{7,8},{8,7},{9,6},... | collective-permute-start | bytes 245768 | tf_op jit(solution)/shard_map/ppermute | solution.py:354
  28.2 12.0 %collective-permute-start.10 = (f32[16,1280]{1,0:T(8,128)S(1)}, f32[16,1280]{1,0:T(8,128)S(1)}, u32[]{:S(2)}, u32[]{:S(2)}) collective-permute-start(f32[16,1280]{1,0:T(8,128)S(1)} %get-tuple-element.56), channel_id=1, source_target_pairs={{0,20},{1,21},{2,22},{3,23},{4,16},{5,17},{6,18},{7,19},{8,28},{9,... | collective-permute-start | bytes 245768 | tf_op jit(solution)/shard_map/ppermute | solution.py:354
  28.3 12.0 %collective-permute-start.11 = (f32[16,1280]{1,0:T(8,128)S(1)}, f32[16,1280]{1,0:T(8,128)S(1)}, u32[]{:S(2)}, u32[]{:S(2)}) collective-permute-start(f32[16,1280]{1,0:T(8,128)S(1)} %get-tuple-element.57), channel_id=1, source_target_pairs={{0,10},{1,11},{2,8},{3,9},{4,14},{5,15},{6,12},{7,13},{8,2},{9,3},... | collective-permute-start | bytes 245768 | tf_op jit(solution)/shard_map/ppermute | solution.py:354
  31.7 9.7 %collective-permute-start.12 = (f32[16,1280]{1,0:T(8,128)S(1)}, f32[16,1280]{1,0:T(8,128)S(1)}, u32[]{:S(2)}, u32[]{:S(2)}) collective-permute-start(f32[16,1280]{1,0:T(8,128)S(1)} %get-tuple-element.58), channel_id=1, source_target_pairs={{0,21},{1,20},{2,23},{3,22},{4,17},{5,16},{6,19},{7,18},{8,29},{9,... | collective-permute-start | bytes 245768 | tf_op jit(solution)/shard_map/ppermute | solution.py:354
  33.2 9.7 %collective-permute-start.13 = (f32[16,1280]{1,0:T(8,128)S(1)}, f32[16,1280]{1,0:T(8,128)S(1)}, u32[]{:S(2)}, u32[]{:S(2)}) collective-permute-start(f32[16,1280]{1,0:T(8,128)S(1)} %get-tuple-element.59), channel_id=1, source_target_pairs={{0,11},{1,10},{2,9},{3,8},{4,15},{5,14},{6,13},{7,12},{8,3},{9,2},... | collective-permute-start | bytes 245768 | tf_op jit(solution)/shard_map/ppermute | solution.py:354
  35.6 9.1 %collective-permute-start.14 = (f32[16,1280]{1,0:T(8,128)S(1)}, f32[16,1280]{1,0:T(8,128)S(1)}, u32[]{:S(2)}, u32[]{:S(2)}) collective-permute-start(f32[16,1280]{1,0:T(8,128)S(1)} %get-tuple-element.60), channel_id=1, source_target_pairs={{0,28},{1,29},{2,30},{3,31},{4,24},{5,25},{6,26},{7,27},{8,20},{9,... | collective-permute-start | bytes 245768 | tf_op jit(solution)/shard_map/ppermute | solution.py:354
  40.3 7.2 %collective-permute-start.15 = (f32[16,1280]{1,0:T(8,128)S(1)}, f32[16,1280]{1,0:T(8,128)S(1)}, u32[]{:S(2)}, u32[]{:S(2)}) collective-permute-start(f32[16,1280]{1,0:T(8,128)S(1)} %get-tuple-element.61), channel_id=1, source_target_pairs={{0,8},{1,9},{2,10},{3,11},{4,12},{5,13},{6,14},{7,15},{8,0},{9,1},... | collective-permute-start | bytes 245768 | tf_op jit(solution)/shard_map/ppermute | solution.py:354
  40.3 9.1 %collective-permute-start.16 = (f32[16,1280]{1,0:T(8,128)S(1)}, f32[16,1280]{1,0:T(8,128)S(1)}, u32[]{:S(2)}, u32[]{:S(2)}) collective-permute-start(f32[16,1280]{1,0:T(8,128)S(1)} %get-tuple-element.62), channel_id=1, source_target_pairs={{0,29},{1,28},{2,31},{3,30},{4,25},{5,24},{6,27},{7,26},{8,21},{9,... | collective-permute-start | bytes 245768 | tf_op jit(solution)/shard_map/ppermute | solution.py:354
  41.4 9.5 %collective-permute-start.17 = (f32[16,1280]{1,0:T(8,128)S(1)}, f32[16,1280]{1,0:T(8,128)S(1)}, u32[]{:S(2)}, u32[]{:S(2)}) collective-permute-start(f32[16,1280]{1,0:T(8,128)S(1)} %get-tuple-element.63), channel_id=1, source_target_pairs={{0,9},{1,8},{2,11},{3,10},{4,13},{5,12},{6,15},{7,14},{8,1},{9,0},... | collective-permute-start | bytes 245768 | tf_op jit(solution)/shard_map/ppermute | solution.py:354
  42.9 10.6 %collective-permute-start.18 = (f32[16,1280]{1,0:T(8,128)S(1)}, f32[16,1280]{1,0:T(8,128)S(1)}, u32[]{:S(2)}, u32[]{:S(2)}) collective-permute-start(f32[16,1280]{1,0:T(8,128)S(1)} %get-tuple-element.64), channel_id=1, source_target_pairs={{0,1},{1,0},{2,3},{3,2},{4,5},{5,4},{6,7},{7,6},{8,9},{9,8},{10,11... | collective-permute-start | bytes 245768 | tf_op jit(solution)/shard_map/ppermute | solution.py:354
  44.8 9.8 %collective-permute-start.19 = (f32[16,1280]{1,0:T(8,128)S(1)}, f32[16,1280]{1,0:T(8,128)S(1)}, u32[]{:S(2)}, u32[]{:S(2)}) collective-permute-start(f32[16,1280]{1,0:T(8,128)S(1)} %get-tuple-element.65), channel_id=1, source_target_pairs={{0,30},{1,31},{2,28},{3,29},{4,26},{5,27},{6,24},{7,25},{8,22},{9,... | collective-permute-start | bytes 245768 | tf_op jit(solution)/shard_map/ppermute | solution.py:354
  47.4 10.5 %collective-permute-start.20 = (f32[16,1280]{1,0:T(8,128)S(1)}, f32[16,1280]{1,0:T(8,128)S(1)}, u32[]{:S(2)}, u32[]{:S(2)}) collective-permute-start(f32[16,1280]{1,0:T(8,128)S(1)} %get-tuple-element.66), channel_id=1, source_target_pairs={{0,2},{1,3},{2,0},{3,1},{4,6},{5,7},{6,4},{7,5},{8,10},{9,11},{10,... | collective-permute-start | bytes 245768 | tf_op jit(solution)/shard_map/ppermute | solution.py:354
  49.4 8.6 %collective-permute-start.21 = (f32[16,1280]{1,0:T(8,128)S(1)}, f32[16,1280]{1,0:T(8,128)S(1)}, u32[]{:S(2)}, u32[]{:S(2)}) collective-permute-start(f32[16,1280]{1,0:T(8,128)S(1)} %get-tuple-element.67), channel_id=1, source_target_pairs={{0,31},{1,30},{2,29},{3,28},{4,27},{5,26},{6,25},{7,24},{8,23},{9,... | collective-permute-start | bytes 245768 | tf_op jit(solution)/shard_map/ppermute | solution.py:354
  50.8 11.2 %collective-permute-start.22 = (f32[16,1280]{1,0:T(8,128)S(1)}, f32[16,1280]{1,0:T(8,128)S(1)}, u32[]{:S(2)}, u32[]{:S(2)}) collective-permute-start(f32[16,1280]{1,0:T(8,128)S(1)} %get-tuple-element.68), channel_id=1, source_target_pairs={{0,3},{1,2},{2,1},{3,0},{4,7},{5,6},{6,5},{7,4},{8,11},{9,10},{10,... | collective-permute-start | bytes 245768 | tf_op jit(solution)/shard_map/ppermute | solution.py:354
  53.4 8.6 %collective-permute-start.23 = (f32[16,1280]{1,0:T(8,128)S(1)}, f32[16,1280]{1,0:T(8,128)S(1)}, u32[]{:S(2)}, u32[]{:S(2)}) collective-permute-start(f32[16,1280]{1,0:T(8,128)S(1)} %get-tuple-element.69), channel_id=1, source_target_pairs={{0,26},{1,27},{2,24},{3,25},{4,30},{5,31},{6,28},{7,29},{8,18},{9,... | collective-permute-start | bytes 245768 | tf_op jit(solution)/shard_map/ppermute | solution.py:354
  54.6 8.7 %collective-permute-start.24 = (f32[16,1280]{1,0:T(8,128)S(1)}, f32[16,1280]{1,0:T(8,128)S(1)}, u32[]{:S(2)}, u32[]{:S(2)}) collective-permute-start(f32[16,1280]{1,0:T(8,128)S(1)} %get-tuple-element.70), channel_id=1, source_target_pairs={{0,6},{1,7},{2,4},{3,5},{4,2},{5,3},{6,0},{7,1},{8,14},{9,15},{10,... | collective-permute-start | bytes 245768 | tf_op jit(solution)/shard_map/ppermute | solution.py:354
  57.9 7.8 %collective-permute-start.25 = (f32[16,1280]{1,0:T(8,128)S(1)}, f32[16,1280]{1,0:T(8,128)S(1)}, u32[]{:S(2)}, u32[]{:S(2)}) collective-permute-start(f32[16,1280]{1,0:T(8,128)S(1)} %get-tuple-element.71), channel_id=1, source_target_pairs={{0,7},{1,6},{2,5},{3,4},{4,3},{5,2},{6,1},{7,0},{8,15},{9,14},{10,... | collective-permute-start | bytes 245768 | tf_op jit(solution)/shard_map/ppermute | solution.py:354
  58.0 10.6 %collective-permute-start.26 = (f32[16,1280]{1,0:T(8,128)S(1)}, f32[16,1280]{1,0:T(8,128)S(1)}, u32[]{:S(2)}, u32[]{:S(2)}) collective-permute-start(f32[16,1280]{1,0:T(8,128)S(1)} %get-tuple-element.72), channel_id=1, source_target_pairs={{0,27},{1,26},{2,25},{3,24},{4,31},{5,30},{6,29},{7,28},{8,19},{9,... | collective-permute-start | bytes 245768 | tf_op jit(solution)/shard_map/ppermute | solution.py:354
  62.0 6.6 %collective-permute-start.27 = (f32[16,1280]{1,0:T(8,128)S(1)}, f32[16,1280]{1,0:T(8,128)S(1)}, u32[]{:S(2)}, u32[]{:S(2)}) collective-permute-start(f32[16,1280]{1,0:T(8,128)S(1)} %get-tuple-element.73), channel_id=1, source_target_pairs={{0,4},{1,5},{2,6},{3,7},{4,0},{5,1},{6,2},{7,3},{8,12},{9,13},{10,... | collective-permute-start | bytes 245768 | tf_op jit(solution)/shard_map/ppermute | solution.py:354
  62.0 6.6 %collective-permute-start.28 = (f32[16,1280]{1,0:T(8,128)S(1)}, f32[16,1280]{1,0:T(8,128)S(1)}, u32[]{:S(2)}, u32[]{:S(2)}) collective-permute-start(f32[16,1280]{1,0:T(8,128)S(1)} %get-tuple-element.74), channel_id=1, source_target_pairs={{0,5},{1,4},{2,7},{3,6},{4,1},{5,0},{6,3},{7,2},{8,13},{9,12},{10,... | collective-permute-start | bytes 245768 | tf_op jit(solution)/shard_map/ppermute | solution.py:354
  63.3 7.5 %collective-permute-start.29 = (f32[16,1280]{1,0:T(8,128)S(1)}, f32[16,1280]{1,0:T(8,128)S(1)}, u32[]{:S(2)}, u32[]{:S(2)}) collective-permute-start(f32[16,1280]{1,0:T(8,128)S(1)} %get-tuple-element.77), channel_id=1, source_target_pairs={{0,24},{1,25},{2,26},{3,27},{4,28},{5,29},{6,30},{7,31},{8,16},{9,... | collective-permute-start | bytes 245768 | tf_op jit(solution)/shard_map/ppermute | solution.py:354
  65.7 6.8 %collective-permute-start.30 = (f32[16,1280]{1,0:T(8,128)S(1)}, f32[16,1280]{1,0:T(8,128)S(1)}, u32[]{:S(2)}, u32[]{:S(2)}) collective-permute-start(f32[16,1280]{1,0:T(8,128)S(1)} %get-tuple-element.78), channel_id=1, source_target_pairs={{0,25},{1,24},{2,27},{3,26},{4,29},{5,28},{6,31},{7,30},{8,17},{9,... | collective-permute-start | bytes 245768 | tf_op jit(solution)/shard_map/ppermute | solution.py:354

commit v5 on v4

--- a/solution.py
+++ b/solution.py
@@ -16,7 +16,7 @@
 KERNEL_BYTES = 20 << 20
 WIDTH = 256
 STAGES = (1,)
-LATER = 1.15
+LATER = 1.25
 AHEAD = 4
 
 
@@ -65,9 +65,11 @@
     return value
 
 
-def tile_rows(tile, tiles):
+def tile_rows(tile, tiles, base=0):
     spots = (jnp.maximum(tile - 1, 0), tile, jnp.minimum(tile + 1, tiles - 1))
-    return [pl.ds(pl.multiple_of(spot * SUBLANES, SUBLANES), SUBLANES) for spot in spots]
+    return [
+        pl.ds(pl.multiple_of((spot - base) * SUBLANES, SUBLANES), SUBLANES) for spot in spots
+    ]
 
 
 def stencil_kernel(kernel_ref, frames_ref, *refs, groups, rows, direct):
@@ -83,24 +85,24 @@
     copies = []
     if direct:
         near_ref, near_sem = near
-        for place, parts in enumerate(spans):
-            for part, span in enumerate(parts):
-                copies.append(
-                    pltpu.make_async_copy(
-                        frames_ref.at[:, span, :],
-                        near_ref.at[place, part],
-                        near_sem.at[place, part],
-                    )
+        base = [jnp.clip(tile - 1, 0, tiles - 3) for tile in chosen]
+        for place, first in enumerate(base):
+            span = pl.ds(pl.multiple_of(first * SUBLANES, SUBLANES), 3 * SUBLANES)
+            copies.append(
+                pltpu.make_async_copy(
+                    frames_ref.at[:, span, :], near_ref.at[place], near_sem.at[place]
                 )
-                copies[-1].start()
+            )
+            copies[-1].start()
     tap_copy.wait()
     tap = [[tap_ref[a, b] for b in range(3)] for a in range(3)]
     for place, tile in enumerate(chosen):
-        for copy in copies[3 * place : 3 * place + 3]:
+        for copy in copies[place : place + 1]:
             copy.wait()
         for frame in range(count):
             if direct:
-                parts = [near_ref[place, part, frame] for part in range(3)]
+                at = tile_rows(tile, tiles, base[place])
+                parts = [near_ref[place, frame, span, :] for span in at]
             else:
                 parts = [frames_ref[frame, span, :] for span in spans[place]]
             value = filter_tile(me, tap, *parts, tile, tiles, rows)
@@ -120,8 +122,8 @@
     total = 4 * outs * count * rows * columns
     scratch = [SMEM(kernel.shape, jnp.float32), pltpu.SemaphoreType.DMA]
     if direct:
-        near = (len(groups), 3, count, SUBLANES, columns)
-        scratch += [VMEM(near, jnp.float32), pltpu.SemaphoreType.DMA(near[:2])]
+        near = (len(groups), count, 3 * SUBLANES, columns)
+        scratch += [VMEM(near, jnp.float32), pltpu.SemaphoreType.DMA(near[:1])]
     return pl.pallas_call(
         functools.partial(stencil_kernel, groups=groups, rows=rows, direct=direct),
         in_specs=[

time: 73.8 us -> 72.1 us (0.977)
  starting transfers between devices: 55.6 us -> 54.2 us
    ppermute x31, starting transfers between devices: 55.6 us -> 54.2 us  [local(): lax.ppermute(made[k], 'blk', [(i, i ^ k) for i in range(devices)])]
  transfers between devices with their start and end apart: 31 -> 31, of which waited for: 6 -> 8; matrix products, arithmetic and copies ran while one was open for 0% -> 0% of each run, Pallas kernels for 10% -> 10%
where the time goes in v5:
time: 72.1 us; the launch traced here: 71.8 us
  starting transfers between devices  54.2 us (75%)
  Pallas kernels  10 us (14%)
  waiting for transfers between devices  7.4 us (10%)
    ppermute x31, starting transfers between devices, local(): lax.ppermute(made[k], 'blk', [(i, i ^ k) for i in range(devices)])  54.2 us
    ppermute x31, waiting for transfers between devices, local(): lax.ppermute(made[k], 'blk', [(i, i ^ k) for i in range(devices)])  7.4 us
    pallas_call x2, Pallas kernels, stencil(): pl.pallas_call(functools.partial(stencil_kernel, groups=groups, rows=rows...  4.28 us
    pallas_call x2, Pallas kernels, gather(): pl.pallas_call(functools.partial(gather_kernel if first else write_kernel...  3.43 us
  transfers between devices with their start and end apart: 31, of which 8 were waited for; matrix products, arithmetic and copies ran while one was open for 0% of the time, Pallas kernels for 10%

profile of v5, /device:TPU:0, one launch (start us, length us, event | category | flops | bytes accessed | tf_op | source)
XLA Modules:
  0.0 71.8 jit_solution(14963551659320275031)
XLA Ops:
  0.0 1.4 %stencil.3 = (f32[16,1280]{1,0:T(8,128)S(1)}, f32[16,1280]{1,0:T(8,128)S(1)}) custom-call(f32[3,3]{1,0:T(4,128)} %kernel_ref.3, f32[4,128,1280]{2,1,0:T(8,128)} %frames_ref.3), custom_call_target="tpu_custom_call" | custom-call | flops 819200 | bytes 327680 | tf_op jit(solution)/shard_map/stencil/pallas_call | solution.py:127
  1.4 4.2 %collective-permute-start = (f32[16,1280]{1,0:T(8,128)S(1)}, f32[16,1280]{1,0:T(8,128)S(1)}, u32[]{:S(2)}, u32[]{:S(2)}) collective-permute-start(f32[16,1280]{1,0:T(8,128)S(1)} %get-tuple-element.46), channel_id=1, source_target_pairs={{0,16},{1,17},{2,18},{3,19},{4,20},{5,21},{6,22},{7,23},{8,24},{9,... | collective-permute-start | bytes 245768 | tf_op jit(solution)/shard_map/ppermute | solution.py:356
  5.5 0.0 collective-permute-start.1
  5.5 2.9 %stencil.2 = (f32[16,1280]{1,0:T(8,128)S(1)}, f32[16,1280]{1,0:T(8,128)S(1)}, f32[16,1280]{1,0:T(8,128)S(1)}, f32[16,1280]{1,0:T(8,128)S(1)}, f32[16,1280]{1,0:T...) custom-call(f32[3,3]{1,0:T(4,128)} %kernel_ref.3, ...), custom_call_target="tpu_custom_call" | custom-call | flops 12288000 | bytes 4915200 | tf_op jit(solution)/shard_map/stencil/pallas_call | solution.py:127
  8.5 3.1 %collective-permute-start.2 = (f32[16,1280]{1,0:T(8,128)S(1)}, f32[16,1280]{1,0:T(8,128)S(1)}, u32[]{:S(2)}, u32[]{:S(2)}) collective-permute-start(f32[16,1280]{1,0:T(8,128)S(1)} %get-tuple-element.48), channel_id=1, source_target_pairs={{0,18},{1,19},{2,16},{3,17},{4,22},{5,23},{6,20},{7,21},{8,26},{9,... | collective-permute-start | bytes 245768 | tf_op jit(solution)/shard_map/ppermute | solution.py:356
  11.5 0.6 collective-permute-start.3
  12.2 2.5 %collective-permute-start.4 = (f32[16,1280]{1,0:T(8,128)S(1)}, f32[16,1280]{1,0:T(8,128)S(1)}, u32[]{:S(2)}, u32[]{:S(2)}) collective-permute-start(f32[16,1280]{1,0:T(8,128)S(1)} %get-tuple-element.50), channel_id=1, source_target_pairs={{0,12},{1,13},{2,14},{3,15},{4,8},{5,9},{6,10},{7,11},{8,4},{9,5},... | collective-permute-start | bytes 245768 | tf_op jit(solution)/shard_map/ppermute | solution.py:356
  14.7 0.0 collective-permute-done.refs_1_
  14.7 3.4 %collective-permute-start.5 = (f32[16,1280]{1,0:T(8,128)S(1)}, f32[16,1280]{1,0:T(8,128)S(1)}, u32[]{:S(2)}, u32[]{:S(2)}) collective-permute-start(f32[16,1280]{1,0:T(8,128)S(1)} %get-tuple-element.51), channel_id=1, source_target_pairs={{0,22},{1,23},{2,20},{3,21},{4,18},{5,19},{6,16},{7,17},{8,30},{9,... | collective-permute-start | bytes 245768 | tf_op jit(solution)/shard_map/ppermute | solution.py:356
  18.1 0.0 collective-permute-done.1.refs_2_
  18.1 0.3 collective-permute-start.6
  18.4 1.7 %collective-permute-done.2.refs_3_ = f32[16,1280]{1,0:T(8,128)S(1)} collective-permute-done((f32[16,1280]{1,0:T(8,128)S(1)}, f32[16,1280]{1,0:T(8,128)S(1)}, u32[]{:S(2)}, u32[]{:S(2)}) %collective-permute-start.2) | collective-permute-done | bytes 81952 | tf_op jit(solution)/shard_map/ppermute | solution.py:356
  20.1 2.3 %collective-permute-start.7 = (f32[16,1280]{1,0:T(8,128)S(1)}, f32[16,1280]{1,0:T(8,128)S(1)}, u32[]{:S(2)}, u32[]{:S(2)}) collective-permute-start(f32[16,1280]{1,0:T(8,128)S(1)} %get-tuple-element.53), channel_id=1, source_target_pairs={{0,23},{1,22},{2,21},{3,20},{4,19},{5,18},{6,17},{7,16},{8,31},{9,... | collective-permute-start | bytes 245768 | tf_op jit(solution)/shard_map/ppermute | solution.py:356
  22.4 0.0 collective-permute-done.3.refs_4_
  22.4 4.4 %collective-permute-start.8 = (f32[16,1280]{1,0:T(8,128)S(1)}, f32[16,1280]{1,0:T(8,128)S(1)}, u32[]{:S(2)}, u32[]{:S(2)}) collective-permute-start(f32[16,1280]{1,0:T(8,128)S(1)} %get-tuple-element.54), channel_id=1, source_target_pairs={{0,14},{1,15},{2,12},{3,13},{4,10},{5,11},{6,8},{7,9},{8,6},{9,7},... | collective-permute-start | bytes 245768 | tf_op jit(solution)/shard_map/ppermute | solution.py:356
  26.8 0.0 collective-permute-done.4.refs_5_
  26.8 1.4 %collective-permute-start.9 = (f32[16,1280]{1,0:T(8,128)S(1)}, f32[16,1280]{1,0:T(8,128)S(1)}, u32[]{:S(2)}, u32[]{:S(2)}) collective-permute-start(f32[16,1280]{1,0:T(8,128)S(1)} %get-tuple-element.55), channel_id=1, source_target_pairs={{0,20},{1,21},{2,22},{3,23},{4,16},{5,17},{6,18},{7,19},{8,28},{9,... | collective-permute-start | bytes 245768 | tf_op jit(solution)/shard_map/ppermute | solution.py:356
  28.2 0.0 collective-permute-done.5.refs_6_
  28.2 0.0 collective-permute-start.10
  28.2 0.0 collective-permute-done.6.refs_7_
  28.2 4.0 %collective-permute-start.11 = (f32[16,1280]{1,0:T(8,128)S(1)}, f32[16,1280]{1,0:T(8,128)S(1)}, u32[]{:S(2)}, u32[]{:S(2)}) collective-permute-start(f32[16,1280]{1,0:T(8,128)S(1)} %get-tuple-element.57), channel_id=1, source_target_pairs={{0,21},{1,20},{2,23},{3,22},{4,17},{5,16},{6,19},{7,18},{8,29},{9,... | collective-permute-start | bytes 245768 | tf_op jit(solution)/shard_map/ppermute | solution.py:356
  32.2 0.0 collective-permute-done.7.refs_8_
  32.2 3.6 %collective-permute-start.12 = (f32[16,1280]{1,0:T(8,128)S(1)}, f32[16,1280]{1,0:T(8,128)S(1)}, u32[]{:S(2)}, u32[]{:S(2)}) collective-permute-start(f32[16,1280]{1,0:T(8,128)S(1)} %get-tuple-element.58), channel_id=1, source_target_pairs={{0,10},{1,11},{2,8},{3,9},{4,14},{5,15},{6,12},{7,13},{8,2},{9,3},... | collective-permute-start | bytes 245768 | tf_op jit(solution)/shard_map/ppermute | solution.py:356
  35.8 0.3 collective-permute-start.13
  36.1 0.4 collective-permute-done.9.refs_10_
  36.5 2.1 %collective-permute-start.14 = (f32[16,1280]{1,0:T(8,128)S(1)}, f32[16,1280]{1,0:T(8,128)S(1)}, u32[]{:S(2)}, u32[]{:S(2)}) collective-permute-start(f32[16,1280]{1,0:T(8,128)S(1)} %get-tuple-element.60), channel_id=1, source_target_pairs={{0,28},{1,29},{2,30},{3,31},{4,24},{5,25},{6,26},{7,27},{8,20},{9,... | collective-permute-start | bytes 245768 | tf_op jit(solution)/shard_map/ppermute | solution.py:356
  38.5 0.0 collective-permute-done.10.refs_11_
  38.5 0.0 collective-permute-start.15
  38.5 0.0 collective-permute-done.11.refs_12_
  38.6 2.4 %collective-permute-start.16 = (f32[16,1280]{1,0:T(8,128)S(1)}, f32[16,1280]{1,0:T(8,128)S(1)}, u32[]{:S(2)}, u32[]{:S(2)}) collective-permute-start(f32[16,1280]{1,0:T(8,128)S(1)} %get-tuple-element.62), channel_id=1, source_target_pairs={{0,29},{1,28},{2,31},{3,30},{4,25},{5,24},{6,27},{7,26},{8,21},{9,... | collective-permute-start | bytes 245768 | tf_op jit(solution)/shard_map/ppermute | solution.py:356
  41.0 0.0 collective-permute-done.12.refs_13_
  41.0 1.1 %collective-permute-start.17 = (f32[16,1280]{1,0:T(8,128)S(1)}, f32[16,1280]{1,0:T(8,128)S(1)}, u32[]{:S(2)}, u32[]{:S(2)}) collective-permute-start(f32[16,1280]{1,0:T(8,128)S(1)} %get-tuple-element.63), channel_id=1, source_target_pairs={{0,9},{1,8},{2,11},{3,10},{4,13},{5,12},{6,15},{7,14},{8,1},{9,0},... | collective-permute-start | bytes 245768 | tf_op jit(solution)/shard_map/ppermute | solution.py:356
  42.1 1.8 %collective-permute-done.13.refs_14_ = f32[16,1280]{1,0:T(8,128)S(1)} collective-permute-done((f32[16,1280]{1,0:T(8,128)S(1)}, f32[16,1280]{1,0:T(8,128)S(1)}, u32[]{:S(2)}, u32[]{:S(2)}) %collective-permute-start.13) | collective-permute-done | bytes 81952 | tf_op jit(solution)/shard_map/ppermute | solution.py:356
  43.9 0.0 collective-permute-start.18
  43.9 0.6 collective-permute-done.14.refs_15_
  44.5 0.0 collective-permute-start.19
  44.5 1.1 %collective-permute-done.15.refs_0_ = f32[16,1280]{1,0:T(8,128)S(1)} collective-permute-done((f32[16,1280]{1,0:T(8,128)S(1)}, f32[16,1280]{1,0:T(8,128)S(1)}, u32[]{:S(2)}, u32[]{:S(2)}) %collective-permute-start.15) | collective-permute-done | bytes 81952 | tf_op jit(solution)/shard_map/ppermute | solution.py:356
  45.6 2.5 %collective-permute-start.20 = (f32[16,1280]{1,0:T(8,128)S(1)}, f32[16,1280]{1,0:T(8,128)S(1)}, u32[]{:S(2)}, u32[]{:S(2)}) collective-permute-start(f32[16,1280]{1,0:T(8,128)S(1)} %get-tuple-element.66), channel_id=1, source_target_pairs={{0,2},{1,3},{2,0},{3,1},{4,6},{5,7},{6,4},{7,5},{8,10},{9,11},{10,... | collective-permute-start | bytes 245768 | tf_op jit(solution)/shard_map/ppermute | solution.py:356
  48.1 1.6 %collective-permute-start.21 = (f32[16,1280]{1,0:T(8,128)S(1)}, f32[16,1280]{1,0:T(8,128)S(1)}, u32[]{:S(2)}, u32[]{:S(2)}) collective-permute-start(f32[16,1280]{1,0:T(8,128)S(1)} %get-tuple-element.67), channel_id=1, source_target_pairs={{0,31},{1,30},{2,29},{3,28},{4,27},{5,26},{6,25},{7,24},{8,23},{9,... | collective-permute-start | bytes 245768 | tf_op jit(solution)/shard_map/ppermute | solution.py:356
  49.7 0.0 collective-permute-done.17.refs_2_
  49.7 1.7 %collective-permute-start.22 = (f32[16,1280]{1,0:T(8,128)S(1)}, f32[16,1280]{1,0:T(8,128)S(1)}, u32[]{:S(2)}, u32[]{:S(2)}) collective-permute-start(f32[16,1280]{1,0:T(8,128)S(1)} %get-tuple-element.68), channel_id=1, source_target_pairs={{0,3},{1,2},{2,1},{3,0},{4,7},{5,6},{6,5},{7,4},{8,11},{9,10},{10,... | collective-permute-start | bytes 245768 | tf_op jit(solution)/shard_map/ppermute | solution.py:356
  51.4 0.8 %collective-permute-done.18.refs_3_ = f32[16,1280]{1,0:T(8,128)S(1)} collective-permute-done((f32[16,1280]{1,0:T(8,128)S(1)}, f32[16,1280]{1,0:T(8,128)S(1)}, u32[]{:S(2)}, u32[]{:S(2)}) %collective-permute-start.18) | collective-permute-done | bytes 81952 | tf_op jit(solution)/shard_map/ppermute | solution.py:356
  52.2 0.6 collective-permute-start.23
  52.8 1.1 %weights.1 = (bf16[512,512]{1,0:T(8,128)(2,1)S(1)}, bf16[512,512]{1,0:T(8,128)(2,1)S(1)}, bf16[512,96]{1,0:T(8,128)(2,1)S(1)}) custom-call(f32[1,128]{1,0:T(1,128)S(1)} %bitcast.1, s32[1,128]{1,0:T(1,128)S(1)} %copy-done.2), custom_call_target="tpu_custom_call" | custom-call | flops 268435456 | bytes 1048576 | tf_op jit(solution)/shard_map/weights/pallas_call | solution.py:191
  53.9 0.0 collective-permute-done.19.refs_4_
  53.9 2.7 %collective-permute-start.24 = (f32[16,1280]{1,0:T(8,128)S(1)}, f32[16,1280]{1,0:T(8,128)S(1)}, u32[]{:S(2)}, u32[]{:S(2)}) collective-permute-start(f32[16,1280]{1,0:T(8,128)S(1)} %get-tuple-element.70), channel_id=1, source_target_pairs={{0,6},{1,7},{2,4},{3,5},{4,2},{5,3},{6,0},{7,1},{8,14},{9,15},{10,... | collective-permute-start | bytes 245768 | tf_op jit(solution)/shard_map/ppermute | solution.py:356
  56.7 1.6 %collective-permute-start.25 = (f32[16,1280]{1,0:T(8,128)S(1)}, f32[16,1280]{1,0:T(8,128)S(1)}, u32[]{:S(2)}, u32[]{:S(2)}) collective-permute-start(f32[16,1280]{1,0:T(8,128)S(1)} %get-tuple-element.71), channel_id=1, source_target_pairs={{0,27},{1,26},{2,25},{3,24},{4,31},{5,30},{6,29},{7,28},{8,19},{9,... | collective-permute-start | bytes 245768 | tf_op jit(solution)/shard_map/ppermute | solution.py:356
  58.3 0.0 collective-permute-done.21.refs_6_
  58.3 2.4 %collective-permute-start.26 = (f32[16,1280]{1,0:T(8,128)S(1)}, f32[16,1280]{1,0:T(8,128)S(1)}, u32[]{:S(2)}, u32[]{:S(2)}) collective-permute-start(f32[16,1280]{1,0:T(8,128)S(1)} %get-tuple-element.72), channel_id=1, source_target_pairs={{0,7},{1,6},{2,5},{3,4},{4,3},{5,2},{6,1},{7,0},{8,15},{9,14},{10,... | collective-permute-start | bytes 245768 | tf_op jit(solution)/shard_map/ppermute | solution.py:356
  60.8 0.0 collective-permute-done.22.refs_7_
  60.8 0.4 collective-permute-start.27
  61.2 0.0 collective-permute-done.23.refs_8_
  61.2 0.0 collective-permute-start.28
  61.2 1.2 %temporal.2.so_far_ref = f32[512,1280]{1,0:T(8,128)S(1)} custom-call(bf16[512,512]{1,0:T(8,128)(2,1)S(1)} %get-tuple-element.43.high_ref, bf16[512,512]{1,0:T(8,128)(2,1)S(1)} %get-tuple-element.44.low_ref, f32[16,1280]{1,0:T(8,128)S(1)} %get-tuple-element.45.refs_0_, f32[16,1280]{1,0:T(8,128)S(1)} %collective-permute-done.refs_1_, ...), custom_call_target="tpu_custom_call" | custom-call | flops 1006632960 | bytes 5242880 | tf_op jit(solution)/shard_map/temporal/pallas_call | solution.py:265
  62.4 0.0 collective-permute-done.24.refs_9_
  62.4 2.0 %collective-permute-start.29 = (f32[16,1280]{1,0:T(8,128)S(1)}, f32[16,1280]{1,0:T(8,128)S(1)}, u32[]{:S(2)}, u32[]{:S(2)}) collective-permute-start(f32[16,1280]{1,0:T(8,128)S(1)} %get-tuple-element.77), channel_id=1, source_target_pairs={{0,24},{1,25},{2,26},{3,27},{4,28},{5,29},{6,30},{7,31},{8,16},{9,... | collective-permute-start | bytes 245768 | tf_op jit(solution)/shard_map/ppermute | solution.py:356
  64.5 0.0 collective-permute-done.25.refs_10_
  64.5 2.9 %collective-permute-start.30 = (f32[16,1280]{1,0:T(8,128)S(1)}, f32[16,1280]{1,0:T(8,128)S(1)}, u32[]{:S(2)}, u32[]{:S(2)}) collective-permute-start(f32[16,1280]{1,0:T(8,128)S(1)} %get-tuple-element.78), channel_id=1, source_target_pairs={{0,25},{1,24},{2,27},{3,26},{4,29},{5,28},{6,31},{7,30},{8,17},{9,... | collective-permute-start | bytes 245768 | tf_op jit(solution)/shard_map/ppermute | solution.py:356
  67.4 0.0 collective-permute-done.26.refs_11_
  67.4 0.1 collective-permute-done.27.refs_12_
  67.5 0.0 collective-permute-done.28.refs_13_
  67.5 2.2 %temporal.3 = (f32[512,1280]{1,0:T(8,128)S(1)}, f32[128,4,1280]{2,1,0:T(4,128)}) custom-call(bf16[512,512]{1,0:T(8,128)(2,1)S(1)} %get-tuple-element.43.high_ref, bf16[512,512]{1,0:T(8,128)(2,1)S(1)} %get-tuple-element.44.low_ref, f32[512,1280]{1,0:T(8,128)S(1)} %temporal.2.so_far_ref, f32[16,1280]{1,0:T(8,128)S(1)} %collective-permute-done.15.refs_0_, ...), custom_call_target="tpu_custom_call" | custom-call | flops 880803840 | bytes 5242880 | tf_op jit(solution)/shard_map/temporal/pallas_call | solution.py:265
  69.7 0.8 %collective-permute-done.30.refs_1_ = f32[16,1280]{1,0:T(8,128)S(1)} collective-permute-done((f32[16,1280]{1,0:T(8,128)S(1)}, f32[16,1280]{1,0:T(8,128)S(1)}, u32[]{:S(2)}, u32[]{:S(2)}) %collective-permute-start.30) | collective-permute-done | bytes 81952 | tf_op jit(solution)/shard_map/ppermute | solution.py:356
  70.5 1.2 %finish.1 = f32[128,4,1280]{2,1,0:T(4,128)} custom-call(bf16[512,96]{1,0:T(8,128)(2,1)S(1)} %get-tuple-element.42.weights_ref, f32[512,1280]{1,0:T(8,128)S(1)} %get-tuple-element.75.so_far_ref, f32[128,4,1280]{2,1,0:T(4,128)} %get-tuple-element.76._, f32[16,1280]{1,0:T(8,128)S(1)} %collective-permute-done.29.refs_0_, ...), custom_call_target="tpu_custom_call", output_to_operand_aliasing={{}: (2, {})} | custom-call | flops 55050240 | bytes 2293760 | tf_op jit(solution)/shard_map/finish/pallas_call | solution.py:320
  (10 shorter events, 0.0 us)
Async XLA Ops:
  0.0 52.8 %copy-start.2 = (s32[1,128]{1,0:T(1,128)S(1)}, s32[1,128]{1,0:T(1,128)}, u32[]{:S(2)}) copy-start(s32[1,128]{1,0:T(1,128)} %constant.2.clone.partner_ref) | copy-start | bytes 1540
  0.0 5.5 %copy-start = (f32[4,128,1280]{2,1,0:T(8,128)S(1)}, f32[4,128,1280]{2,1,0:T(8,128)}, u32[]{:S(2)}) copy-start(f32[4,128,1280]{2,1,0:T(8,128)} %frames_ref.3) | copy-start | bytes 7864324
  0.0 52.8 %copy-start.1 = (f32[128]{0:T(128)S(1)}, f32[128]{0:T(128)}, u32[]{:S(2)}) copy-start(f32[128]{0:T(128)} %param.5) | copy-start | bytes 1540
  1.4 13.3 %collective-permute-start = (f32[16,1280]{1,0:T(8,128)S(1)}, f32[16,1280]{1,0:T(8,128)S(1)}, u32[]{:S(2)}, u32[]{:S(2)}) collective-permute-start(f32[16,1280]{1,0:T(8,128)S(1)} %get-tuple-element.46), channel_id=1, source_target_pairs={{0,16},{1,17},{2,18},{3,19},{4,20},{5,21},{6,22},{7,23},{8,24},{9,... | collective-permute-start | bytes 245768 | tf_op jit(solution)/shard_map/ppermute | solution.py:356
  5.5 12.6 %collective-permute-start.1 = (f32[16,1280]{1,0:T(8,128)S(1)}, f32[16,1280]{1,0:T(8,128)S(1)}, u32[]{:S(2)}, u32[]{:S(2)}) collective-permute-start(f32[16,1280]{1,0:T(8,128)S(1)} %get-tuple-element.47), channel_id=1, source_target_pairs={{0,17},{1,16},{2,19},{3,18},{4,21},{5,20},{6,23},{7,22},{8,25},{9,... | collective-permute-start | bytes 245768 | tf_op jit(solution)/shard_map/ppermute | solution.py:356
  8.5 11.7 %collective-permute-start.2 = (f32[16,1280]{1,0:T(8,128)S(1)}, f32[16,1280]{1,0:T(8,128)S(1)}, u32[]{:S(2)}, u32[]{:S(2)}) collective-permute-start(f32[16,1280]{1,0:T(8,128)S(1)} %get-tuple-element.48), channel_id=1, source_target_pairs={{0,18},{1,19},{2,16},{3,17},{4,22},{5,23},{6,20},{7,21},{8,26},{9,... | collective-permute-start | bytes 245768 | tf_op jit(solution)/shard_map/ppermute | solution.py:356
  11.5 10.9 %collective-permute-start.3 = (f32[16,1280]{1,0:T(8,128)S(1)}, f32[16,1280]{1,0:T(8,128)S(1)}, u32[]{:S(2)}, u32[]{:S(2)}) collective-permute-start(f32[16,1280]{1,0:T(8,128)S(1)} %get-tuple-element.49), channel_id=1, source_target_pairs={{0,19},{1,18},{2,17},{3,16},{4,23},{5,22},{6,21},{7,20},{8,27},{9,... | collective-permute-start | bytes 245768 | tf_op jit(solution)/shard_map/ppermute | solution.py:356
  12.2 14.6 %collective-permute-start.4 = (f32[16,1280]{1,0:T(8,128)S(1)}, f32[16,1280]{1,0:T(8,128)S(1)}, u32[]{:S(2)}, u32[]{:S(2)}) collective-permute-start(f32[16,1280]{1,0:T(8,128)S(1)} %get-tuple-element.50), channel_id=1, source_target_pairs={{0,12},{1,13},{2,14},{3,15},{4,8},{5,9},{6,10},{7,11},{8,4},{9,5},... | collective-permute-start | bytes 245768 | tf_op jit(solution)/shard_map/ppermute | solution.py:356
  14.7 13.5 %collective-permute-start.5 = (f32[16,1280]{1,0:T(8,128)S(1)}, f32[16,1280]{1,0:T(8,128)S(1)}, u32[]{:S(2)}, u32[]{:S(2)}) collective-permute-start(f32[16,1280]{1,0:T(8,128)S(1)} %get-tuple-element.51), channel_id=1, source_target_pairs={{0,22},{1,23},{2,20},{3,21},{4,18},{5,19},{6,16},{7,17},{8,30},{9,... | collective-permute-start | bytes 245768 | tf_op jit(solution)/shard_map/ppermute | solution.py:356
  18.1 10.1 %collective-permute-start.6 = (f32[16,1280]{1,0:T(8,128)S(1)}, f32[16,1280]{1,0:T(8,128)S(1)}, u32[]{:S(2)}, u32[]{:S(2)}) collective-permute-start(f32[16,1280]{1,0:T(8,128)S(1)} %get-tuple-element.52), channel_id=1, source_target_pairs={{0,13},{1,12},{2,15},{3,14},{4,9},{5,8},{6,11},{7,10},{8,5},{9,4},... | collective-permute-start | bytes 245768 | tf_op jit(solution)/shard_map/ppermute | solution.py:356
  20.1 12.1 %collective-permute-start.7 = (f32[16,1280]{1,0:T(8,128)S(1)}, f32[16,1280]{1,0:T(8,128)S(1)}, u32[]{:S(2)}, u32[]{:S(2)}) collective-permute-start(f32[16,1280]{1,0:T(8,128)S(1)} %get-tuple-element.53), channel_id=1, source_target_pairs={{0,23},{1,22},{2,21},{3,20},{4,19},{5,18},{6,17},{7,16},{8,31},{9,... | collective-permute-start | bytes 245768 | tf_op jit(solution)/shard_map/ppermute | solution.py:356
  22.4 13.4 %collective-permute-start.8 = (f32[16,1280]{1,0:T(8,128)S(1)}, f32[16,1280]{1,0:T(8,128)S(1)}, u32[]{:S(2)}, u32[]{:S(2)}) collective-permute-start(f32[16,1280]{1,0:T(8,128)S(1)} %get-tuple-element.54), channel_id=1, source_target_pairs={{0,14},{1,15},{2,12},{3,13},{4,10},{5,11},{6,8},{7,9},{8,6},{9,7},... | collective-permute-start | bytes 245768 | tf_op jit(solution)/shard_map/ppermute | solution.py:356
  26.8 9.7 %collective-permute-start.9 = (f32[16,1280]{1,0:T(8,128)S(1)}, f32[16,1280]{1,0:T(8,128)S(1)}, u32[]{:S(2)}, u32[]{:S(2)}) collective-permute-start(f32[16,1280]{1,0:T(8,128)S(1)} %get-tuple-element.55), channel_id=1, source_target_pairs={{0,20},{1,21},{2,22},{3,23},{4,16},{5,17},{6,18},{7,19},{8,28},{9,... | collective-permute-start | bytes 245768 | tf_op jit(solution)/shard_map/ppermute | solution.py:356
  28.2 10.4 %collective-permute-start.10 = (f32[16,1280]{1,0:T(8,128)S(1)}, f32[16,1280]{1,0:T(8,128)S(1)}, u32[]{:S(2)}, u32[]{:S(2)}) collective-permute-start(f32[16,1280]{1,0:T(8,128)S(1)} %get-tuple-element.56), channel_id=1, source_target_pairs={{0,15},{1,14},{2,13},{3,12},{4,11},{5,10},{6,9},{7,8},{8,7},{9,6},... | collective-permute-start | bytes 245768 | tf_op jit(solution)/shard_map/ppermute | solution.py:356
  28.2 10.4 %collective-permute-start.11 = (f32[16,1280]{1,0:T(8,128)S(1)}, f32[16,1280]{1,0:T(8,128)S(1)}, u32[]{:S(2)}, u32[]{:S(2)}) collective-permute-start(f32[16,1280]{1,0:T(8,128)S(1)} %get-tuple-element.57), channel_id=1, source_target_pairs={{0,21},{1,20},{2,23},{3,22},{4,17},{5,16},{6,19},{7,18},{8,29},{9,... | collective-permute-start | bytes 245768 | tf_op jit(solution)/shard_map/ppermute | solution.py:356
  32.2 8.8 %collective-permute-start.12 = (f32[16,1280]{1,0:T(8,128)S(1)}, f32[16,1280]{1,0:T(8,128)S(1)}, u32[]{:S(2)}, u32[]{:S(2)}) collective-permute-start(f32[16,1280]{1,0:T(8,128)S(1)} %get-tuple-element.58), channel_id=1, source_target_pairs={{0,10},{1,11},{2,8},{3,9},{4,14},{5,15},{6,12},{7,13},{8,2},{9,3},... | collective-permute-start | bytes 245768 | tf_op jit(solution)/shard_map/ppermute | solution.py:356
  35.8 8.1 %collective-permute-start.13 = (f32[16,1280]{1,0:T(8,128)S(1)}, f32[16,1280]{1,0:T(8,128)S(1)}, u32[]{:S(2)}, u32[]{:S(2)}) collective-permute-start(f32[16,1280]{1,0:T(8,128)S(1)} %get-tuple-element.59), channel_id=1, source_target_pairs={{0,11},{1,10},{2,9},{3,8},{4,15},{5,14},{6,13},{7,12},{8,3},{9,2},... | collective-permute-start | bytes 245768 | tf_op jit(solution)/shard_map/ppermute | solution.py:356
  36.5 8.0 %collective-permute-start.14 = (f32[16,1280]{1,0:T(8,128)S(1)}, f32[16,1280]{1,0:T(8,128)S(1)}, u32[]{:S(2)}, u32[]{:S(2)}) collective-permute-start(f32[16,1280]{1,0:T(8,128)S(1)} %get-tuple-element.60), channel_id=1, source_target_pairs={{0,28},{1,29},{2,30},{3,31},{4,24},{5,25},{6,26},{7,27},{8,20},{9,... | collective-permute-start | bytes 245768 | tf_op jit(solution)/shard_map/ppermute | solution.py:356
  38.5 7.0 %collective-permute-start.15 = (f32[16,1280]{1,0:T(8,128)S(1)}, f32[16,1280]{1,0:T(8,128)S(1)}, u32[]{:S(2)}, u32[]{:S(2)}) collective-permute-start(f32[16,1280]{1,0:T(8,128)S(1)} %get-tuple-element.61), channel_id=1, source_target_pairs={{0,8},{1,9},{2,10},{3,11},{4,12},{5,13},{6,14},{7,15},{8,0},{9,1},... | collective-permute-start | bytes 245768 | tf_op jit(solution)/shard_map/ppermute | solution.py:356
  38.6 9.6 %collective-permute-start.16 = (f32[16,1280]{1,0:T(8,128)S(1)}, f32[16,1280]{1,0:T(8,128)S(1)}, u32[]{:S(2)}, u32[]{:S(2)}) collective-permute-start(f32[16,1280]{1,0:T(8,128)S(1)} %get-tuple-element.62), channel_id=1, source_target_pairs={{0,29},{1,28},{2,31},{3,30},{4,25},{5,24},{6,27},{7,26},{8,21},{9,... | collective-permute-start | bytes 245768 | tf_op jit(solution)/shard_map/ppermute | solution.py:356
  41.0 8.7 %collective-permute-start.17 = (f32[16,1280]{1,0:T(8,128)S(1)}, f32[16,1280]{1,0:T(8,128)S(1)}, u32[]{:S(2)}, u32[]{:S(2)}) collective-permute-start(f32[16,1280]{1,0:T(8,128)S(1)} %get-tuple-element.63), channel_id=1, source_target_pairs={{0,9},{1,8},{2,11},{3,10},{4,13},{5,12},{6,15},{7,14},{8,1},{9,0},... | collective-permute-start | bytes 245768 | tf_op jit(solution)/shard_map/ppermute | solution.py:356
  43.9 8.3 %collective-permute-start.18 = (f32[16,1280]{1,0:T(8,128)S(1)}, f32[16,1280]{1,0:T(8,128)S(1)}, u32[]{:S(2)}, u32[]{:S(2)}) collective-permute-start(f32[16,1280]{1,0:T(8,128)S(1)} %get-tuple-element.64), channel_id=1, source_target_pairs={{0,30},{1,31},{2,28},{3,29},{4,26},{5,27},{6,24},{7,25},{8,22},{9,... | collective-permute-start | bytes 245768 | tf_op jit(solution)/shard_map/ppermute | solution.py:356
  44.5 9.5 %collective-permute-start.19 = (f32[16,1280]{1,0:T(8,128)S(1)}, f32[16,1280]{1,0:T(8,128)S(1)}, u32[]{:S(2)}, u32[]{:S(2)}) collective-permute-start(f32[16,1280]{1,0:T(8,128)S(1)} %get-tuple-element.65), channel_id=1, source_target_pairs={{0,1},{1,0},{2,3},{3,2},{4,5},{5,4},{6,7},{7,6},{8,9},{9,8},{10,11... | collective-permute-start | bytes 245768 | tf_op jit(solution)/shard_map/ppermute | solution.py:356
  45.6 11.1 %collective-permute-start.20 = (f32[16,1280]{1,0:T(8,128)S(1)}, f32[16,1280]{1,0:T(8,128)S(1)}, u32[]{:S(2)}, u32[]{:S(2)}) collective-permute-start(f32[16,1280]{1,0:T(8,128)S(1)} %get-tuple-element.66), channel_id=1, source_target_pairs={{0,2},{1,3},{2,0},{3,1},{4,6},{5,7},{6,4},{7,5},{8,10},{9,11},{10,... | collective-permute-start | bytes 245768 | tf_op jit(solution)/shard_map/ppermute | solution.py:356
  48.1 10.2 %collective-permute-start.21 = (f32[16,1280]{1,0:T(8,128)S(1)}, f32[16,1280]{1,0:T(8,128)S(1)}, u32[]{:S(2)}, u32[]{:S(2)}) collective-permute-start(f32[16,1280]{1,0:T(8,128)S(1)} %get-tuple-element.67), channel_id=1, source_target_pairs={{0,31},{1,30},{2,29},{3,28},{4,27},{5,26},{6,25},{7,24},{8,23},{9,... | collective-permute-start | bytes 245768 | tf_op jit(solution)/shard_map/ppermute | solution.py:356
  49.7 11.1 %collective-permute-start.22 = (f32[16,1280]{1,0:T(8,128)S(1)}, f32[16,1280]{1,0:T(8,128)S(1)}, u32[]{:S(2)}, u32[]{:S(2)}) collective-permute-start(f32[16,1280]{1,0:T(8,128)S(1)} %get-tuple-element.68), channel_id=1, source_target_pairs={{0,3},{1,2},{2,1},{3,0},{4,7},{5,6},{6,5},{7,4},{8,11},{9,10},{10,... | collective-permute-start | bytes 245768 | tf_op jit(solution)/shard_map/ppermute | solution.py:356
  52.2 9.0 %collective-permute-start.23 = (f32[16,1280]{1,0:T(8,128)S(1)}, f32[16,1280]{1,0:T(8,128)S(1)}, u32[]{:S(2)}, u32[]{:S(2)}) collective-permute-start(f32[16,1280]{1,0:T(8,128)S(1)} %get-tuple-element.69), channel_id=1, source_target_pairs={{0,26},{1,27},{2,24},{3,25},{4,30},{5,31},{6,28},{7,29},{8,18},{9,... | collective-permute-start | bytes 245768 | tf_op jit(solution)/shard_map/ppermute | solution.py:356
  53.9 8.5 %collective-permute-start.24 = (f32[16,1280]{1,0:T(8,128)S(1)}, f32[16,1280]{1,0:T(8,128)S(1)}, u32[]{:S(2)}, u32[]{:S(2)}) collective-permute-start(f32[16,1280]{1,0:T(8,128)S(1)} %get-tuple-element.70), channel_id=1, source_target_pairs={{0,6},{1,7},{2,4},{3,5},{4,2},{5,3},{6,0},{7,1},{8,14},{9,15},{10,... | collective-permute-start | bytes 245768 | tf_op jit(solution)/shard_map/ppermute | solution.py:356
  56.7 7.8 %collective-permute-start.25 = (f32[16,1280]{1,0:T(8,128)S(1)}, f32[16,1280]{1,0:T(8,128)S(1)}, u32[]{:S(2)}, u32[]{:S(2)}) collective-permute-start(f32[16,1280]{1,0:T(8,128)S(1)} %get-tuple-element.71), channel_id=1, source_target_pairs={{0,27},{1,26},{2,25},{3,24},{4,31},{5,30},{6,29},{7,28},{8,19},{9,... | collective-permute-start | bytes 245768 | tf_op jit(solution)/shard_map/ppermute | solution.py:356
  58.3 9.0 %collective-permute-start.26 = (f32[16,1280]{1,0:T(8,128)S(1)}, f32[16,1280]{1,0:T(8,128)S(1)}, u32[]{:S(2)}, u32[]{:S(2)}) collective-permute-start(f32[16,1280]{1,0:T(8,128)S(1)} %get-tuple-element.72), channel_id=1, source_target_pairs={{0,7},{1,6},{2,5},{3,4},{4,3},{5,2},{6,1},{7,0},{8,15},{9,14},{10,... | collective-permute-start | bytes 245768 | tf_op jit(solution)/shard_map/ppermute | solution.py:356
  60.8 6.7 %collective-permute-start.27 = (f32[16,1280]{1,0:T(8,128)S(1)}, f32[16,1280]{1,0:T(8,128)S(1)}, u32[]{:S(2)}, u32[]{:S(2)}) collective-permute-start(f32[16,1280]{1,0:T(8,128)S(1)} %get-tuple-element.73), channel_id=1, source_target_pairs={{0,4},{1,5},{2,6},{3,7},{4,0},{5,1},{6,2},{7,3},{8,12},{9,13},{10,... | collective-permute-start | bytes 245768 | tf_op jit(solution)/shard_map/ppermute | solution.py:356
  61.2 6.3 %collective-permute-start.28 = (f32[16,1280]{1,0:T(8,128)S(1)}, f32[16,1280]{1,0:T(8,128)S(1)}, u32[]{:S(2)}, u32[]{:S(2)}) collective-permute-start(f32[16,1280]{1,0:T(8,128)S(1)} %get-tuple-element.74), channel_id=1, source_target_pairs={{0,5},{1,4},{2,7},{3,6},{4,1},{5,0},{6,3},{7,2},{8,13},{9,12},{10,... | collective-permute-start | bytes 245768 | tf_op jit(solution)/shard_map/ppermute | solution.py:356
  62.4 7.3 %collective-permute-start.29 = (f32[16,1280]{1,0:T(8,128)S(1)}, f32[16,1280]{1,0:T(8,128)S(1)}, u32[]{:S(2)}, u32[]{:S(2)}) collective-permute-start(f32[16,1280]{1,0:T(8,128)S(1)} %get-tuple-element.77), channel_id=1, source_target_pairs={{0,24},{1,25},{2,26},{3,27},{4,28},{5,29},{6,30},{7,31},{8,16},{9,... | collective-permute-start | bytes 245768 | tf_op jit(solution)/shard_map/ppermute | solution.py:356
  64.5 6.1 %collective-permute-start.30 = (f32[16,1280]{1,0:T(8,128)S(1)}, f32[16,1280]{1,0:T(8,128)S(1)}, u32[]{:S(2)}, u32[]{:S(2)}) collective-permute-start(f32[16,1280]{1,0:T(8,128)S(1)} %get-tuple-element.78), channel_id=1, source_target_pairs={{0,25},{1,24},{2,27},{3,26},{4,29},{5,28},{6,31},{7,30},{8,17},{9,... | collective-permute-start | bytes 245768 | tf_op jit(solution)/shard_map/ppermute | solution.py:356

commit v6 on v5

--- a/solution.py
+++ b/solution.py
@@ -14,6 +14,7 @@
 VMEM = pltpu.VMEM
 SMEM = pltpu.SMEM
 KERNEL_BYTES = 20 << 20
+FIRST_BYTES = 56000000
 WIDTH = 256
 STAGES = (1,)
 LATER = 1.25
@@ -29,7 +30,9 @@
     half = devices // 2
     lows = gray_order(half, strips)
     across = [half ^ low for low in lows]
-    within = [low for low in lows if low >= half // 2] + [k for k in lows if 0 < k < half // 2]
+    within = [low for low in lows if low >= half // 2] + [
+        k for k in lows[::-1] if 0 < k < half // 2
+    ]
     order, rest = across[:AHEAD], across[AHEAD:]
     done = 0
     for at, k in enumerate(rest):
@@ -136,7 +139,7 @@
         cost_estimate=pl.CostEstimate(
             flops=5 * total, bytes_accessed=2 * total, transcendentals=0
         ),
-        compiler_params=pltpu.CompilerParams(vmem_limit_bytes=KERNEL_BYTES),
+        compiler_params=pltpu.CompilerParams(vmem_limit_bytes=FIRST_BYTES - total if direct else KERNEL_BYTES),
         name="stencil",
     )(far(kernel), far(frames) if direct else frames)
 

time: 72.1 us -> 72.2 us (level)
  waiting for transfers between devices: 7.4 us -> 10.3 us
  starting transfers between devices: 54.2 us -> 51.6 us
    ppermute x31, waiting for transfers between devices: 7.4 us -> 10.3 us  [local(): lax.ppermute(made[k], 'blk', [(i, i ^ k) for i in range(devices)])]
    ppermute x31, starting transfers between devices: 54.2 us -> 51.6 us  [local(): lax.ppermute(made[k], 'blk', [(i, i ^ k) for i in range(devices)])]
  transfers between devices with their start and end apart: 31 -> 31, of which waited for: 8 -> 10; matrix products, arithmetic and copies ran while one was open for 0% -> 0% of each run, Pallas kernels for 10% -> 10%
where the time goes in v6:
time: 72.2 us; the launch traced here: 72 us
  starting transfers between devices  51.6 us (71%)
  waiting for transfers between devices  10.3 us (14%)
  Pallas kernels  10 us (14%)
    ppermute x31, starting transfers between devices, local(): lax.ppermute(made[k], 'blk', [(i, i ^ k) for i in range(devices)])  51.6 us
    ppermute x31, waiting for transfers between devices, local(): lax.ppermute(made[k], 'blk', [(i, i ^ k) for i in range(devices)])  10.3 us
    pallas_call x2, Pallas kernels, stencil(): pl.pallas_call(functools.partial(stencil_kernel, groups=groups, rows=rows...  4.28 us
    pallas_call x2, Pallas kernels, gather(): pl.pallas_call(functools.partial(gather_kernel if first else write_kernel...  3.43 us
  transfers between devices with their start and end apart: 31, of which 10 were waited for; matrix products, arithmetic and copies ran while one was open for 0% of the time, Pallas kernels for 10%

profile of v6, /device:TPU:0, one launch (start us, length us, event | category | flops | bytes accessed | tf_op | source)
XLA Modules:
  0.0 72.0 jit_solution(7440192361192319672)
XLA Ops:
  0.0 1.4 %stencil.3 = (f32[16,1280]{1,0:T(8,128)S(1)}, f32[16,1280]{1,0:T(8,128)S(1)}) custom-call(f32[3,3]{1,0:T(4,128)} %kernel_ref.3, f32[4,128,1280]{2,1,0:T(8,128)} %frames_ref.3), custom_call_target="tpu_custom_call" | custom-call | flops 819200 | bytes 327680 | tf_op jit(solution)/shard_map/stencil/pallas_call | solution.py:130
  1.4 4.2 %collective-permute-start = (f32[16,1280]{1,0:T(8,128)S(1)}, f32[16,1280]{1,0:T(8,128)S(1)}, u32[]{:S(2)}, u32[]{:S(2)}) collective-permute-start(f32[16,1280]{1,0:T(8,128)S(1)} %get-tuple-element.46), channel_id=1, source_target_pairs={{0,16},{1,17},{2,18},{3,19},{4,20},{5,21},{6,22},{7,23},{8,24},{9,... | collective-permute-start | bytes 245768 | tf_op jit(solution)/shard_map/ppermute | solution.py:359
  5.5 0.0 collective-permute-start.1
  5.5 2.9 %stencil.2 = (f32[16,1280]{1,0:T(8,128)S(1)}, f32[16,1280]{1,0:T(8,128)S(1)}, f32[16,1280]{1,0:T(8,128)S(1)}, f32[16,1280]{1,0:T(8,128)S(1)}, f32[16,1280]{1,0:T...) custom-call(f32[3,3]{1,0:T(4,128)} %kernel_ref.3, ...), custom_call_target="tpu_custom_call" | custom-call | flops 12288000 | bytes 4915200 | tf_op jit(solution)/shard_map/stencil/pallas_call | solution.py:130
  8.5 3.1 %collective-permute-start.2 = (f32[16,1280]{1,0:T(8,128)S(1)}, f32[16,1280]{1,0:T(8,128)S(1)}, u32[]{:S(2)}, u32[]{:S(2)}) collective-permute-start(f32[16,1280]{1,0:T(8,128)S(1)} %get-tuple-element.48), channel_id=1, source_target_pairs={{0,18},{1,19},{2,16},{3,17},{4,22},{5,23},{6,20},{7,21},{8,26},{9,... | collective-permute-start | bytes 245768 | tf_op jit(solution)/shard_map/ppermute | solution.py:359
  11.5 0.6 collective-permute-start.3
  12.2 2.5 %collective-permute-start.4 = (f32[16,1280]{1,0:T(8,128)S(1)}, f32[16,1280]{1,0:T(8,128)S(1)}, u32[]{:S(2)}, u32[]{:S(2)}) collective-permute-start(f32[16,1280]{1,0:T(8,128)S(1)} %get-tuple-element.50), channel_id=1, source_target_pairs={{0,12},{1,13},{2,14},{3,15},{4,8},{5,9},{6,10},{7,11},{8,4},{9,5},... | collective-permute-start | bytes 245768 | tf_op jit(solution)/shard_map/ppermute | solution.py:359
  14.7 0.0 collective-permute-done.refs_1_
  14.7 3.4 %collective-permute-start.5 = (f32[16,1280]{1,0:T(8,128)S(1)}, f32[16,1280]{1,0:T(8,128)S(1)}, u32[]{:S(2)}, u32[]{:S(2)}) collective-permute-start(f32[16,1280]{1,0:T(8,128)S(1)} %get-tuple-element.51), channel_id=1, source_target_pairs={{0,22},{1,23},{2,20},{3,21},{4,18},{5,19},{6,16},{7,17},{8,30},{9,... | collective-permute-start | bytes 245768 | tf_op jit(solution)/shard_map/ppermute | solution.py:359
  18.1 0.0 collective-permute-done.1.refs_2_
  18.1 0.3 collective-permute-start.6
  18.4 1.7 %collective-permute-done.2.refs_3_ = f32[16,1280]{1,0:T(8,128)S(1)} collective-permute-done((f32[16,1280]{1,0:T(8,128)S(1)}, f32[16,1280]{1,0:T(8,128)S(1)}, u32[]{:S(2)}, u32[]{:S(2)}) %collective-permute-start.2) | collective-permute-done | bytes 81952 | tf_op jit(solution)/shard_map/ppermute | solution.py:359
  20.1 2.3 %collective-permute-start.7 = (f32[16,1280]{1,0:T(8,128)S(1)}, f32[16,1280]{1,0:T(8,128)S(1)}, u32[]{:S(2)}, u32[]{:S(2)}) collective-permute-start(f32[16,1280]{1,0:T(8,128)S(1)} %get-tuple-element.53), channel_id=1, source_target_pairs={{0,23},{1,22},{2,21},{3,20},{4,19},{5,18},{6,17},{7,16},{8,31},{9,... | collective-permute-start | bytes 245768 | tf_op jit(solution)/shard_map/ppermute | solution.py:359
  22.4 0.0 collective-permute-done.3.refs_4_
  22.4 4.4 %collective-permute-start.8 = (f32[16,1280]{1,0:T(8,128)S(1)}, f32[16,1280]{1,0:T(8,128)S(1)}, u32[]{:S(2)}, u32[]{:S(2)}) collective-permute-start(f32[16,1280]{1,0:T(8,128)S(1)} %get-tuple-element.54), channel_id=1, source_target_pairs={{0,14},{1,15},{2,12},{3,13},{4,10},{5,11},{6,8},{7,9},{8,6},{9,7},... | collective-permute-start | bytes 245768 | tf_op jit(solution)/shard_map/ppermute | solution.py:359
  26.8 0.0 collective-permute-done.4.refs_5_
  26.8 1.4 %collective-permute-start.9 = (f32[16,1280]{1,0:T(8,128)S(1)}, f32[16,1280]{1,0:T(8,128)S(1)}, u32[]{:S(2)}, u32[]{:S(2)}) collective-permute-start(f32[16,1280]{1,0:T(8,128)S(1)} %get-tuple-element.55), channel_id=1, source_target_pairs={{0,20},{1,21},{2,22},{3,23},{4,16},{5,17},{6,18},{7,19},{8,28},{9,... | collective-permute-start | bytes 245768 | tf_op jit(solution)/shard_map/ppermute | solution.py:359
  28.2 0.0 collective-permute-done.5.refs_6_
  28.2 0.0 collective-permute-start.10
  28.2 0.0 collective-permute-done.6.refs_7_
  28.2 4.0 %collective-permute-start.11 = (f32[16,1280]{1,0:T(8,128)S(1)}, f32[16,1280]{1,0:T(8,128)S(1)}, u32[]{:S(2)}, u32[]{:S(2)}) collective-permute-start(f32[16,1280]{1,0:T(8,128)S(1)} %get-tuple-element.57), channel_id=1, source_target_pairs={{0,21},{1,20},{2,23},{3,22},{4,17},{5,16},{6,19},{7,18},{8,29},{9,... | collective-permute-start | bytes 245768 | tf_op jit(solution)/shard_map/ppermute | solution.py:359
  32.2 0.0 collective-permute-done.7.refs_8_
  32.2 3.6 %collective-permute-start.12 = (f32[16,1280]{1,0:T(8,128)S(1)}, f32[16,1280]{1,0:T(8,128)S(1)}, u32[]{:S(2)}, u32[]{:S(2)}) collective-permute-start(f32[16,1280]{1,0:T(8,128)S(1)} %get-tuple-element.58), channel_id=1, source_target_pairs={{0,10},{1,11},{2,8},{3,9},{4,14},{5,15},{6,12},{7,13},{8,2},{9,3},... | collective-permute-start | bytes 245768 | tf_op jit(solution)/shard_map/ppermute | solution.py:359
  35.8 0.0 collective-permute-done.8.refs_9_
  35.8 0.3 collective-permute-start.13
  36.1 0.4 collective-permute-done.9.refs_10_
  36.5 2.1 %collective-permute-start.14 = (f32[16,1280]{1,0:T(8,128)S(1)}, f32[16,1280]{1,0:T(8,128)S(1)}, u32[]{:S(2)}, u32[]{:S(2)}) collective-permute-start(f32[16,1280]{1,0:T(8,128)S(1)} %get-tuple-element.60), channel_id=1, source_target_pairs={{0,28},{1,29},{2,30},{3,31},{4,24},{5,25},{6,26},{7,27},{8,20},{9,... | collective-permute-start | bytes 245768 | tf_op jit(solution)/shard_map/ppermute | solution.py:359
  38.5 0.0 collective-permute-done.10.refs_11_
  38.5 0.0 collective-permute-start.15
  38.5 0.0 collective-permute-done.11.refs_12_
  38.6 2.4 %collective-permute-start.16 = (f32[16,1280]{1,0:T(8,128)S(1)}, f32[16,1280]{1,0:T(8,128)S(1)}, u32[]{:S(2)}, u32[]{:S(2)}) collective-permute-start(f32[16,1280]{1,0:T(8,128)S(1)} %get-tuple-element.62), channel_id=1, source_target_pairs={{0,29},{1,28},{2,31},{3,30},{4,25},{5,24},{6,27},{7,26},{8,21},{9,... | collective-permute-start | bytes 245768 | tf_op jit(solution)/shard_map/ppermute | solution.py:359
  41.0 0.0 collective-permute-done.12.refs_13_
  41.0 1.1 %collective-permute-start.17 = (f32[16,1280]{1,0:T(8,128)S(1)}, f32[16,1280]{1,0:T(8,128)S(1)}, u32[]{:S(2)}, u32[]{:S(2)}) collective-permute-start(f32[16,1280]{1,0:T(8,128)S(1)} %get-tuple-element.63), channel_id=1, source_target_pairs={{0,9},{1,8},{2,11},{3,10},{4,13},{5,12},{6,15},{7,14},{8,1},{9,0},... | collective-permute-start | bytes 245768 | tf_op jit(solution)/shard_map/ppermute | solution.py:359
  42.0 1.8 %collective-permute-done.13.refs_14_ = f32[16,1280]{1,0:T(8,128)S(1)} collective-permute-done((f32[16,1280]{1,0:T(8,128)S(1)}, f32[16,1280]{1,0:T(8,128)S(1)}, u32[]{:S(2)}, u32[]{:S(2)}) %collective-permute-start.13) | collective-permute-done | bytes 81952 | tf_op jit(solution)/shard_map/ppermute | solution.py:359
  43.9 0.0 collective-permute-start.18
  43.9 0.6 collective-permute-done.14.refs_15_
  44.5 0.4 collective-permute-start.19
  44.9 0.7 collective-permute-done.15.refs_0_
  45.6 0.2 collective-permute-start.20
  45.8 1.6 %collective-permute-done.16.refs_1_ = f32[16,1280]{1,0:T(8,128)S(1)} collective-permute-done((f32[16,1280]{1,0:T(8,128)S(1)}, f32[16,1280]{1,0:T(8,128)S(1)}, u32[]{:S(2)}, u32[]{:S(2)}) %collective-permute-start.16) | collective-permute-done | bytes 81952 | tf_op jit(solution)/shard_map/ppermute | solution.py:359
  47.4 3.5 %collective-permute-start.21 = (f32[16,1280]{1,0:T(8,128)S(1)}, f32[16,1280]{1,0:T(8,128)S(1)}, u32[]{:S(2)}, u32[]{:S(2)}) collective-permute-start(f32[16,1280]{1,0:T(8,128)S(1)} %get-tuple-element.67), channel_id=1, source_target_pairs={{0,31},{1,30},{2,29},{3,28},{4,27},{5,26},{6,25},{7,24},{8,23},{9,... | collective-permute-start | bytes 245768 | tf_op jit(solution)/shard_map/ppermute | solution.py:359
  51.0 0.0 collective-permute-done.17.refs_2_
  51.0 0.0 collective-permute-start.22
  51.0 1.2 %collective-permute-done.18.refs_3_ = f32[16,1280]{1,0:T(8,128)S(1)} collective-permute-done((f32[16,1280]{1,0:T(8,128)S(1)}, f32[16,1280]{1,0:T(8,128)S(1)}, u32[]{:S(2)}, u32[]{:S(2)}) %collective-permute-start.18) | collective-permute-done | bytes 81952 | tf_op jit(solution)/shard_map/ppermute | solution.py:359
  52.2 1.8 %collective-permute-start.23 = (f32[16,1280]{1,0:T(8,128)S(1)}, f32[16,1280]{1,0:T(8,128)S(1)}, u32[]{:S(2)}, u32[]{:S(2)}) collective-permute-start(f32[16,1280]{1,0:T(8,128)S(1)} %get-tuple-element.69), channel_id=1, source_target_pairs={{0,26},{1,27},{2,24},{3,25},{4,30},{5,31},{6,28},{7,29},{8,18},{9,... | collective-permute-start | bytes 245768 | tf_op jit(solution)/shard_map/ppermute | solution.py:359
  54.0 1.1 %weights.1 = (bf16[512,512]{1,0:T(8,128)(2,1)S(1)}, bf16[512,512]{1,0:T(8,128)(2,1)S(1)}, bf16[512,96]{1,0:T(8,128)(2,1)S(1)}) custom-call(f32[1,128]{1,0:T(1,128)S(1)} %bitcast.1, s32[1,128]{1,0:T(1,128)S(1)} %copy-done.2), custom_call_target="tpu_custom_call" | custom-call | flops 268435456 | bytes 1048576 | tf_op jit(solution)/shard_map/weights/pallas_call | solution.py:194
  55.1 0.0 collective-permute-done.19.refs_4_
  55.2 1.5 %collective-permute-start.24 = (f32[16,1280]{1,0:T(8,128)S(1)}, f32[16,1280]{1,0:T(8,128)S(1)}, u32[]{:S(2)}, u32[]{:S(2)}) collective-permute-start(f32[16,1280]{1,0:T(8,128)S(1)} %get-tuple-element.70), channel_id=1, source_target_pairs={{0,6},{1,7},{2,4},{3,5},{4,2},{5,3},{6,0},{7,1},{8,14},{9,15},{10,... | collective-permute-start | bytes 245768 | tf_op jit(solution)/shard_map/ppermute | solution.py:359
  56.7 0.0 collective-permute-done.20.refs_5_
  56.7 2.3 %collective-permute-start.25 = (f32[16,1280]{1,0:T(8,128)S(1)}, f32[16,1280]{1,0:T(8,128)S(1)}, u32[]{:S(2)}, u32[]{:S(2)}) collective-permute-start(f32[16,1280]{1,0:T(8,128)S(1)} %get-tuple-element.71), channel_id=1, source_target_pairs={{0,27},{1,26},{2,25},{3,24},{4,31},{5,30},{6,29},{7,28},{8,19},{9,... | collective-permute-start | bytes 245768 | tf_op jit(solution)/shard_map/ppermute | solution.py:359
  59.0 0.0 collective-permute-done.21.refs_6_
  59.0 1.0 %collective-permute-start.26 = (f32[16,1280]{1,0:T(8,128)S(1)}, f32[16,1280]{1,0:T(8,128)S(1)}, u32[]{:S(2)}, u32[]{:S(2)}) collective-permute-start(f32[16,1280]{1,0:T(8,128)S(1)} %get-tuple-element.72), channel_id=1, source_target_pairs={{0,3},{1,2},{2,1},{3,0},{4,7},{5,6},{6,5},{7,4},{8,11},{9,10},{10,... | collective-permute-start | bytes 245768 | tf_op jit(solution)/shard_map/ppermute | solution.py:359
  60.0 1.5 %collective-permute-start.27 = (f32[16,1280]{1,0:T(8,128)S(1)}, f32[16,1280]{1,0:T(8,128)S(1)}, u32[]{:S(2)}, u32[]{:S(2)}) collective-permute-start(f32[16,1280]{1,0:T(8,128)S(1)} %get-tuple-element.73), channel_id=1, source_target_pairs={{0,2},{1,3},{2,0},{3,1},{4,6},{5,7},{6,4},{7,5},{8,10},{9,11},{10,... | collective-permute-start | bytes 245768 | tf_op jit(solution)/shard_map/ppermute | solution.py:359
  61.5 0.0 collective-permute-start.28
  61.5 1.2 %temporal.2.so_far_ref = f32[512,1280]{1,0:T(8,128)S(1)} custom-call(bf16[512,512]{1,0:T(8,128)(2,1)S(1)} %get-tuple-element.43.high_ref, bf16[512,512]{1,0:T(8,128)(2,1)S(1)} %get-tuple-element.44.low_ref, f32[16,1280]{1,0:T(8,128)S(1)} %get-tuple-element.45.refs_0_, f32[16,1280]{1,0:T(8,128)S(1)} %collective-permute-done.refs_1_, ...), custom_call_target="tpu_custom_call" | custom-call | flops 1006632960 | bytes 5242880 | tf_op jit(solution)/shard_map/temporal/pallas_call | solution.py:268
  62.7 0.0 collective-permute-done.24.refs_9_
  62.7 1.9 %collective-permute-start.29 = (f32[16,1280]{1,0:T(8,128)S(1)}, f32[16,1280]{1,0:T(8,128)S(1)}, u32[]{:S(2)}, u32[]{:S(2)}) collective-permute-start(f32[16,1280]{1,0:T(8,128)S(1)} %get-tuple-element.77), channel_id=1, source_target_pairs={{0,24},{1,25},{2,26},{3,27},{4,28},{5,29},{6,30},{7,31},{8,16},{9,... | collective-permute-start | bytes 245768 | tf_op jit(solution)/shard_map/ppermute | solution.py:359
  64.5 0.0 collective-permute-done.25.refs_10_
  64.5 1.9 %collective-permute-start.30 = (f32[16,1280]{1,0:T(8,128)S(1)}, f32[16,1280]{1,0:T(8,128)S(1)}, u32[]{:S(2)}, u32[]{:S(2)}) collective-permute-start(f32[16,1280]{1,0:T(8,128)S(1)} %get-tuple-element.78), channel_id=1, source_target_pairs={{0,25},{1,24},{2,27},{3,26},{4,29},{5,28},{6,31},{7,30},{8,17},{9,... | collective-permute-start | bytes 245768 | tf_op jit(solution)/shard_map/ppermute | solution.py:359
  66.4 0.3 collective-permute-done.27.refs_12_
  66.7 2.2 %temporal.3 = (f32[512,1280]{1,0:T(8,128)S(1)}, f32[128,4,1280]{2,1,0:T(4,128)}) custom-call(bf16[512,512]{1,0:T(8,128)(2,1)S(1)} %get-tuple-element.43.high_ref, bf16[512,512]{1,0:T(8,128)(2,1)S(1)} %get-tuple-element.44.low_ref, f32[512,1280]{1,0:T(8,128)S(1)} %temporal.2.so_far_ref, f32[16,1280]{1,0:T(8,128)S(1)} %collective-permute-done.15.refs_0_, ...), custom_call_target="tpu_custom_call" | custom-call | flops 880803840 | bytes 5242880 | tf_op jit(solution)/shard_map/temporal/pallas_call | solution.py:268
  68.9 0.5 collective-permute-done.29.refs_0_
  69.5 1.4 %collective-permute-done.30.refs_1_ = f32[16,1280]{1,0:T(8,128)S(1)} collective-permute-done((f32[16,1280]{1,0:T(8,128)S(1)}, f32[16,1280]{1,0:T(8,128)S(1)}, u32[]{:S(2)}, u32[]{:S(2)}) %collective-permute-start.30) | collective-permute-done | bytes 81952 | tf_op jit(solution)/shard_map/ppermute | solution.py:359
  70.8 1.2 %finish.1 = f32[128,4,1280]{2,1,0:T(4,128)} custom-call(bf16[512,96]{1,0:T(8,128)(2,1)S(1)} %get-tuple-element.42.weights_ref, f32[512,1280]{1,0:T(8,128)S(1)} %get-tuple-element.75.so_far_ref, f32[128,4,1280]{2,1,0:T(4,128)} %get-tuple-element.76._, f32[16,1280]{1,0:T(8,128)S(1)} %collective-permute-done.29.refs_0_, ...), custom_call_target="tpu_custom_call", output_to_operand_aliasing={{}: (2, {})} | custom-call | flops 55050240 | bytes 2293760 | tf_op jit(solution)/shard_map/finish/pallas_call | solution.py:323
  (10 shorter events, 0.0 us)
Async XLA Ops:
  0.0 54.0 %copy-start.2 = (s32[1,128]{1,0:T(1,128)S(1)}, s32[1,128]{1,0:T(1,128)}, u32[]{:S(2)}) copy-start(s32[1,128]{1,0:T(1,128)} %constant.2.clone.partner_ref) | copy-start | bytes 1540
  0.0 5.5 %copy-start = (f32[4,128,1280]{2,1,0:T(8,128)S(1)}, f32[4,128,1280]{2,1,0:T(8,128)}, u32[]{:S(2)}) copy-start(f32[4,128,1280]{2,1,0:T(8,128)} %frames_ref.3) | copy-start | bytes 7864324
  0.0 54.0 %copy-start.1 = (f32[128]{0:T(128)S(1)}, f32[128]{0:T(128)}, u32[]{:S(2)}) copy-start(f32[128]{0:T(128)} %param.5) | copy-start | bytes 1540
  1.4 13.3 %collective-permute-start = (f32[16,1280]{1,0:T(8,128)S(1)}, f32[16,1280]{1,0:T(8,128)S(1)}, u32[]{:S(2)}, u32[]{:S(2)}) collective-permute-start(f32[16,1280]{1,0:T(8,128)S(1)} %get-tuple-element.46), channel_id=1, source_target_pairs={{0,16},{1,17},{2,18},{3,19},{4,20},{5,21},{6,22},{7,23},{8,24},{9,... | collective-permute-start | bytes 245768 | tf_op jit(solution)/shard_map/ppermute | solution.py:359
  5.5 12.6 %collective-permute-start.1 = (f32[16,1280]{1,0:T(8,128)S(1)}, f32[16,1280]{1,0:T(8,128)S(1)}, u32[]{:S(2)}, u32[]{:S(2)}) collective-permute-start(f32[16,1280]{1,0:T(8,128)S(1)} %get-tuple-element.47), channel_id=1, source_target_pairs={{0,17},{1,16},{2,19},{3,18},{4,21},{5,20},{6,23},{7,22},{8,25},{9,... | collective-permute-start | bytes 245768 | tf_op jit(solution)/shard_map/ppermute | solution.py:359
  8.5 11.7 %collective-permute-start.2 = (f32[16,1280]{1,0:T(8,128)S(1)}, f32[16,1280]{1,0:T(8,128)S(1)}, u32[]{:S(2)}, u32[]{:S(2)}) collective-permute-start(f32[16,1280]{1,0:T(8,128)S(1)} %get-tuple-element.48), channel_id=1, source_target_pairs={{0,18},{1,19},{2,16},{3,17},{4,22},{5,23},{6,20},{7,21},{8,26},{9,... | collective-permute-start | bytes 245768 | tf_op jit(solution)/shard_map/ppermute | solution.py:359
  11.5 10.9 %collective-permute-start.3 = (f32[16,1280]{1,0:T(8,128)S(1)}, f32[16,1280]{1,0:T(8,128)S(1)}, u32[]{:S(2)}, u32[]{:S(2)}) collective-permute-start(f32[16,1280]{1,0:T(8,128)S(1)} %get-tuple-element.49), channel_id=1, source_target_pairs={{0,19},{1,18},{2,17},{3,16},{4,23},{5,22},{6,21},{7,20},{8,27},{9,... | collective-permute-start | bytes 245768 | tf_op jit(solution)/shard_map/ppermute | solution.py:359
  12.2 14.6 %collective-permute-start.4 = (f32[16,1280]{1,0:T(8,128)S(1)}, f32[16,1280]{1,0:T(8,128)S(1)}, u32[]{:S(2)}, u32[]{:S(2)}) collective-permute-start(f32[16,1280]{1,0:T(8,128)S(1)} %get-tuple-element.50), channel_id=1, source_target_pairs={{0,12},{1,13},{2,14},{3,15},{4,8},{5,9},{6,10},{7,11},{8,4},{9,5},... | collective-permute-start | bytes 245768 | tf_op jit(solution)/shard_map/ppermute | solution.py:359
  14.7 13.5 %collective-permute-start.5 = (f32[16,1280]{1,0:T(8,128)S(1)}, f32[16,1280]{1,0:T(8,128)S(1)}, u32[]{:S(2)}, u32[]{:S(2)}) collective-permute-start(f32[16,1280]{1,0:T(8,128)S(1)} %get-tuple-element.51), channel_id=1, source_target_pairs={{0,22},{1,23},{2,20},{3,21},{4,18},{5,19},{6,16},{7,17},{8,30},{9,... | collective-permute-start | bytes 245768 | tf_op jit(solution)/shard_map/ppermute | solution.py:359
  18.1 10.1 %collective-permute-start.6 = (f32[16,1280]{1,0:T(8,128)S(1)}, f32[16,1280]{1,0:T(8,128)S(1)}, u32[]{:S(2)}, u32[]{:S(2)}) collective-permute-start(f32[16,1280]{1,0:T(8,128)S(1)} %get-tuple-element.52), channel_id=1, source_target_pairs={{0,13},{1,12},{2,15},{3,14},{4,9},{5,8},{6,11},{7,10},{8,5},{9,4},... | collective-permute-start | bytes 245768 | tf_op jit(solution)/shard_map/ppermute | solution.py:359
  20.1 12.1 %collective-permute-start.7 = (f32[16,1280]{1,0:T(8,128)S(1)}, f32[16,1280]{1,0:T(8,128)S(1)}, u32[]{:S(2)}, u32[]{:S(2)}) collective-permute-start(f32[16,1280]{1,0:T(8,128)S(1)} %get-tuple-element.53), channel_id=1, source_target_pairs={{0,23},{1,22},{2,21},{3,20},{4,19},{5,18},{6,17},{7,16},{8,31},{9,... | collective-permute-start | bytes 245768 | tf_op jit(solution)/shard_map/ppermute | solution.py:359
  22.4 13.4 %collective-permute-start.8 = (f32[16,1280]{1,0:T(8,128)S(1)}, f32[16,1280]{1,0:T(8,128)S(1)}, u32[]{:S(2)}, u32[]{:S(2)}) collective-permute-start(f32[16,1280]{1,0:T(8,128)S(1)} %get-tuple-element.54), channel_id=1, source_target_pairs={{0,14},{1,15},{2,12},{3,13},{4,10},{5,11},{6,8},{7,9},{8,6},{9,7},... | collective-permute-start | bytes 245768 | tf_op jit(solution)/shard_map/ppermute | solution.py:359
  26.8 9.7 %collective-permute-start.9 = (f32[16,1280]{1,0:T(8,128)S(1)}, f32[16,1280]{1,0:T(8,128)S(1)}, u32[]{:S(2)}, u32[]{:S(2)}) collective-permute-start(f32[16,1280]{1,0:T(8,128)S(1)} %get-tuple-element.55), channel_id=1, source_target_pairs={{0,20},{1,21},{2,22},{3,23},{4,16},{5,17},{6,18},{7,19},{8,28},{9,... | collective-permute-start | bytes 245768 | tf_op jit(solution)/shard_map/ppermute | solution.py:359
  28.2 10.4 %collective-permute-start.10 = (f32[16,1280]{1,0:T(8,128)S(1)}, f32[16,1280]{1,0:T(8,128)S(1)}, u32[]{:S(2)}, u32[]{:S(2)}) collective-permute-start(f32[16,1280]{1,0:T(8,128)S(1)} %get-tuple-element.56), channel_id=1, source_target_pairs={{0,15},{1,14},{2,13},{3,12},{4,11},{5,10},{6,9},{7,8},{8,7},{9,6},... | collective-permute-start | bytes 245768 | tf_op jit(solution)/shard_map/ppermute | solution.py:359
  28.2 10.4 %collective-permute-start.11 = (f32[16,1280]{1,0:T(8,128)S(1)}, f32[16,1280]{1,0:T(8,128)S(1)}, u32[]{:S(2)}, u32[]{:S(2)}) collective-permute-start(f32[16,1280]{1,0:T(8,128)S(1)} %get-tuple-element.57), channel_id=1, source_target_pairs={{0,21},{1,20},{2,23},{3,22},{4,17},{5,16},{6,19},{7,18},{8,29},{9,... | collective-permute-start | bytes 245768 | tf_op jit(solution)/shard_map/ppermute | solution.py:359
  32.2 8.8 %collective-permute-start.12 = (f32[16,1280]{1,0:T(8,128)S(1)}, f32[16,1280]{1,0:T(8,128)S(1)}, u32[]{:S(2)}, u32[]{:S(2)}) collective-permute-start(f32[16,1280]{1,0:T(8,128)S(1)} %get-tuple-element.58), channel_id=1, source_target_pairs={{0,10},{1,11},{2,8},{3,9},{4,14},{5,15},{6,12},{7,13},{8,2},{9,3},... | collective-permute-start | bytes 245768 | tf_op jit(solution)/shard_map/ppermute | solution.py:359
  35.8 8.1 %collective-permute-start.13 = (f32[16,1280]{1,0:T(8,128)S(1)}, f32[16,1280]{1,0:T(8,128)S(1)}, u32[]{:S(2)}, u32[]{:S(2)}) collective-permute-start(f32[16,1280]{1,0:T(8,128)S(1)} %get-tuple-element.59), channel_id=1, source_target_pairs={{0,11},{1,10},{2,9},{3,8},{4,15},{5,14},{6,13},{7,12},{8,3},{9,2},... | collective-permute-start | bytes 245768 | tf_op jit(solution)/shard_map/ppermute | solution.py:359
  36.5 8.0 %collective-permute-start.14 = (f32[16,1280]{1,0:T(8,128)S(1)}, f32[16,1280]{1,0:T(8,128)S(1)}, u32[]{:S(2)}, u32[]{:S(2)}) collective-permute-start(f32[16,1280]{1,0:T(8,128)S(1)} %get-tuple-element.60), channel_id=1, source_target_pairs={{0,28},{1,29},{2,30},{3,31},{4,24},{5,25},{6,26},{7,27},{8,20},{9,... | collective-permute-start | bytes 245768 | tf_op jit(solution)/shard_map/ppermute | solution.py:359
  38.5 7.0 %collective-permute-start.15 = (f32[16,1280]{1,0:T(8,128)S(1)}, f32[16,1280]{1,0:T(8,128)S(1)}, u32[]{:S(2)}, u32[]{:S(2)}) collective-permute-start(f32[16,1280]{1,0:T(8,128)S(1)} %get-tuple-element.61), channel_id=1, source_target_pairs={{0,8},{1,9},{2,10},{3,11},{4,12},{5,13},{6,14},{7,15},{8,0},{9,1},... | collective-permute-start | bytes 245768 | tf_op jit(solution)/shard_map/ppermute | solution.py:359
  38.6 8.9 %collective-permute-start.16 = (f32[16,1280]{1,0:T(8,128)S(1)}, f32[16,1280]{1,0:T(8,128)S(1)}, u32[]{:S(2)}, u32[]{:S(2)}) collective-permute-start(f32[16,1280]{1,0:T(8,128)S(1)} %get-tuple-element.62), channel_id=1, source_target_pairs={{0,29},{1,28},{2,31},{3,30},{4,25},{5,24},{6,27},{7,26},{8,21},{9,... | collective-permute-start | bytes 245768 | tf_op jit(solution)/shard_map/ppermute | solution.py:359
  41.0 10.0 %collective-permute-start.17 = (f32[16,1280]{1,0:T(8,128)S(1)}, f32[16,1280]{1,0:T(8,128)S(1)}, u32[]{:S(2)}, u32[]{:S(2)}) collective-permute-start(f32[16,1280]{1,0:T(8,128)S(1)} %get-tuple-element.63), channel_id=1, source_target_pairs={{0,9},{1,8},{2,11},{3,10},{4,13},{5,12},{6,15},{7,14},{8,1},{9,0},... | collective-permute-start | bytes 245768 | tf_op jit(solution)/shard_map/ppermute | solution.py:359
  43.9 8.3 %collective-permute-start.18 = (f32[16,1280]{1,0:T(8,128)S(1)}, f32[16,1280]{1,0:T(8,128)S(1)}, u32[]{:S(2)}, u32[]{:S(2)}) collective-permute-start(f32[16,1280]{1,0:T(8,128)S(1)} %get-tuple-element.64), channel_id=1, source_target_pairs={{0,30},{1,31},{2,28},{3,29},{4,26},{5,27},{6,24},{7,25},{8,22},{9,... | collective-permute-start | bytes 245768 | tf_op jit(solution)/shard_map/ppermute | solution.py:359
  44.5 10.7 %collective-permute-start.19 = (f32[16,1280]{1,0:T(8,128)S(1)}, f32[16,1280]{1,0:T(8,128)S(1)}, u32[]{:S(2)}, u32[]{:S(2)}) collective-permute-start(f32[16,1280]{1,0:T(8,128)S(1)} %get-tuple-element.65), channel_id=1, source_target_pairs={{0,5},{1,4},{2,7},{3,6},{4,1},{5,0},{6,3},{7,2},{8,13},{9,12},{10,... | collective-permute-start | bytes 245768 | tf_op jit(solution)/shard_map/ppermute | solution.py:359
  45.6 11.1 %collective-permute-start.20 = (f32[16,1280]{1,0:T(8,128)S(1)}, f32[16,1280]{1,0:T(8,128)S(1)}, u32[]{:S(2)}, u32[]{:S(2)}) collective-permute-start(f32[16,1280]{1,0:T(8,128)S(1)} %get-tuple-element.66), channel_id=1, source_target_pairs={{0,4},{1,5},{2,6},{3,7},{4,0},{5,1},{6,2},{7,3},{8,12},{9,13},{10,... | collective-permute-start | bytes 245768 | tf_op jit(solution)/shard_map/ppermute | solution.py:359
  47.4 11.5 %collective-permute-start.21 = (f32[16,1280]{1,0:T(8,128)S(1)}, f32[16,1280]{1,0:T(8,128)S(1)}, u32[]{:S(2)}, u32[]{:S(2)}) collective-permute-start(f32[16,1280]{1,0:T(8,128)S(1)} %get-tuple-element.67), channel_id=1, source_target_pairs={{0,31},{1,30},{2,29},{3,28},{4,27},{5,26},{6,25},{7,24},{8,23},{9,... | collective-permute-start | bytes 245768 | tf_op jit(solution)/shard_map/ppermute | solution.py:359
  51.0 9.0 %collective-permute-start.22 = (f32[16,1280]{1,0:T(8,128)S(1)}, f32[16,1280]{1,0:T(8,128)S(1)}, u32[]{:S(2)}, u32[]{:S(2)}) collective-permute-start(f32[16,1280]{1,0:T(8,128)S(1)} %get-tuple-element.68), channel_id=1, source_target_pairs={{0,7},{1,6},{2,5},{3,4},{4,3},{5,2},{6,1},{7,0},{8,15},{9,14},{10,... | collective-permute-start | bytes 245768 | tf_op jit(solution)/shard_map/ppermute | solution.py:359
  52.2 9.3 %collective-permute-start.23 = (f32[16,1280]{1,0:T(8,128)S(1)}, f32[16,1280]{1,0:T(8,128)S(1)}, u32[]{:S(2)}, u32[]{:S(2)}) collective-permute-start(f32[16,1280]{1,0:T(8,128)S(1)} %get-tuple-element.69), channel_id=1, source_target_pairs={{0,26},{1,27},{2,24},{3,25},{4,30},{5,31},{6,28},{7,29},{8,18},{9,... | collective-permute-start | bytes 245768 | tf_op jit(solution)/shard_map/ppermute | solution.py:359
  55.2 7.5 %collective-permute-start.24 = (f32[16,1280]{1,0:T(8,128)S(1)}, f32[16,1280]{1,0:T(8,128)S(1)}, u32[]{:S(2)}, u32[]{:S(2)}) collective-permute-start(f32[16,1280]{1,0:T(8,128)S(1)} %get-tuple-element.70), channel_id=1, source_target_pairs={{0,6},{1,7},{2,4},{3,5},{4,2},{5,3},{6,0},{7,1},{8,14},{9,15},{10,... | collective-permute-start | bytes 245768 | tf_op jit(solution)/shard_map/ppermute | solution.py:359
  56.7 7.9 %collective-permute-start.25 = (f32[16,1280]{1,0:T(8,128)S(1)}, f32[16,1280]{1,0:T(8,128)S(1)}, u32[]{:S(2)}, u32[]{:S(2)}) collective-permute-start(f32[16,1280]{1,0:T(8,128)S(1)} %get-tuple-element.71), channel_id=1, source_target_pairs={{0,27},{1,26},{2,25},{3,24},{4,31},{5,30},{6,29},{7,28},{8,19},{9,... | collective-permute-start | bytes 245768 | tf_op jit(solution)/shard_map/ppermute | solution.py:359
  59.0 7.4 %collective-permute-start.26 = (f32[16,1280]{1,0:T(8,128)S(1)}, f32[16,1280]{1,0:T(8,128)S(1)}, u32[]{:S(2)}, u32[]{:S(2)}) collective-permute-start(f32[16,1280]{1,0:T(8,128)S(1)} %get-tuple-element.72), channel_id=1, source_target_pairs={{0,3},{1,2},{2,1},{3,0},{4,7},{5,6},{6,5},{7,4},{8,11},{9,10},{10,... | collective-permute-start | bytes 245768 | tf_op jit(solution)/shard_map/ppermute | solution.py:359
  60.0 6.7 %collective-permute-start.27 = (f32[16,1280]{1,0:T(8,128)S(1)}, f32[16,1280]{1,0:T(8,128)S(1)}, u32[]{:S(2)}, u32[]{:S(2)}) collective-permute-start(f32[16,1280]{1,0:T(8,128)S(1)} %get-tuple-element.73), channel_id=1, source_target_pairs={{0,2},{1,3},{2,0},{3,1},{4,6},{5,7},{6,4},{7,5},{8,10},{9,11},{10,... | collective-permute-start | bytes 245768 | tf_op jit(solution)/shard_map/ppermute | solution.py:359
  61.5 5.2 %collective-permute-start.28 = (f32[16,1280]{1,0:T(8,128)S(1)}, f32[16,1280]{1,0:T(8,128)S(1)}, u32[]{:S(2)}, u32[]{:S(2)}) collective-permute-start(f32[16,1280]{1,0:T(8,128)S(1)} %get-tuple-element.74), channel_id=1, source_target_pairs={{0,1},{1,0},{2,3},{3,2},{4,5},{5,4},{6,7},{7,6},{8,9},{9,8},{10,11... | collective-permute-start | bytes 245768 | tf_op jit(solution)/shard_map/ppermute | solution.py:359
  62.7 6.8 %collective-permute-start.29 = (f32[16,1280]{1,0:T(8,128)S(1)}, f32[16,1280]{1,0:T(8,128)S(1)}, u32[]{:S(2)}, u32[]{:S(2)}) collective-permute-start(f32[16,1280]{1,0:T(8,128)S(1)} %get-tuple-element.77), channel_id=1, source_target_pairs={{0,24},{1,25},{2,26},{3,27},{4,28},{5,29},{6,30},{7,31},{8,16},{9,... | collective-permute-start | bytes 245768 | tf_op jit(solution)/shard_map/ppermute | solution.py:359
  64.5 6.3 %collective-permute-start.30 = (f32[16,1280]{1,0:T(8,128)S(1)}, f32[16,1280]{1,0:T(8,128)S(1)}, u32[]{:S(2)}, u32[]{:S(2)}) collective-permute-start(f32[16,1280]{1,0:T(8,128)S(1)} %get-tuple-element.78), channel_id=1, source_target_pairs={{0,25},{1,24},{2,27},{3,26},{4,29},{5,28},{6,31},{7,30},{8,17},{9,... | collective-permute-start | bytes 245768 | tf_op jit(solution)/shard_map/ppermute | solution.py:359
